TPU v7x, 128 devices: a whole 4x4x4 slice. The times are simulated.
128 devices in a mesh: gx: 8 (over y, core), gy: 16 (over z, x).
Axes of the slice: x: 4, y: 4, z: 4, core: 2. Of those that a mesh axis runs over, the one named last changes fastest.
Arguments:
- forcing: float32 [16, 512, 2048], P(None, 'gy', 'gx'), may hold values from -6 to 6
- damping: float32 [16, 512, 2048], P(None, 'gy', 'gx'), may hold values from 0.5 to 4
- coupling: float32 [16, 16], replicated, may hold values from -1.5 to 1.5
- wind_lon: float32 [512, 2048], P('gy', 'gx'), may hold values from -0.5 to 0.5
- wind_lat: float32 [512, 2048], P('gy', 'gx'), may hold values from -0.5 to 0.5
Outputs:
- solution: float32 [16, 512, 2048], P(None, 'gy', 'gx')
- residual: float32 [16, 512, 2048], P(None, 'gy', 'gx')
All inputs are finite; a program needn't handle non-finite values.
Results may differ from a plain program's by a relative error of at most 0.0003.
Values sent between devices are 32-bit elements; how exact they have to be, the bound alone decides.
No kernel may reach another device: no remote copies, remote signals or barrier semaphores. Data moves between devices by JAX's collectives and lax.ppermute only.
A program may use at most 64 MiB of HBM per device.

v0:
```python
import math

import jax
import jax.numpy as jnp
from jax import lax
from jax.sharding import Mesh
from jax.sharding import PartitionSpec as P

ITERS = 8
GY = ("gy_0", "gy_1")
GX = ("gx_0", "gx_1")
GX_GY = ("gx_0", "gx_1", "gy_0", "gy_1")


COUPLE = 0.25
DIFF_LAT = 0.5
DIFF_LON = 0.5
GUARD = 1.0


def with_halo(cells, sides, width, closed):
    for axis, dim in sides:
        count = lax.axis_size(axis)
        ends = count if closed else count - 1
        head = lax.slice_in_dim(cells, 0, width, axis=dim)
        tail = lax.slice_in_dim(cells, cells.shape[dim] - width, cells.shape[dim], axis=dim)
        cells = jnp.concatenate(
            [
                lax.ppermute(tail, axis, [(i, (i + 1) % count) for i in range(ends)]),
                cells,
                lax.ppermute(head, axis, [((i + 1) % count, i) for i in range(ends)]),
            ],
            axis=dim,
        )
    return cells


def one_axis_at_a_time(value, axes):
    for axis in axes:
        value = lax.psum(value, axis)
    return value


def apply_core(padded, damping, coupling, wind_lon, wind_lat, diffuse_lon):
    centre = padded[:, 2:-2, 2:-2]
    east_one = padded[:, 2:-2, 3:-1]
    west_one = padded[:, 2:-2, 1:-3]
    east_two = padded[:, 2:-2, 4:]
    west_two = padded[:, 2:-2, :-4]
    north_one = padded[:, 3:-1, 2:-2]
    south_one = padded[:, 1:-3, 2:-2]
    north_two = padded[:, 4:, 2:-2]
    south_two = padded[:, :-4, 2:-2]
    slope_lon = (8.0 * (east_one - west_one) - (east_two - west_two)) / 12.0
    slope_lat = (8.0 * (north_one - south_one) - (north_two - south_two)) / 12.0
    coupled = COUPLE * jnp.einsum("ij,jab->iab", coupling, centre, precision=lax.Precision.HIGHEST)
    return (
        (1.0 + damping) * centre
        + coupled
        + diffuse_lon * (2.0 * centre - east_one - west_one)
        + DIFF_LAT * (2.0 * centre - north_one - south_one)
        + wind_lon * slope_lon
        + wind_lat * slope_lat
    )


def lon_diffusion(row_pos, lat_total):
    phi = -math.pi / 2 + (row_pos + 0.5) * (math.pi / lat_total)
    return DIFF_LON / (jnp.cos(phi) ** 2 + 0.1)


def crop_rim(source, rim_have, rim_want):
    margin = rim_have - rim_want
    if margin == 0:
        return source
    return source[:, margin : source.shape[1] - margin, margin : source.shape[2] - margin]


def least_squares(heights, first):
    num_steps = heights.shape[1]
    target = jnp.zeros((num_steps + 1,), jnp.float32).at[0].set(first)
    rotated = heights
    cosines = []
    sines = []
    for column in range(num_steps):
        column_vec = rotated[:, column]
        for earlier in range(column):
            upper_val = column_vec[earlier]
            lower_val = column_vec[earlier + 1]
            column_vec = column_vec.at[earlier].set(
                cosines[earlier] * upper_val + sines[earlier] * lower_val
            )
            column_vec = column_vec.at[earlier + 1].set(
                -sines[earlier] * upper_val + cosines[earlier] * lower_val
            )
        upper_val = column_vec[column]
        lower_val = column_vec[column + 1]
        radius = jnp.sqrt(upper_val * upper_val + lower_val * lower_val)
        cosine = upper_val / radius
        sine_val = lower_val / radius
        column_vec = column_vec.at[column].set(radius).at[column + 1].set(0.0)
        rotated = rotated.at[:, column].set(column_vec)
        upper_val = target[column]
        lower_val = target[column + 1]
        target = target.at[column].set(cosine * upper_val + sine_val * lower_val)
        target = target.at[column + 1].set(-sine_val * upper_val + cosine * lower_val)
        cosines.append(cosine)
        sines.append(sine_val)
    weights = [None] * num_steps
    for column in reversed(range(num_steps)):
        partial_value = target[column]
        for later_col in range(column + 1, num_steps):
            partial_value = partial_value - rotated[column, later_col] * weights[later_col]
        weights[column] = partial_value / rotated[column, column]
    return weights


def per_device(forcing, damping, coupling, wind_lon, wind_lat):
    channels, lat_rows, lon_cols = forcing.shape
    lat_total = lat_rows * lax.axis_size(GY)
    extent = 2 * ITERS
    stacked = jnp.concatenate([forcing, damping, wind_lon[None], wind_lat[None]], axis=0)
    stacked = with_halo(stacked, ((GX, 2),), extent, True)
    stacked = with_halo(stacked, ((GY, 1),), extent, False)
    row_pos = (lax.axis_index(GY) * lat_rows - extent + jnp.arange(lat_rows + 2 * extent)).astype(
        jnp.float32
    )
    full_shape = (1, lat_rows + 2 * extent, lon_cols + 2 * extent)
    inside = ((row_pos >= 0.0) & (row_pos < lat_total)).astype(jnp.float32)
    inside_full = jnp.broadcast_to(inside[None, :, None], full_shape)
    diffuse_full = jnp.broadcast_to(lon_diffusion(row_pos, lat_total)[None, :, None], full_shape)
    damp_ext = stacked[channels : 2 * channels]
    zonal_ext = stacked[2 * channels : 2 * channels + 1]
    merid_ext = stacked[2 * channels + 1 :]

    def matvec(source, rim_in):
        rim_out = rim_in - 2
        result = apply_core(
            source,
            crop_rim(damp_ext, extent, rim_out),
            coupling,
            crop_rim(zonal_ext, extent, rim_out),
            crop_rim(merid_ext, extent, rim_out),
            crop_rim(diffuse_full, extent, rim_out),
        )
        return (result * crop_rim(inside_full, extent, rim_out), rim_out)

    initial = (stacked[:channels], extent)
    interior = crop_rim(initial[0], initial[1], 0)
    total_sq = one_axis_at_a_time(jnp.sum(interior * interior), GX_GY)
    scale_first = jnp.sqrt(total_sq + GUARD)
    krylov = [(initial[0] / scale_first, initial[1])]
    heights = jnp.zeros((ITERS + 1, ITERS), jnp.float32)
    gram = (
        jnp.zeros((ITERS, ITERS), jnp.float32).at[0, 0].set(total_sq / (scale_first * scale_first))
    )
    for column in range(ITERS):
        applied, rim_new = matvec(krylov[column][0], krylov[column][1])
        applied_in = crop_rim(applied, rim_new, 0)
        local_dots = jnp.stack(
            [jnp.sum(crop_rim(vector, rim_vec, 0) * applied_in) for vector, rim_vec in krylov]
        )
        count = len(krylov)
        coeffs, squared = (
            one_axis_at_a_time(local_dots, GX_GY),
            one_axis_at_a_time(jnp.sum(applied_in * applied_in), GX_GY),
        )
        for earlier in range(count):
            applied = applied - coeffs[earlier] * crop_rim(
                krylov[earlier][0], krylov[earlier][1], rim_new
            )
        gram_now = gram[:count, :count]
        gram_coef = jnp.sum(gram_now * coeffs[None, :], axis=1)
        norm_sq = jnp.maximum(
            squared - 2.0 * jnp.sum(coeffs * coeffs) + jnp.sum(coeffs * gram_coef), 0.0
        )
        subdiag = jnp.sqrt(norm_sq + GUARD)
        if column + 1 < ITERS:
            cross = (coeffs - gram_coef) / subdiag
            gram = gram.at[count, :count].set(cross).at[:count, count].set(cross)
            gram = gram.at[count, count].set(norm_sq / (subdiag * subdiag))
        heights = heights.at[: column + 1, column].set(coeffs).at[column + 1, column].set(subdiag)
        if column + 1 < ITERS:
            krylov.append((applied / subdiag, rim_new))
    weights = least_squares(heights, scale_first)
    rim_last = krylov[-1][1]
    solution = weights[0] * crop_rim(krylov[0][0], krylov[0][1], rim_last)
    for column in range(1, ITERS):
        solution = solution + weights[column] * crop_rim(
            krylov[column][0], krylov[column][1], rim_last
        )
    applied, rim_done = matvec(solution, rim_last)
    residual = interior - crop_rim(applied, rim_done, 0)
    return (crop_rim(solution, rim_last, 0), residual)


def solution(mesh):
    finer = Mesh(mesh.devices.reshape(4, 2, 4, 4), ("gx_0", "gx_1", "gy_0", "gy_1"))
    in_specs = (P(None, GY, GX), P(None, GY, GX), P(), P(GY, GX), P(GY, GX))
    out_specs = (P(None, GY, GX), P(None, GY, GX))
    return jax.shard_map(
        per_device, mesh=finer, in_specs=in_specs, out_specs=out_specs, check_vma=False
    )
```

profile of v0, /device:TPU:0, one launch (start us, length us, event | category | flops | bytes accessed | tf_op | source)
XLA Modules:
  0.0 691.3 jit_solution(11253868314345148001)
XLA Ops:
  13.4 9.4 %psum.476 = f32[]{:T(128)} all-reduce(f32[]{:T(128)} %multiply_reduce_fusion.44), channel_id=1, replica_groups=mesh['gx_0'=4,'gx_1'=2,'gy_0'=4,'gy_1'=4] {'gx_0'}, use_global_device_ids=true, to_apply=%region_1.0 | all-reduce | flops 1 | bytes 8 | tf_op jit(solution)/shard_map/psum | solution.py:40
  27.3 12.4 %psum.478 = f32[]{:T(128)} all-reduce(f32[]{:T(128)} %psum.477), channel_id=1, replica_groups=mesh['gx_0'=4,'gx_1'=2,'gy_0'=4,'gy_1'=4] {'gy_0'}, use_global_device_ids=true, to_apply=%region_3.0 | all-reduce | flops 1 | bytes 8 | tf_op jit(solution)/shard_map/psum | solution.py:40
  40.4 11.1 %psum.479 = f32[]{:T(128)} all-reduce(f32[]{:T(128)} %psum.478), channel_id=1, replica_groups=mesh['gx_0'=4,'gx_1'=2,'gy_0'=4,'gy_1'=4] {'gy_1'}, use_global_device_ids=true, to_apply=%region_4.0 | all-reduce | flops 1 | bytes 8 | tf_op jit(solution)/shard_map/psum | solution.py:40
  67.4 4.6 collective-permute-start.2
  72.1 12.4 %collective-permute-done.3 = f32[34,16,288]{2,1,0:T(8,128)S(1)} collective-permute-done((f32[34,16,288]{2,1,0:T(8,128)S(1)}, f32[34,16,288]{2,1,0:T(8,128)S(1)}, u32[]{:S(2)}, u32[]{:S(2)}) %collective-permute-start.3) | collective-permute-done | bytes 626720 | tf_op jit(solution)/shard_map/ppermute | solution.py:31
  86.2 5.5 pad_maximum_fusion
  93.5 4.6 fusion.3
  99.2 9.3 %all-reduce.26 = (f32[]{:T(128)}, f32[1]{0:T(128)}) all-reduce(f32[]{:T(128)} %get-tuple-element.1627, f32[1]{0:T(128)} %bitcast.5), channel_id=1, replica_groups=mesh['gx_0'=4,'gx_1'=2,'gy_0'=4,'gy_1'=4] {'gx_0'}, use_global_device_ids=true, to_apply=%region_11.0 | all-reduce | flops 2 | bytes 16 | tf_op jit(solution)/shard_map/psum | solution.py:40
  111.6 12.4 %all-reduce.18 = (f32[]{:T(128)}, f32[1]{0:T(128)}) all-reduce(f32[]{:T(128)} %get-tuple-element.1746, f32[1]{0:T(128)} %get-tuple-element.1747), channel_id=1, replica_groups=mesh['gx_0'=4,'gx_1'=2,'gy_0'=4,'gy_1'=4] {'gy_0'}, use_global_device_ids=true, to_apply=%region_13.0 | all-reduce | flops 2 | bytes 16 | tf_op jit(solution)/shard_map/psum | solution.py:40
  124.1 8.6 %all-reduce.10 = (f32[]{:T(128)}, f32[1]{0:T(128)}) all-reduce(f32[]{:T(128)} %get-tuple-element.1714, f32[1]{0:T(128)} %get-tuple-element.1715), channel_id=1, replica_groups=mesh['gx_0'=4,'gx_1'=2,'gy_0'=4,'gy_1'=4] {'gy_1'}, use_global_device_ids=true, to_apply=%region_14.0 | all-reduce | flops 2 | bytes 16 | tf_op jit(solution)/shard_map/psum | solution.py:40
  140.9 5.4 fusion.21
  154.7 9.5 %all-reduce.25 = (f32[]{:T(128)}, f32[2]{0:T(128)S(1)}) all-reduce(f32[]{:T(128)} %get-tuple-element.1630, f32[2]{0:T(128)S(1)} %pad_maximum_fusion.3), channel_id=1, replica_groups=mesh['gx_0'=4,'gx_1'=2,'gy_0'=4,'gy_1'=4] {'gx_0'}, use_global_device_ids=true, to_apply=%region_23.0 | all-reduce | flops 3 | bytes 24 | tf_op jit(solution)/shard_map/psum | solution.py:40
  167.3 8.8 %all-reduce.17 = (f32[]{:T(128)}, f32[2]{0:T(128)S(1)}) all-reduce(f32[]{:T(128)} %get-tuple-element.1744, f32[2]{0:T(128)S(1)} %get-tuple-element.1745), channel_id=1, replica_groups=mesh['gx_0'=4,'gx_1'=2,'gy_0'=4,'gy_1'=4] {'gy_0'}, use_global_device_ids=true, to_apply=%region_25.0 | all-reduce | flops 3 | bytes 24 | tf_op jit(solution)/shard_map/psum | solution.py:40
  176.0 10.0 %all-reduce.9 = (f32[]{:T(128)}, f32[2]{0:T(128)S(1)}) all-reduce(f32[]{:T(128)} %get-tuple-element.1712, f32[2]{0:T(128)S(1)} %get-tuple-element.1713), channel_id=1, replica_groups=mesh['gx_0'=4,'gx_1'=2,'gy_0'=4,'gy_1'=4] {'gy_1'}, use_global_device_ids=true, to_apply=%region_26.0 | all-reduce | flops 3 | bytes 24 | tf_op jit(solution)/shard_map/psum | solution.py:40
  194.4 5.6 fusion.39
  206.9 9.2 %all-reduce.24 = (f32[]{:T(128)}, f32[3]{0:T(128)S(1)}) all-reduce(f32[]{:T(128)} %get-tuple-element.1634, f32[3]{0:T(128)S(1)} %pad_maximum_fusion.4), channel_id=1, replica_groups=mesh['gx_0'=4,'gx_1'=2,'gy_0'=4,'gy_1'=4] {'gx_0'}, use_global_device_ids=true, to_apply=%region_39.0 | all-reduce | flops 4 | bytes 32 | tf_op jit(solution)/shard_map/psum | solution.py:40
  219.2 10.4 %all-reduce.16 = (f32[]{:T(128)}, f32[3]{0:T(128)S(1)}) all-reduce(f32[]{:T(128)} %get-tuple-element.1742, f32[3]{0:T(128)S(1)} %get-tuple-element.1743), channel_id=1, replica_groups=mesh['gx_0'=4,'gx_1'=2,'gy_0'=4,'gy_1'=4] {'gy_0'}, use_global_device_ids=true, to_apply=%region_41.0 | all-reduce | flops 4 | bytes 32 | tf_op jit(solution)/shard_map/psum | solution.py:40
  229.6 8.3 %all-reduce.8 = (f32[]{:T(128)}, f32[3]{0:T(128)S(1)}) all-reduce(f32[]{:T(128)} %get-tuple-element.1710, f32[3]{0:T(128)S(1)} %get-tuple-element.1711), channel_id=1, replica_groups=mesh['gx_0'=4,'gx_1'=2,'gy_0'=4,'gy_1'=4] {'gy_1'}, use_global_device_ids=true, to_apply=%region_42.0 | all-reduce | flops 4 | bytes 32 | tf_op jit(solution)/shard_map/psum | solution.py:40
  243.3 4.7 fusion.34
  248.0 5.2 fusion.73
  262.5 9.6 %all-reduce.23 = (f32[]{:T(128)}, f32[4]{0:T(128)S(1)}) all-reduce(f32[]{:T(128)} %get-tuple-element.1639, f32[4]{0:T(128)S(1)} %pad_maximum_fusion.5), channel_id=1, replica_groups=mesh['gx_0'=4,'gx_1'=2,'gy_0'=4,'gy_1'=4] {'gx_0'}, use_global_device_ids=true, to_apply=%region_56.0 | all-reduce | flops 5 | bytes 40 | tf_op jit(solution)/shard_map/psum | solution.py:40
  275.2 8.8 %all-reduce.15 = (f32[]{:T(128)}, f32[4]{0:T(128)S(1)}) all-reduce(f32[]{:T(128)} %get-tuple-element.1740, f32[4]{0:T(128)S(1)} %get-tuple-element.1741), channel_id=1, replica_groups=mesh['gx_0'=4,'gx_1'=2,'gy_0'=4,'gy_1'=4] {'gy_0'}, use_global_device_ids=true, to_apply=%region_58.0 | all-reduce | flops 5 | bytes 40 | tf_op jit(solution)/shard_map/psum | solution.py:40
  284.1 10.0 %all-reduce.7 = (f32[]{:T(128)}, f32[4]{0:T(128)S(1)}) all-reduce(f32[]{:T(128)} %get-tuple-element.1708, f32[4]{0:T(128)S(1)} %get-tuple-element.1709), channel_id=1, replica_groups=mesh['gx_0'=4,'gx_1'=2,'gy_0'=4,'gy_1'=4] {'gy_1'}, use_global_device_ids=true, to_apply=%region_59.0 | all-reduce | flops 5 | bytes 40 | tf_op jit(solution)/shard_map/psum | solution.py:40
  299.0 5.8 fusion.67
  304.8 4.9 fusion.93
  320.0 9.3 %all-reduce.22 = (f32[]{:T(128)}, f32[5]{0:T(128)S(1)}) all-reduce(f32[]{:T(128)} %get-tuple-element.1644, f32[5]{0:T(128)S(1)} %stack.147), channel_id=1, replica_groups=mesh['gx_0'=4,'gx_1'=2,'gy_0'=4,'gy_1'=4] {'gx_0'}, use_global_device_ids=true, to_apply=%region_74.0 | all-reduce | flops 6 | bytes 48 | tf_op jit(solution)/shard_map/psum | solution.py:40
  332.4 10.4 %all-reduce.14 = (f32[]{:T(128)}, f32[5]{0:T(128)S(1)}) all-reduce(f32[]{:T(128)} %get-tuple-element.1738, f32[5]{0:T(128)S(1)} %get-tuple-element.1739), channel_id=1, replica_groups=mesh['gx_0'=4,'gx_1'=2,'gy_0'=4,'gy_1'=4] {'gy_0'}, use_global_device_ids=true, to_apply=%region_76.0 | all-reduce | flops 6 | bytes 48 | tf_op jit(solution)/shard_map/psum | solution.py:40
  342.8 8.3 %all-reduce.6 = (f32[]{:T(128)}, f32[5]{0:T(128)S(1)}) all-reduce(f32[]{:T(128)} %get-tuple-element.1706, f32[5]{0:T(128)S(1)} %get-tuple-element.1707), channel_id=1, replica_groups=mesh['gx_0'=4,'gx_1'=2,'gy_0'=4,'gy_1'=4] {'gy_1'}, use_global_device_ids=true, to_apply=%region_77.0 | all-reduce | flops 6 | bytes 48 | tf_op jit(solution)/shard_map/psum | solution.py:40
  356.2 6.8 fusion.86
  363.1 4.5 fusion.114
  374.9 3.8 stack.154
  378.7 9.5 %all-reduce.21 = (f32[]{:T(128)}, f32[6]{0:T(128)S(1)}) all-reduce(f32[]{:T(128)} %get-tuple-element.1651, f32[6]{0:T(128)S(1)} %stack.154), channel_id=1, replica_groups=mesh['gx_0'=4,'gx_1'=2,'gy_0'=4,'gy_1'=4] {'gx_0'}, use_global_device_ids=true, to_apply=%region_93.0 | all-reduce | flops 7 | bytes 56 | tf_op jit(solution)/shard_map/psum | solution.py:40
  391.3 8.8 %all-reduce.13 = (f32[]{:T(128)}, f32[6]{0:T(128)S(1)}) all-reduce(f32[]{:T(128)} %get-tuple-element.1736, f32[6]{0:T(128)S(1)} %get-tuple-element.1737), channel_id=1, replica_groups=mesh['gx_0'=4,'gx_1'=2,'gy_0'=4,'gy_1'=4] {'gy_0'}, use_global_device_ids=true, to_apply=%region_95.0 | all-reduce | flops 7 | bytes 56 | tf_op jit(solution)/shard_map/psum | solution.py:40
  400.1 10.0 %all-reduce.5 = (f32[]{:T(128)}, f32[6]{0:T(128)S(1)}) all-reduce(f32[]{:T(128)} %get-tuple-element.1704, f32[6]{0:T(128)S(1)} %get-tuple-element.1705), channel_id=1, replica_groups=mesh['gx_0'=4,'gx_1'=2,'gy_0'=4,'gy_1'=4] {'gy_1'}, use_global_device_ids=true, to_apply=%region_96.0 | all-reduce | flops 7 | bytes 56 | tf_op jit(solution)/shard_map/psum | solution.py:40
  414.1 7.7 %fusion.106 = f32[16,40,264]{2,0,1:T(8,128)S(1)} fusion(f32[16,48,272]{2,0,1:T(8,128)} %copy-done.3, f32[16,52,276]{2,0,1:T(8,128)} %copy-done.2, f32[16,56,280]{2,0,1:T(8,128)} %copy-done.1, f32[16,60,284]{2,0,1:T(8,128)S(1)} %subtract_divide_fusion, f32[16,40,264]{2,0,1:T(8,128)} %copy-done.16, f32[16,64,288]{2,0,1:T(8,128)S(1)} %slice_divide_fusion, ...), kind=kLoop, calls=%fused_computation.139 | loop fusion | flops 2196480 | bytes 5406748 | tf_op jit(solution)/shard_map/div | solution.py:184
  421.8 4.2 fusion.128
  426.1 4.1 multiply_reduce_fusion.10
  433.9 4.5 stack.162
  438.4 9.2 %all-reduce.20 = (f32[]{:T(128)}, f32[7]{0:T(128)S(1)}) all-reduce(f32[]{:T(128)} %get-tuple-element.1659, f32[7]{0:T(128)S(1)} %stack.162), channel_id=1, replica_groups=mesh['gx_0'=4,'gx_1'=2,'gy_0'=4,'gy_1'=4] {'gx_0'}, use_global_device_ids=true, to_apply=%region_113.0 | all-reduce | flops 8 | bytes 64 | tf_op jit(solution)/shard_map/psum | solution.py:40
  450.7 10.3 %all-reduce.12 = (f32[]{:T(128)}, f32[7]{0:T(128)S(1)}) all-reduce(f32[]{:T(128)} %get-tuple-element.1734, f32[7]{0:T(128)S(1)} %get-tuple-element.1735), channel_id=1, replica_groups=mesh['gx_0'=4,'gx_1'=2,'gy_0'=4,'gy_1'=4] {'gy_0'}, use_global_device_ids=true, to_apply=%region_115.0 | all-reduce | flops 8 | bytes 64 | tf_op jit(solution)/shard_map/psum | solution.py:40
  461.1 8.3 %all-reduce.4 = (f32[]{:T(128)}, f32[7]{0:T(128)S(1)}) all-reduce(f32[]{:T(128)} %get-tuple-element.1702, f32[7]{0:T(128)S(1)} %get-tuple-element.1703), channel_id=1, replica_groups=mesh['gx_0'=4,'gx_1'=2,'gy_0'=4,'gy_1'=4] {'gy_1'}, use_global_device_ids=true, to_apply=%region_116.0 | all-reduce | flops 8 | bytes 64 | tf_op jit(solution)/shard_map/psum | solution.py:40
  494.3 8.8 %subtract_divide_fusion.1 = f32[16,36,260]{2,0,1:T(8,128)S(1)} fusion(f32[16,36,260]{2,0,1:T(8,128)} %copy-done.17, f32[16,44,268]{2,0,1:T(8,128)} %copy-done.4, f32[16,48,272]{2,0,1:T(8,128)} %copy-done.3, f32[16,52,276]{2,0,1:T(8,128)} %copy-done.2, f32[16,56,280]{2,0,1:T(8,128)} %copy-done.1, f32[16,60,284]{2,0,1:T(8,128)S(1)} %subtract_divide_fusion, ...), kind=kLoop, calls=%fused_computation.178 | loop fusion | flops 2246400 | bytes 5391392 | tf_op jit(solution)/shard_map/div | solution.py:184
  503.1 5.2 multiply_reduce_fusion
  508.3 5.1 stack.171
  513.3 9.4 %all-reduce.19 = (f32[8]{0:T(128)S(1)}, f32[]{:T(128)}) all-reduce(f32[8]{0:T(128)S(1)} %stack.171, f32[]{:T(128)} %get-tuple-element.1661), channel_id=1, replica_groups=mesh['gx_0'=4,'gx_1'=2,'gy_0'=4,'gy_1'=4] {'gx_0'}, use_global_device_ids=true, to_apply=%region_129.0 | all-reduce | flops 9 | bytes 72 | tf_op jit(solution)/shard_map/psum | solution.py:40
  525.8 8.8 %all-reduce.11 = (f32[8]{0:T(128)S(1)}, f32[]{:T(128)}) all-reduce(f32[8]{0:T(128)S(1)} %get-tuple-element.1732, f32[]{:T(128)} %get-tuple-element.1733), channel_id=1, replica_groups=mesh['gx_0'=4,'gx_1'=2,'gy_0'=4,'gy_1'=4] {'gy_0'}, use_global_device_ids=true, to_apply=%region_131.0 | all-reduce | flops 9 | bytes 72 | tf_op jit(solution)/shard_map/psum | solution.py:40
  534.7 9.9 %all-reduce.3 = (f32[8]{0:T(128)S(1)}, f32[]{:T(128)}) all-reduce(f32[8]{0:T(128)S(1)} %get-tuple-element.1700, f32[]{:T(128)} %get-tuple-element.1701), channel_id=1, replica_groups=mesh['gx_0'=4,'gx_1'=2,'gy_0'=4,'gy_1'=4] {'gy_1'}, use_global_device_ids=true, to_apply=%region_132.0 | all-reduce | flops 9 | bytes 72 | tf_op jit(solution)/shard_map/psum | solution.py:40
  682.0 4.3 multiply_add_fusion
  (386 shorter events, 197.1 us)
Async XLA Ops:
  0.6 92.9 %copy-start = (f32[16,16]{1,0:T(8,128)S(1)}, f32[16,16]{1,0:T(8,128)}, u32[]{:S(2)}) copy-start(f32[16,16]{1,0:T(8,128)} %param.277) | copy-start | bytes 3076
  0.6 3.0 copy-start.18
  5.1 4.3 copy-start.19
  5.1 48.3 %copy-start.30 = (s32[2]{0:T(128)S(1)}, s32[2]{0:T(128)}, u32[]{:S(2)}) copy-start(s32[2]{0:T(128)} %constant.2816.clone.1) | copy-start | bytes 28
  5.1 49.7 %copy-start.29 = (s32[2]{0:T(128)S(1)}, s32[2]{0:T(128)}, u32[]{:S(2)}) copy-start(s32[2]{0:T(128)} %constant.2818.clone.1) | copy-start | bytes 28
  5.1 51.0 %copy-start.28 = (s32[2]{0:T(128)S(1)}, s32[2]{0:T(128)}, u32[]{:S(2)}) copy-start(s32[2]{0:T(128)} %constant.2819.clone.1) | copy-start | bytes 28
  5.1 52.2 %copy-start.27 = (s32[2]{0:T(128)S(1)}, s32[2]{0:T(128)}, u32[]{:S(2)}) copy-start(s32[2]{0:T(128)} %constant.2821.clone.1) | copy-start | bytes 28
  5.1 53.4 %copy-start.26 = (s32[2]{0:T(128)S(1)}, s32[2]{0:T(128)}, u32[]{:S(2)}) copy-start(s32[2]{0:T(128)} %constant.2823.clone.1) | copy-start | bytes 28
  5.2 54.7 %copy-start.25 = (s32[2]{0:T(128)S(1)}, s32[2]{0:T(128)}, u32[]{:S(2)}) copy-start(s32[2]{0:T(128)} %constant.2824.clone.1) | copy-start | bytes 28
  6.6 54.5 %collective-permute-start.1 = (f32[34,32,16]{0,2,1:T(8,128)S(1)}, f32[34,32,16]{0,2,1:T(8,128)S(1)}, u32[]{:S(2)}, u32[]{:S(2)}) collective-permute-start(f32[34,32,16]{0,2,1:T(8,128)S(1)} %copy.22), channel_id=1, source_target_pairs={{16,0},{32,16},{48,32},{64,48},{80,64},{96,80},{112,96},{0,112},{1... | collective-permute-start | bytes 208904 | tf_op jit(solution)/shard_map/ppermute | solution.py:31
  9.4 52.8 %collective-permute-start = (f32[34,32,16]{0,2,1:T(8,128)S(1)}, f32[34,32,16]{0,2,1:T(8,128)S(1)}, u32[]{:S(2)}, u32[]{:S(2)}) collective-permute-start(f32[34,32,16]{0,2,1:T(8,128)S(1)} %copy.21), channel_id=1, source_target_pairs={{0,16},{16,32},{32,48},{48,64},{64,80},{80,96},{96,112},{112,0},{1... | collective-permute-start | bytes 208904 | tf_op jit(solution)/shard_map/ppermute | solution.py:29
  65.9 6.3 copy-start.23
  65.9 6.2 copy-start.24
  65.9 18.6 %collective-permute-start.3 = (f32[34,16,288]{2,1,0:T(8,128)S(1)}, f32[34,16,288]{2,1,0:T(8,128)S(1)}, u32[]{:S(2)}, u32[]{:S(2)}) collective-permute-start(f32[34,16,288]{2,1,0:T(8,128)S(1)} %copy.26), channel_id=1, source_target_pairs={{1,0},{2,1},{3,2},{4,3},{5,4},{6,5},{7,6},{8,7},{9,8},{10,9},{11,1... | collective-permute-start | bytes 1880072 | tf_op jit(solution)/shard_map/ppermute | solution.py:31
  67.4 18.5 %collective-permute-start.2 = (f32[34,16,288]{2,1,0:T(8,128)S(1)}, f32[34,16,288]{2,1,0:T(8,128)S(1)}, u32[]{:S(2)}, u32[]{:S(2)}) collective-permute-start(f32[34,16,288]{2,1,0:T(8,128)S(1)} %copy.25), channel_id=1, source_target_pairs={{0,1},{1,2},{2,3},{3,4},{4,5},{5,6},{6,7},{7,8},{8,9},{9,10},{10,1... | collective-permute-start | bytes 1880072 | tf_op jit(solution)/shard_map/ppermute | solution.py:29
  84.8 1.4 copy-start.8
  84.8 1.4 copy-start.9
  91.7 1.9 copy-start.7
  98.2 40.2 %copy-start.11 = (f32[16,60,284]{2,0,1:T(8,128)}, f32[16,60,284]{2,0,1:T(8,128)S(1)}, u32[]{:S(2)}) copy-start(f32[16,60,284]{2,0,1:T(8,128)S(1)} %fusion.3) | copy-start | bytes 3271684
  146.4 1.1 copy-start.12
  194.3 5.6 copy-start.1
  199.9 1.3 copy-start.13
  248.0 5.2 copy-start.2
  253.2 3.0 copy-start.14
  304.8 4.9 copy-start.3
  309.8 3.4 copy-start.15
  363.0 4.5 copy-start.4
  367.6 3.7 copy-start.16
  421.8 4.2 copy-start.5
  426.1 4.1 copy-start.17
  494.3 8.8 %copy-start.6 = (f32[16,40,264]{2,0,1:T(8,128)S(1)}, f32[16,40,264]{2,0,1:T(8,128)}, u32[]{:S(2)}) copy-start(f32[16,40,264]{2,0,1:T(8,128)} %copy-done.5) | copy-start | bytes 2027524
  494.3 8.8 %copy-start.21 = (f32[16,32,256]{2,1,0:T(8,128)S(1)}, f32[16,32,256]{2,1,0:T(8,128)}, u32[]{:S(2)}) copy-start(f32[16,32,256]{2,1,0:T(8,128)} %param.276) | copy-start | bytes 1572868
  503.1 5.2 copy-start.10
  682.0 4.5 copy-start.20
  682.0 4.5 copy-start.22
where the time goes:
time: 704 us; the launch traced here: 691 us
  blocking collectives  288 us (41%)
  other arithmetic  128 us (18%)
  between operations  117 us (17%)
  local copies, waits for them, and re-layouts  94.7 us (13%)
  matrix products  41.7 us (6%)
  waiting for transfers between devices  13.4 us (2%)
  starting transfers between devices  8.48 us (1%)
    psum x36, blocking collectives, one_axis_at_a_time(): value = lax.psum(value, axis)  288 us
    dot_general x9, matrix products, apply_core(): jnp.einsum('ij,jab->iab', coupling, centre, precision=lax.Precision.HIGHEST)  41.7 us
    div x7, other arithmetic, per_device(): krylov.append((applied / subdiag, rim_new))  39.6 us
    another operation x38, other arithmetic  38.6 us
    reduce_sum x7, other arithmetic, per_device(): jnp.sum(crop_rim(vector, rim_vec, 0) * applied_in)  17.7 us
    another operation x4, local copies, waits for them, and re-layouts, per_device(): jnp.stack([jnp.sum(crop_rim(vector, rim_vec, 0) * applied_in) for vector,...  16.5 us
    slice x25, local copies, waits for them, and re-layouts, least_squares(): lower_val = column_vec[earlier + 1]  15.2 us
  transfers between devices with their start and end apart: 4, of which 2 were waited for; matrix products, arithmetic and copies ran while one was open for 2% of the time, Pallas kernels for 0%

commit v1 on v0

v1 whole, which is shorter than its diff:
```python
import functools
import math

import jax
import jax.numpy as jnp
import numpy as np
from jax import lax
from jax.experimental import pallas as pl
from jax.experimental.pallas import tpu as pltpu
from jax.sharding import PartitionSpec as P

ITERS = 8
CH = 16
ROWS = 32
COLS = 256
RIM = 2 * ITERS
EXT_ROWS = ROWS + 2 * RIM
EXT_COLS = COLS + 128
COUPLE = 0.25
DIFF_LAT = 0.5
DIFF_LON = 0.5
GUARD = 1.0

LOW, HIGH = 1.5, 26.0
CENTRE = (LOW + HIGH) / 2
SCALE = 4.0 / (HIGH - LOW)
NUM = ITERS + 1
PAIRS = [(i, j) for j in range(NUM) for i in range(j + 1)]
F32 = jnp.float32


def pack_kernel(f_ref, d_ref, wl_ref, wt_ref, s1_ref, s2_ref, x1_ref, x2_ref):
    par_y = lax.rem(lax.axis_index("gy"), 2)
    par_x = lax.rem(lax.axis_index("gx"), 2)
    for ref, half in ((s1_ref, 1 - par_y), (s2_ref, par_y)):
        for q in range(2):
            off = pl.multiple_of(half * 16 + 8 * q, 8)
            for src, base in ((f_ref, 0), (d_ref, 16)):
                for c in range(2):
                    ref[base + 8 * q : base + 8 * q + 8, 8 * c : 8 * c + 8, :] = jnp.swapaxes(
                        src[8 * c : 8 * c + 8, pl.ds(off, 8), :], 0, 1
                    )
        off = pl.multiple_of(half * 16, 16)
        ref[32] = wl_ref[pl.ds(off, 16), :]
        ref[33] = wt_ref[pl.ds(off, 16), :]
    group = lax.broadcasted_iota(jnp.int32, (8, 128), 1) // 16

    def gather(tiles):
        left = jnp.zeros((8, 128), F32)
        right = jnp.zeros((8, 128), F32)
        for g, (low, high) in enumerate(tiles):
            left = jnp.where(group == g, pltpu.roll(low, 16 * g, 1) if g else low, left)
            shift = (16 * g + 16) % 128
            right = jnp.where(group == g, pltpu.roll(high, shift, 1) if shift else high, right)
        return jnp.where(par_x == 0, right, left), jnp.where(par_x == 0, left, right)

    winds = gather(
        [
            (ref[8 * q : 8 * q + 8, :128], ref[8 * q : 8 * q + 8, 128:])
            for ref in (wl_ref, wt_ref)
            for q in range(4)
        ]
    )
    for half in range(2):
        slot = 0
        for base in (0, 16):
            for q in range(2):
                for c in range(2):
                    tiles = []
                    for g in range(8):
                        row = base + 8 * q + g
                        pick = []
                        for t in range(2):
                            one = s1_ref[row, 8 * c : 8 * c + 8, 128 * t : 128 * t + 128]
                            two = s2_ref[row, 8 * c : 8 * c + 8, 128 * t : 128 * t + 128]
                            pick.append(jnp.where(par_y == half, two, one))
                        tiles.append(tuple(pick))
                    first, second = gather(tiles)
                    x1_ref[half, 8 * slot : 8 * slot + 8, :] = first
                    x2_ref[half, 8 * slot : 8 * slot + 8, :] = second
                    slot += 1
        x1_ref[half, 64:72, :] = winds[0]
        x2_ref[half, 64:72, :] = winds[1]


def main_kernel(
    s1_ref, s2_ref, r1_ref, r2_ref, g1_ref, g2_ref, c1_ref, c2_ref, tab_ref, kron_ref,
    out_ref, gram_ref,
    p_ref, d_ref, w_ref, k_ref, coef_ref, sums_ref, in_sem, out_sem,
):
    par_y = lax.rem(lax.axis_index("gy"), 2)
    par_x = lax.rem(lax.axis_index("gx"), 2)
    copies = []

    def fetch(src, dst):
        copy = pltpu.make_async_copy(src, dst, in_sem.at[len(copies)])
        copy.start()
        copies.append(copy)

    start = pl.multiple_of(lax.axis_index("gy") * ROWS, ROWS)
    fetch(tab_ref.at[pl.ds(start, EXT_ROWS)], k_ref)
    dest = ((s1_ref, 32 - 16 * par_y), (s2_ref, 16 + 16 * par_y), (r1_ref, 48 - 48 * par_y), (r2_ref, 48 * par_y))
    for src, row in dest:
        row = pl.multiple_of(row, 16)
        fetch(src.at[0:16], p_ref.at[0, pl.ds(row, 16), :, pl.ds(0, COLS)])
        fetch(src.at[16:32], d_ref.at[pl.ds(row, 16), :, pl.ds(0, COLS)])
        fetch(src.at[32:34], w_ref.at[:, pl.ds(row, 16), pl.ds(0, COLS)])

    lane = lax.broadcasted_iota(jnp.int32, (8, 128), 1)

    def spread(east, west, g):
        e = pltpu.roll(east, (128 - 16 * g) % 128, 1) if g else east
        shift = (112 - 16 * g) % 128
        w = pltpu.roll(west, shift, 1) if shift else west
        return jnp.where(lane < 16, e, jnp.where(lane >= 112, w, 0.0))

    places = (
        (lambda sl: g1_ref[0, sl], lambda sl: g2_ref[0, sl], 16, 0),
        (lambda sl: g1_ref[1, sl], lambda sl: g2_ref[1, sl], 32, 1),
        (lambda sl: c1_ref[0, sl], lambda sl: c1_ref[1, sl], 48 - 48 * par_y, par_y),
        (lambda sl: c2_ref[0, sl], lambda sl: c2_ref[1, sl], 48 * par_y, 1 - par_y),
    )
    for one, two, row, half in places:
        slot = 0
        for ref in (p_ref.at[0], d_ref):
            for q in range(2):
                for c in range(2):
                    a = one(slice(8 * slot, 8 * slot + 8))
                    b = two(slice(8 * slot, 8 * slot + 8))
                    east = jnp.where(par_x == 0, a, b)
                    west = jnp.where(par_x == 0, b, a)
                    for g in range(8):
                        ref[row + 8 * q + g, 8 * c : 8 * c + 8, COLS:] = spread(east, west, g)
                    slot += 1
        a = one(slice(64, 72))
        b = two(slice(64, 72))
        east = jnp.where(par_x == 0, a, b)
        west = jnp.where(par_x == 0, b, a)
        for field in range(2):
            for q in range(2):
                low = spread(east, west, 4 * field + q)
                high = spread(east, west, 4 * field + 2 + q)
                tile = jnp.where(half == 0, low, high)
                w_ref[field, pl.ds(pl.multiple_of(row + 8 * q, 8), 8), COLS:] = tile

    kron = kron_ref[...]
    kron_hi = kron.astype(jnp.bfloat16)
    kron_lo = (kron - kron_hi.astype(F32)).astype(jnp.bfloat16)
    for copy in copies:
        copy.wait()

    for q in range(EXT_ROWS // 8):
        rows = slice(8 * q, 8 * q + 8)
        diffuse = jnp.concatenate([k_ref[rows]] * 3, axis=1)
        live = jnp.where(diffuse > 0.0, 1.0, 0.0)
        lon = w_ref[0, rows] * (live * (SCALE / 12.0))
        lat = w_ref[1, rows] * (live * (SCALE / 12.0))
        kx = diffuse * SCALE
        half_lat = live * (SCALE * DIFF_LAT)
        coef_ref[0, rows] = 8.0 * lon - kx
        coef_ref[1, rows] = -8.0 * lon - kx
        coef_ref[2, rows] = -lon
        coef_ref[3, rows] = 8.0 * lat - half_lat
        coef_ref[4, rows] = -8.0 * lat - half_lat
        coef_ref[5, rows] = -lat
        coef_ref[6, rows] = live * (SCALE * (1.0 + 2.0 * DIFF_LAT - CENTRE)) + 2.0 * kx
        coef_ref[7, rows] = live * SCALE

    @pl.loop(0, EXT_ROWS, unroll=2)
    def _(r):
        d_ref[r] = d_ref[r] * coef_ref[7, pl.ds(r, 1)] + coef_ref[6, pl.ds(r, 1)]

    outs = []

    def emit(step):
        copy = pltpu.make_async_copy(
            p_ref.at[step, pl.ds(RIM, ROWS), :, pl.ds(0, COLS)], out_ref.at[step], out_sem.at[step]
        )
        copy.start()
        outs.append(copy)

    emit(0)
    for step in range(1, NUM):
        low = 2 * step
        blocks = (EXT_ROWS - 2 * low + 7) // 8

        @pl.loop(0, blocks)
        def _(block, step=step, low=low):
            r0 = jnp.minimum(low + 8 * block, EXT_ROWS - low - 8)
            flat = p_ref[step - 1, pl.ds(r0, 8)].reshape(8 * CH, EXT_COLS)
            hi = flat.astype(jnp.bfloat16)
            lo = (flat - hi.astype(F32)).astype(jnp.bfloat16)
            mixed = jnp.dot(kron_hi, hi, preferred_element_type=F32)
            mixed = mixed + jnp.dot(kron_hi, lo, preferred_element_type=F32)
            mixed = mixed + jnp.dot(kron_lo, hi, preferred_element_type=F32)
            mixed = mixed.reshape(8, CH, EXT_COLS)
            for i in range(8):
                r = r0 + i
                c = p_ref[step - 1, r]
                acc = mixed[i] + d_ref[r] * c
                if step > 1:
                    acc = acc - p_ref[step - 2, r]
                coef = [coef_ref[k, pl.ds(r, 1)] for k in range(6)]
                acc = acc + coef[0] * pltpu.roll(c, EXT_COLS - 1, 1)
                acc = acc + coef[1] * pltpu.roll(c, 1, 1)
                acc = acc + coef[2] * (pltpu.roll(c, EXT_COLS - 2, 1) - pltpu.roll(c, 2, 1))
                acc = acc + coef[3] * p_ref[step - 1, r + 1]
                acc = acc + coef[4] * p_ref[step - 1, r - 1]
                acc = acc + coef[5] * (p_ref[step - 1, r + 2] - p_ref[step - 1, r - 2])
                p_ref[step, r] = acc

        emit(step)

    sums_ref[...] = jnp.zeros_like(sums_ref)
    for lo_k, hi_k in ((0, 6), (6, NUM)):
        pairs = [(n, i, j) for n, (i, j) in enumerate(PAIRS) if lo_k <= j < hi_k]

        def body(r, accs, pairs=pairs, hi_k=hi_k):
            accs = list(accs)
            for c in range(2):
                for t in range(2):
                    vecs = [
                        p_ref[k, RIM + r, 8 * c : 8 * c + 8, 128 * t : 128 * t + 128]
                        for k in range(hi_k)
                    ]
                    for n, (_, i, j) in enumerate(pairs):
                        accs[n] = accs[n] + vecs[i] * vecs[j]
            return tuple(accs)

        accs = lax.fori_loop(0, ROWS, body, tuple(jnp.zeros((8, 128), F32) for _ in pairs))
        for (n, _, _), acc in zip(pairs, accs):
            sums_ref[n : n + 1, :] = jnp.sum(acc, axis=0, keepdims=True)
    gram = lax.dot_general(
        jnp.ones((128, 128), F32), sums_ref[...], (((1,), (1,)), ((), ())),
        precision=lax.Precision.HIGHEST, preferred_element_type=F32,
    )
    gram_ref[...] = gram
    for copy in outs:
        copy.wait()


def small_solve(gram):
    inv = 1.0 / SCALE

    def total(values):
        values = list(values)
        while len(values) > 1:
            nxt = [values[k] + values[k + 1] for k in range(0, len(values) - 1, 2)]
            if len(values) % 2:
                nxt.append(values[-1])
            values = nxt
        return values[0]

    def shifted(vec):
        out = []
        for k in range(len(vec) + 1):
            terms = [vec[m] for m in (k - 1, k + 1) if 0 <= m < len(vec)]
            parts = [total(terms) * inv] if terms else []
            if k < len(vec):
                parts.append(vec[k] * CENTRE)
            out.append(total(parts))
        return out

    def dot(one, two):
        return total(x * y for x, y in zip(one, two))

    first = jnp.sqrt(gram[0][0] + GUARD)
    inv_first = 1.0 / first
    basis = [[inv_first]]
    images = [[gram[k][0] * inv_first for k in range(NUM)]]
    cosines, sines, upper = [], [], []
    target = [first]
    for col in range(ITERS):
        work = shifted(basis[col])
        image = [dot(work, gram[k]) for k in range(NUM)]
        coeffs = [dot(basis[i], image) for i in range(col + 1)]
        work = [
            total([work[k]] + [-(coeffs[i] * basis[i][k]) for i in range(col + 1) if k < len(basis[i])])
            for k in range(len(work))
        ]
        image = [total([image[k]] + [-(coeffs[i] * images[i][k]) for i in range(col + 1)]) for k in range(NUM)]
        subdiag = jnp.sqrt(jnp.maximum(dot(work, image), 0.0) + GUARD)
        if col + 1 < ITERS:
            scale = 1.0 / subdiag
            basis.append([x * scale for x in work])
            images.append([x * scale for x in image])
        column = list(coeffs)
        for k in range(col):
            a, b = column[k], column[k + 1]
            column[k] = cosines[k] * a + sines[k] * b
            column[k + 1] = cosines[k] * b - sines[k] * a
        a, b = column[col], subdiag
        radius = jnp.sqrt(a * a + b * b)
        inv_radius = 1.0 / radius
        cosines.append(a * inv_radius)
        sines.append(b * inv_radius)
        column[col] = radius
        upper.append((column, inv_radius))
        last = target[col]
        target[col] = cosines[col] * last
        target.append(-(sines[col] * last))
    weights = [None] * ITERS
    for col in reversed(range(ITERS)):
        rest = [target[col]] + [-(upper[k][0][col] * weights[k]) for k in range(col + 1, ITERS)]
        weights[col] = total(rest) * upper[col][1]
    coef = [total([weights[j] * basis[j][k] for j in range(k, ITERS)]) for k in range(ITERS)]
    return coef, shifted(coef)


def final_kernel(p_ref, rows_ref, x_ref, r_ref, work_ref):
    summed = jnp.sum(rows_ref[...], axis=0, keepdims=True)
    gram = [[None] * NUM for _ in range(NUM)]
    for n, (i, j) in enumerate(PAIRS):
        gram[i][j] = gram[j][i] = jnp.broadcast_to(summed[:, n : n + 1], (8, 128))
    coef, image = small_solve(gram)
    for k in range(ITERS):
        work_ref[k] = coef[k]
    work_ref[ITERS] = 1.0 - image[0]
    for k in range(1, NUM):
        work_ref[ITERS + k] = -image[k]

    @pl.loop(0, ROWS // 8)
    def _(b):
        off = pl.multiple_of(b * 8, 8)
        for c in range(2):
            for t in range(2):
                xs = rs = None
                for k in range(NUM):
                    vec = p_ref[k, pl.ds(off, 8), 8 * c : 8 * c + 8, 128 * t : 128 * t + 128]
                    part = vec * work_ref[ITERS + k]
                    rs = part if rs is None else rs + part
                    if k < ITERS:
                        part = vec * work_ref[k]
                        xs = part if xs is None else xs + part
                where = (slice(8 * c, 8 * c + 8), pl.ds(off, 8), slice(128 * t, 128 * t + 128))
                x_ref[where] = jnp.swapaxes(xs, 0, 1)
                r_ref[where] = jnp.swapaxes(rs, 0, 1)


def diffusion_table(lat_total):
    row = np.arange(-RIM, lat_total + RIM, dtype=np.float64)
    phi = -math.pi / 2 + (row + 0.5) * (math.pi / lat_total)
    kx = DIFF_LON / (np.cos(phi) ** 2 + 0.1)
    kx = np.where((row >= 0) & (row < lat_total), kx, 0.0)
    return np.repeat(kx[:, None], 128, axis=1).astype(np.float32)


VMEM = pl.BlockSpec(memory_space=pltpu.VMEM)
ANY = pl.BlockSpec(memory_space=pl.ANY)


def shape(*dims):
    return jax.ShapeDtypeStruct(dims, F32)


def pairing(count, odd, closed):
    pairs = []
    for i in range(count):
        partner = i + 1 if (i % 2 == 0) != odd else i - 1
        if closed:
            partner %= count
        if 0 <= partner < count:
            pairs.append((i, partner))
    return pairs


def per_device(forcing, damping, coupling, wind_lon, wind_lat, *, nx, ny):
    s1, s2, x1, x2 = pl.pallas_call(
        pack_kernel,
        in_specs=[VMEM] * 4,
        out_specs=[VMEM] * 4,
        out_shape=[shape(34, 16, COLS)] * 2 + [shape(2, 72, 128)] * 2,
        name="pack",
    )(forcing, damping, wind_lon, wind_lat)
    g1 = lax.ppermute(x1, "gx", pairing(nx, False, True))
    g2 = lax.ppermute(x2, "gx", pairing(nx, True, True))
    r1 = lax.ppermute(s1, "gy", pairing(ny, False, False))
    r2 = lax.ppermute(s2, "gy", pairing(ny, True, False))
    both = jnp.stack([g1, g2])
    par_y = lax.rem(lax.axis_index("gy"), 2)
    k1 = lax.dynamic_index_in_dim(both, 1 - par_y, 1, keepdims=False)
    k2 = lax.dynamic_index_in_dim(both, par_y, 1, keepdims=False)
    c1 = lax.ppermute(k1, "gy", pairing(ny, False, False))
    c2 = lax.ppermute(k2, "gy", pairing(ny, True, False))
    table = jnp.asarray(diffusion_table(ny * ROWS))
    kron = jnp.kron(jnp.eye(8, dtype=F32), coupling * (COUPLE * SCALE))
    basis, gram = pl.pallas_call(
        main_kernel,
        in_specs=[ANY] * 4 + [VMEM] * 4 + [ANY, VMEM],
        out_specs=[ANY, VMEM],
        out_shape=[shape(NUM, ROWS, CH, COLS), shape(128, 128)],
        scratch_shapes=[
            pltpu.VMEM((NUM, EXT_ROWS, CH, EXT_COLS), F32),
            pltpu.VMEM((EXT_ROWS, CH, EXT_COLS), F32),
            pltpu.VMEM((2, EXT_ROWS, EXT_COLS), F32),
            pltpu.VMEM((EXT_ROWS, 128), F32),
            pltpu.VMEM((8, EXT_ROWS, EXT_COLS), F32),
            pltpu.VMEM((128, 128), F32),
            pltpu.SemaphoreType.DMA((13,)),
            pltpu.SemaphoreType.DMA((NUM,)),
        ],
        compiler_params=pltpu.CompilerParams(vmem_limit_bytes=40 * 2**20),
        name="powers",
    )(s1, s2, r1, r2, g1, g2, c1, c2, table, kron)
    rows = lax.all_to_all(gram, ("gx", "gy"), 0, 0, tiled=True)
    return pl.pallas_call(
        final_kernel,
        in_specs=[VMEM, VMEM],
        out_specs=[VMEM, VMEM],
        out_shape=[shape(CH, ROWS, COLS)] * 2,
        scratch_shapes=[pltpu.VMEM((ITERS + NUM, 8, 128), F32)],
        name="finish",
    )(basis, rows)


def solution(mesh):
    spec = P(None, "gy", "gx")
    flat = P("gy", "gx")
    return jax.shard_map(
        functools.partial(per_device, nx=mesh.shape["gx"], ny=mesh.shape["gy"]),
        mesh=mesh,
        in_specs=(spec, spec, P(), flat, flat),
        out_specs=(spec, spec),
        check_vma=False,
    )
```

time: 704 us -> 78.9 us (0.11); the launches traced: 691 us -> 77.9 us
  blocking collectives: 288 us -> 24.5 us
  other arithmetic: 128 us -> 0.83 us
  between operations: 117 us -> 0.71 us
  local copies, waits for them, and re-layouts: 94.7 us -> 5.37 us
  matrix products: 41.7 us -> 0 us
  Pallas kernels: 0 us -> 29.3 us
  waiting for transfers between devices: 13.4 us -> 5.81 us
    psum x36 -> x0, blocking collectives: 288 us -> none  [one_axis_at_a_time(): value = lax.psum(value, axis)]
    another operation x41 -> x0, other arithmetic: 44.4 us -> none
    dot_general x9 -> x0, matrix products: 41.7 us -> none  [apply_core(): jnp.einsum('ij,jab->iab', coupling, centre, precision=lax.Precision.HIGHEST)]
    div x15 -> x0, other arithmetic: 39.9 us -> none  [the longest x7 39.6 us: per_device(): krylov.append((applied / subdiag, rim_new))]
    slice x64 -> x0, local copies, waits for them, and re-layouts: 33.7 us -> none  [the longest x25 15.2 us: least_squares(): lower_val = column_vec[earlier + 1]]
    pallas_call x0 -> x3, Pallas kernels: none -> 29.3 us  [the longest x1 21.8 us: per_device(): pl.pallas_call(main_kernel, in_specs=[ANY] * 4 + [VMEM] * 4 + [ANY, VMEM]...]
    scatter x123 -> x0, local copies, waits for them, and re-layouts: 27.3 us -> none  [the longest x16 11.9 us: per_device(): heights.at[:column + 1, column].set(coeffs).at[column + 1, column]]
    all_to_all x0 -> x1, blocking collectives: none -> 24.5 us  [per_device(): rows = lax.all_to_all(gram, ('gx', 'gy'), 0, 0, tiled=True)]
  transfers between devices with their start and end apart: 4 -> 6, of which waited for: 2 -> 1; matrix products, arithmetic and copies ran while one was open for 2% -> 1% of each run, Pallas kernels for 0% -> 0%
where the time goes in v1:
time: 78.9 us; the launch traced here: 77.9 us
  Pallas kernels  29.3 us (37%)
  blocking collectives  24.5 us (31%)
  starting transfers between devices  11.3 us (14%)
  waiting for transfers between devices  5.81 us (7%)
  local copies, waits for them, and re-layouts  5.37 us (7%)
  other arithmetic  0.83 us (1%)
    all_to_all x1, blocking collectives, per_device(): rows = lax.all_to_all(gram, ('gx', 'gy'), 0, 0, tiled=True)  24.5 us
    pallas_call x1, Pallas kernels, per_device(): pl.pallas_call(main_kernel, in_specs=[ANY] * 4 + [VMEM] * 4 + [ANY, VMEM]...  21.8 us
    ppermute x1, waiting for transfers between devices, per_device(): c1 = lax.ppermute(k1, 'gy', pairing(ny, False, False))  5.79 us
    ppermute x1, starting transfers between devices, per_device(): c1 = lax.ppermute(k1, 'gy', pairing(ny, False, False))  5.23 us
    unnamed x8, local copies, waits for them, and re-layouts  5.19 us
    pallas_call x1, Pallas kernels, per_device(): pl.pallas_call(final_kernel, in_specs=[VMEM, VMEM], out_specs=[VMEM, VMEM...  4.95 us
    ppermute x1, starting transfers between devices, per_device(): g2 = lax.ppermute(x2, 'gx', pairing(nx, True, True))  3.24 us
    pallas_call x1, Pallas kernels, per_device(): pl.pallas_call(pack_kernel, in_specs=[VMEM] * 4, out_specs=[VMEM] * 4, ou...  2.56 us
  transfers between devices with their start and end apart: 6, of which 1 were waited for; matrix products, arithmetic and copies ran while one was open for 1% of the time, Pallas kernels for 0%

profile of v1, /device:TPU:0, one launch (start us, length us, event | category | flops | bytes accessed | tf_op | source)
XLA Modules:
  0.0 77.9 jit_solution(7586191143647196785)
XLA Ops:
  0.6 2.6 %pack.1 = (f32[34,16,256]{2,1,0:T(8,128)}, f32[34,16,256]{2,1,0:T(8,128)}, f32[2,72,128]{2,1,0:T(8,128)}, f32[2,72,128]{2,1,0:T(8,128)}) custom-call(f32[16,32,256]{2,1,0:T(8,128)} %f_ref.1, f32[16,32,256]{2,1,0:T(8,128)} %d_ref.1, f32[32,256]{1,0:T(8,128)} %wl_ref.1, f32[32,256]{1,0:T(8,128)} %wt_ref.1), custom_call_target="tpu_custom_call" | custom-call | tf_op jit(solution)/shard_map/pack/pallas_call | solution.py:368
  3.2 0.0 collective-permute-start.2
  3.2 3.2 %collective-permute-start.3 = (f32[2,72,128]{2,1,0:T(8,128)}, f32[2,72,128]{2,1,0:T(8,128)S(1)}, u32[]{:S(2)}, u32[]{:S(2)}) collective-permute-start(f32[2,72,128]{2,1,0:T(8,128)} %get-tuple-element.11), channel_id=1, source_target_pairs={{0,112},{16,32},{32,16},{48,64},{64,48},{80,96},{96,80},{112,0},{1... | collective-permute-start | bytes 221192 | tf_op jit(solution)/shard_map/ppermute | solution.py:376
  6.4 1.5 %collective-permute-start = (f32[34,16,256]{2,1,0:T(8,128)}, f32[34,16,256]{2,1,0:T(8,128)S(1)}, u32[]{:S(2)}, u32[]{:S(2)}) collective-permute-start(f32[34,16,256]{2,1,0:T(8,128)} %get-tuple-element.8.s1_ref), channel_id=1, source_target_pairs={{0,1},{1,0},{2,3},{3,2},{4,5},{5,4},{6,7},{7,6},{8,9},{9,8},{10,11... | collective-permute-start | bytes 1671176 | tf_op jit(solution)/shard_map/ppermute | solution.py:377
  7.9 0.7 collective-permute-start.1
  8.6 0.7 broadcast_multiply_fusion.1
  9.3 0.0 collective-permute-done.2.g1_ref
  9.3 0.0 collective-permute-done.3.g2_ref
  9.4 0.7 collective-permute-start.5
  10.0 5.2 %collective-permute-start.4 = (f32[2,72,128]{2,1,0:T(8,128)S(1)}, f32[2,72,128]{2,1,0:T(8,128)S(1)}, u32[]{:S(2)}, u32[]{:S(2)}) collective-permute-start(f32[2,72,128]{2,1,0:T(8,128)S(1)} %get-tuple-element.15), channel_id=1, source_target_pairs={{0,1},{1,0},{2,3},{3,2},{4,5},{5,4},{6,7},{7,6},{8,9},{9,8},{10,11... | collective-permute-start | bytes 221192 | tf_op jit(solution)/shard_map/ppermute | solution.py:383
  15.3 0.1 broadcast_multiply_fusion
  15.4 0.2 mul.35.kron_ref
  15.6 0.0 collective-permute-done.5.c2_ref
  15.6 5.8 %collective-permute-done.4.c1_ref = f32[2,72,128]{2,1,0:T(8,128)S(1)} collective-permute-done((f32[2,72,128]{2,1,0:T(8,128)S(1)}, f32[2,72,128]{2,1,0:T(8,128)S(1)}, u32[]{:S(2)}, u32[]{:S(2)}) %collective-permute-start.4) | collective-permute-done | bytes 73760 | tf_op jit(solution)/shard_map/ppermute | solution.py:383
  21.4 0.0 collective-permute-done.r1_ref
  21.4 0.0 collective-permute-done.1.r2_ref
  21.4 0.0 copy-start.1
  21.4 1.1 %copy-done.1 = f32[34,16,256]{2,1,0:T(8,128)S(1)} copy-done((f32[34,16,256]{2,1,0:T(8,128)S(1)}, f32[34,16,256]{2,1,0:T(8,128)}, u32[]{:S(2)}) %copy-start.1) | copy-done | bytes 557080
  22.4 0.0 copy-start.2
  22.4 1.1 %copy-done.2 = f32[34,16,256]{2,1,0:T(8,128)S(1)} copy-done((f32[34,16,256]{2,1,0:T(8,128)S(1)}, f32[34,16,256]{2,1,0:T(8,128)}, u32[]{:S(2)}) %copy-start.2) | copy-done | bytes 557080
  23.5 0.0 copy-start.3
  23.5 1.0 %copy-done.3 = f32[544,128]{1,0:T(8,128)S(1)} copy-done((f32[544,128]{1,0:T(8,128)S(1)}, f32[544,128]{1,0:T(8,128)}, u32[]{:S(2)}) %copy-start.3) | copy-done | bytes 278552
  24.4 21.8 %powers.1 = (f32[9,32,16,256]{3,2,1,0:T(8,128)S(1)}, f32[128,128]{1,0:T(8,128)S(1)}) custom-call(f32[34,16,256]{2,1,0:T(8,128)S(1)} %copy-done.1, f32[34,16,256]{2,1,0:T(8,128)S(1)} %copy-done.2, f32[34,16,256]{2,1,0:T(8,128)S(1)} %collective-permute-done.r1_ref, f32[34,16,256]{2,1,0:T(8,128)S(1)} %collective-permute-done.1.r2_ref, ...), custom_call_target="tpu_custom_call" | custom-call | tf_op jit(solution)/shard_map/powers/pallas_call | solution.py:387
  46.2 0.0 copy-start
  46.2 2.1 %copy-done = f32[9,32,16,256]{3,2,1,0:T(8,128)} copy-done((f32[9,32,16,256]{3,2,1,0:T(8,128)}, f32[9,32,16,256]{3,2,1,0:T(8,128)S(1)}, u32[]{:S(2)}) %copy-start) | copy-done | bytes 4718616
  48.4 24.5 %all_to_all.11 = f32[128,1,128]{2,1,0:T(1,128)} all-to-all(f32[128,1,128]{2,1,0:T(1,128)S(1)} %bitcast.14), channel_id=1, replica_groups=mesh['gx'=8,'gy'=16] {'gx','gy'}, dimensions={0} | all-to-all | bytes 131072 | tf_op jit(solution)/shard_map/all_to_all | solution.py:405
  72.9 4.9 %finish.1 = (f32[16,32,256]{2,1,0:T(8,128)}, f32[16,32,256]{2,1,0:T(8,128)}) custom-call(f32[9,32,16,256]{3,2,1,0:T(8,128)} %copy-done, f32[128,128]{1,0:T(8,128)} %bitcast.15), custom_call_target="tpu_custom_call" | custom-call | tf_op jit(solution)/shard_map/finish/pallas_call | solution.py:406
  (2 shorter events, 0.0 us)
Async XLA Ops:
  3.2 6.1 %collective-permute-start.2 = (f32[2,72,128]{2,1,0:T(8,128)}, f32[2,72,128]{2,1,0:T(8,128)S(1)}, u32[]{:S(2)}, u32[]{:S(2)}) collective-permute-start(f32[2,72,128]{2,1,0:T(8,128)} %get-tuple-element.10), channel_id=1, source_target_pairs={{0,16},{16,0},{32,48},{48,32},{64,80},{80,64},{96,112},{112,96},{1... | collective-permute-start | bytes 221192 | tf_op jit(solution)/shard_map/ppermute | solution.py:375
  3.2 6.1 %collective-permute-start.3 = (f32[2,72,128]{2,1,0:T(8,128)}, f32[2,72,128]{2,1,0:T(8,128)S(1)}, u32[]{:S(2)}, u32[]{:S(2)}) collective-permute-start(f32[2,72,128]{2,1,0:T(8,128)} %get-tuple-element.11), channel_id=1, source_target_pairs={{0,112},{16,32},{32,16},{48,64},{64,48},{80,96},{96,80},{112,0},{1... | collective-permute-start | bytes 221192 | tf_op jit(solution)/shard_map/ppermute | solution.py:376
  6.4 14.9 %collective-permute-start = (f32[34,16,256]{2,1,0:T(8,128)}, f32[34,16,256]{2,1,0:T(8,128)S(1)}, u32[]{:S(2)}, u32[]{:S(2)}) collective-permute-start(f32[34,16,256]{2,1,0:T(8,128)} %get-tuple-element.8.s1_ref), channel_id=1, source_target_pairs={{0,1},{1,0},{2,3},{3,2},{4,5},{5,4},{6,7},{7,6},{8,9},{9,8},{10,11... | collective-permute-start | bytes 1671176 | tf_op jit(solution)/shard_map/ppermute | solution.py:377
  7.9 13.5 %collective-permute-start.1 = (f32[34,16,256]{2,1,0:T(8,128)}, f32[34,16,256]{2,1,0:T(8,128)S(1)}, u32[]{:S(2)}, u32[]{:S(2)}) collective-permute-start(f32[34,16,256]{2,1,0:T(8,128)} %get-tuple-element.9.s2_ref), channel_id=1, source_target_pairs={{1,2},{2,1},{3,4},{4,3},{5,6},{6,5},{7,8},{8,7},{9,10},{10,9},{11,... | collective-permute-start | bytes 1671176 | tf_op jit(solution)/shard_map/ppermute | solution.py:378
  9.4 6.2 %collective-permute-start.5 = (f32[2,72,128]{2,1,0:T(8,128)S(1)}, f32[2,72,128]{2,1,0:T(8,128)S(1)}, u32[]{:S(2)}, u32[]{:S(2)}) collective-permute-start(f32[2,72,128]{2,1,0:T(8,128)S(1)} %get-tuple-element.14), channel_id=1, source_target_pairs={{1,2},{2,1},{3,4},{4,3},{5,6},{6,5},{7,8},{8,7},{9,10},{10,9},{11,... | collective-permute-start | bytes 221192 | tf_op jit(solution)/shard_map/ppermute | solution.py:384
  10.0 11.3 %collective-permute-start.4 = (f32[2,72,128]{2,1,0:T(8,128)S(1)}, f32[2,72,128]{2,1,0:T(8,128)S(1)}, u32[]{:S(2)}, u32[]{:S(2)}) collective-permute-start(f32[2,72,128]{2,1,0:T(8,128)S(1)} %get-tuple-element.15), channel_id=1, source_target_pairs={{0,1},{1,0},{2,3},{3,2},{4,5},{5,4},{6,7},{7,6},{8,9},{9,8},{10,11... | collective-permute-start | bytes 221192 | tf_op jit(solution)/shard_map/ppermute | solution.py:383
  21.4 1.1 %copy-start.1 = (f32[34,16,256]{2,1,0:T(8,128)S(1)}, f32[34,16,256]{2,1,0:T(8,128)}, u32[]{:S(2)}) copy-start(f32[34,16,256]{2,1,0:T(8,128)} %get-tuple-element.8.s1_ref) | copy-start | bytes 1671172
  22.4 1.1 %copy-start.2 = (f32[34,16,256]{2,1,0:T(8,128)S(1)}, f32[34,16,256]{2,1,0:T(8,128)}, u32[]{:S(2)}) copy-start(f32[34,16,256]{2,1,0:T(8,128)} %get-tuple-element.9.s2_ref) | copy-start | bytes 1671172
  23.5 1.0 %copy-start.3 = (f32[544,128]{1,0:T(8,128)S(1)}, f32[544,128]{1,0:T(8,128)}, u32[]{:S(2)}) copy-start(f32[544,128]{1,0:T(8,128)} %constant.23.clone.tab_ref) | copy-start | bytes 835588
  46.2 2.1 %copy-start = (f32[9,32,16,256]{3,2,1,0:T(8,128)}, f32[9,32,16,256]{3,2,1,0:T(8,128)S(1)}, u32[]{:S(2)}) copy-start(f32[9,32,16,256]{3,2,1,0:T(8,128)S(1)} %get-tuple-element.12.p_ref) | copy-start | bytes 14155780

commit v2 on v1

v2 whole, which is shorter than its diff:
```python
import functools
import math

import jax
import jax.numpy as jnp
import numpy as np
from jax import lax
from jax.experimental import pallas as pl
from jax.experimental.pallas import tpu as pltpu
from jax.sharding import PartitionSpec as P

ITERS = 8
CH = 16
ROWS = 32
COLS = 256
RIM = 2 * ITERS
EXT_ROWS = ROWS + 2 * RIM
EXT_COLS = COLS + 128
COUPLE = 0.25
DIFF_LAT = 0.5
DIFF_LON = 0.5
GUARD = 1.0

LOW, HIGH = 1.5, 26.0
CENTRE = (LOW + HIGH) / 2
SCALE = 4.0 / (HIGH - LOW)
NUM = ITERS + 1
PAIRS = [(i, j) for j in range(NUM) for i in range(j + 1)]
F32 = jnp.float32


def pack_kernel(f_ref, d_ref, wl_ref, wt_ref, s1_ref, s2_ref, x1_ref, x2_ref):
    par_y = lax.rem(lax.axis_index("gy"), 2)
    par_x = lax.rem(lax.axis_index("gx"), 2)
    for ref, half in ((s1_ref, 1 - par_y), (s2_ref, par_y)):
        for q in range(2):
            off = pl.multiple_of(half * 16 + 8 * q, 8)
            for src, base in ((f_ref, 0), (d_ref, 16)):
                for c in range(2):
                    ref[base + 8 * q : base + 8 * q + 8, 8 * c : 8 * c + 8, :] = jnp.swapaxes(
                        src[8 * c : 8 * c + 8, pl.ds(off, 8), :], 0, 1
                    )
        off = pl.multiple_of(half * 16, 16)
        ref[32] = wl_ref[pl.ds(off, 16), :]
        ref[33] = wt_ref[pl.ds(off, 16), :]
    group = lax.broadcasted_iota(jnp.int32, (8, 128), 1) // 16

    def gather(tiles):
        left = jnp.zeros((8, 128), F32)
        right = jnp.zeros((8, 128), F32)
        for g, (low, high) in enumerate(tiles):
            left = jnp.where(group == g, pltpu.roll(low, 16 * g, 1) if g else low, left)
            shift = (16 * g + 16) % 128
            right = jnp.where(group == g, pltpu.roll(high, shift, 1) if shift else high, right)
        return jnp.where(par_x == 0, right, left), jnp.where(par_x == 0, left, right)

    winds = gather(
        [
            (ref[8 * q : 8 * q + 8, :128], ref[8 * q : 8 * q + 8, 128:])
            for ref in (wl_ref, wt_ref)
            for q in range(4)
        ]
    )
    for half in range(2):
        slot = 0
        for base in (0, 16):
            for q in range(2):
                for c in range(2):
                    tiles = []
                    for g in range(8):
                        row = base + 8 * q + g
                        pick = []
                        for t in range(2):
                            one = s1_ref[row, 8 * c : 8 * c + 8, 128 * t : 128 * t + 128]
                            two = s2_ref[row, 8 * c : 8 * c + 8, 128 * t : 128 * t + 128]
                            pick.append(jnp.where(par_y == half, two, one))
                        tiles.append(tuple(pick))
                    first, second = gather(tiles)
                    x1_ref[half, 8 * slot : 8 * slot + 8, :] = first
                    x2_ref[half, 8 * slot : 8 * slot + 8, :] = second
                    slot += 1
        x1_ref[half, 64:72, :] = winds[0]
        x2_ref[half, 64:72, :] = winds[1]


LANE_SHAPE = (8, 128)


def place_half(src_ref, one, two, row, half, p0_ref, d_ref, coef_ref, k_ref):
    par_x = lax.rem(lax.axis_index("gx"), 2)
    lane = lax.broadcasted_iota(jnp.int32, LANE_SHAPE, 1)
    row = pl.multiple_of(row, 16)

    def spread(east, west, g):
        e = pltpu.roll(east, (128 - 16 * g) % 128, 1) if g else east
        shift = (112 - 16 * g) % 128
        w = pltpu.roll(west, shift, 1) if shift else west
        return jnp.where(lane < 16, e, jnp.where(lane >= 112, w, 0.0))

    def sides(slot):
        a = one(slice(8 * slot, 8 * slot + 8))
        b = two(slice(8 * slot, 8 * slot + 8))
        return jnp.where(par_x == 0, a, b), jnp.where(par_x == 0, b, a)

    east, west = sides(8)
    scales = []
    for q in range(2):
        rows = pl.ds(pl.multiple_of(row + 8 * q, 8), 8)
        k = k_ref[rows]
        live = jnp.where(k > 0.0, 1.0, 0.0)
        kx = k * SCALE
        half_lat = live * (SCALE * DIFF_LAT)
        fixed = live * (SCALE * (1.0 + 2.0 * DIFF_LAT - CENTRE)) + 2.0 * kx
        for t in range(3):
            lanes = slice(128 * t, 128 * t + 128)
            winds = []
            for field in range(2):
                if t < 2:
                    wind = src_ref[32 + field, 8 * q : 8 * q + 8, lanes]
                else:
                    low = spread(east, west, 4 * field + q)
                    high = spread(east, west, 4 * field + 2 + q)
                    wind = jnp.where(half == 0, low, high)
                winds.append(wind * (live * (SCALE / 12.0)))
            lon, lat = winds
            coef_ref[0, rows, lanes] = 8.0 * lon - kx
            coef_ref[1, rows, lanes] = -8.0 * lon - kx
            coef_ref[2, rows, lanes] = -lon
            coef_ref[3, rows, lanes] = 8.0 * lat - half_lat
            coef_ref[4, rows, lanes] = -8.0 * lat - half_lat
            coef_ref[5, rows, lanes] = -lat
        scales.append((live * SCALE, fixed))
    for q in range(2):
        for c in range(2):
            subs = slice(8 * c, 8 * c + 8)
            fe, fw = sides(2 * q + c)
            de, dw = sides(4 + 2 * q + c)
            for g in range(8):
                r = 8 * q + g
                p0_ref[row + r, subs, :COLS] = src_ref[r, subs]
                p0_ref[row + r, subs, COLS:] = spread(fe, fw, g)
                mul, add = (x[g : g + 1] for x in scales[q])
                for t in range(2):
                    lanes = slice(128 * t, 128 * t + 128)
                    d_ref[row + r, subs, lanes] = src_ref[16 + r, subs, lanes] * mul + add
                d_ref[row + r, subs, COLS:] = spread(de, dw, g) * mul + add


def split_kron(kron_ref):
    kron = kron_ref[...]
    hi = kron.astype(jnp.bfloat16)
    return hi, (kron - hi.astype(F32)).astype(jnp.bfloat16)


def run_blocks(blocks, p_refs, d_ref, coef_ref, kron, mix_refs):
    kron_hi, kron_lo = kron

    def mix(index):
        step, r0 = blocks[index]
        flat = p_refs[step - 1][r0 : r0 + 8].reshape(8 * CH, EXT_COLS)
        hi = flat.astype(jnp.bfloat16)
        lo = (flat - hi.astype(F32)).astype(jnp.bfloat16)
        mixed = jnp.dot(kron_hi, hi, preferred_element_type=F32)
        mixed = mixed + jnp.dot(kron_hi, lo, preferred_element_type=F32)
        mixed = mixed + jnp.dot(kron_lo, hi, preferred_element_type=F32)
        mix_refs[index % 2][...] = mixed.reshape(8, CH, EXT_COLS)

    mix(0)
    for index, (step, r0) in enumerate(blocks):
        more = index + 1 < len(blocks)
        late = more and blocks[index + 1][0] == step + 1 and abs(blocks[index + 1][1] - r0) < 8
        if more and not late:
            mix(index + 1)
        src, dst = p_refs[step - 1], p_refs[step]
        for i in range(8):
            r = r0 + i
            c = src[r]
            acc = mix_refs[index % 2][i] + d_ref[r] * c
            if step > 1:
                acc = acc - p_refs[step - 2][r]
            coef = [coef_ref[k, r : r + 1] for k in range(6)]
            acc = acc + coef[0] * pltpu.roll(c, EXT_COLS - 1, 1)
            acc = acc + coef[1] * pltpu.roll(c, 1, 1)
            acc = acc + coef[2] * (pltpu.roll(c, EXT_COLS - 2, 1) - pltpu.roll(c, 2, 1))
            acc = acc + coef[3] * src[r + 1]
            acc = acc + coef[4] * src[r - 1]
            acc = acc + coef[5] * (src[r + 2] - src[r - 2])
            dst[r] = acc
        if late:
            mix(index + 1)


def cover(low, high):
    return [min(r, high - 8) for r in range(low, high, 8)]


INNER_STEPS = 6
INNER = [(j, r) for j in range(1, INNER_STEPS + 1) for r in cover(RIM + 2 * j, RIM + ROWS - 2 * j)]
OUTER = [
    (j, r)
    for j in range(1, NUM)
    for r in (
        cover(2 * j, RIM + 2 * j) + cover(RIM + ROWS - 2 * j, EXT_ROWS - 2 * j)
        if j <= INNER_STEPS
        else cover(2 * j, EXT_ROWS - 2 * j)
    )
]


def inner_kernel(s1_ref, s2_ref, g1_ref, g2_ref, tab_ref, kron_ref, *refs):
    p_refs = refs[: INNER_STEPS + 1]
    d_ref, coef_ref, k_ref = refs[INNER_STEPS + 1 : INNER_STEPS + 4]
    mix_refs, sem = refs[INNER_STEPS + 4 : INNER_STEPS + 6], refs[-1]
    start = pl.multiple_of(lax.axis_index("gy") * ROWS, ROWS)
    copy = pltpu.make_async_copy(tab_ref.at[pl.ds(start, EXT_ROWS)], k_ref, sem)
    copy.start()
    par_y = lax.rem(lax.axis_index("gy"), 2)
    kron = split_kron(kron_ref)
    copy.wait()
    for src_ref, half in ((s1_ref, 1 - par_y), (s2_ref, par_y)):
        place_half(
            src_ref, lambda sl, h=half: g1_ref[h, sl], lambda sl, h=half: g2_ref[h, sl],
            RIM + 16 * half, half, p_refs[0], d_ref, coef_ref, k_ref,
        )
    run_blocks(INNER, p_refs, d_ref, coef_ref, kron, mix_refs)


def outer_kernel(r1_ref, r2_ref, c1_ref, c2_ref, k_ref, kron_ref, *refs):
    refs = refs[INNER_STEPS + 3 :]
    p_refs = refs[: INNER_STEPS + 1] + refs[INNER_STEPS + 3 : NUM + 2]
    d_ref, coef_ref = refs[INNER_STEPS + 1 : INNER_STEPS + 3]
    gram_ref, mix_a, mix_b, sums_ref = refs[NUM + 2 :]
    par_y = lax.rem(lax.axis_index("gy"), 2)
    kron = split_kron(kron_ref)
    for src_ref, c_ref, row, half in (
        (r1_ref, c1_ref, 48 - 48 * par_y, par_y),
        (r2_ref, c2_ref, 48 * par_y, 1 - par_y),
    ):
        place_half(
            src_ref, lambda sl, c=c_ref: c[0, sl], lambda sl, c=c_ref: c[1, sl],
            row, half, p_refs[0], d_ref, coef_ref, k_ref,
        )
    run_blocks(OUTER, p_refs, d_ref, coef_ref, kron, (mix_a, mix_b))

    sums_ref[...] = jnp.zeros_like(sums_ref)
    for lo_k, hi_k in ((0, 6), (6, NUM)):
        pairs = [(n, i, j) for n, (i, j) in enumerate(PAIRS) if lo_k <= j < hi_k]

        def body(r, accs, pairs=pairs, hi_k=hi_k):
            accs = list(accs)
            for u in range(2):
                for c in range(2):
                    for t in range(2):
                        vecs = [
                            p_refs[k][RIM + 2 * r + u, 8 * c : 8 * c + 8, 128 * t : 128 * t + 128]
                            for k in range(hi_k)
                        ]
                        for n, (_, i, j) in enumerate(pairs):
                            accs[n] = accs[n] + vecs[i] * vecs[j]
            return tuple(accs)

        accs = lax.fori_loop(0, ROWS // 2, body, tuple(jnp.zeros((8, 128), F32) for _ in pairs))
        for (n, _, _), acc in zip(pairs, accs):
            sums_ref[n : n + 1, :] = jnp.sum(acc, axis=0, keepdims=True)
    gram_ref[...] = lax.dot_general(
        jnp.ones((128, 128), F32), sums_ref[...], (((1,), (1,)), ((), ())),
        precision=lax.Precision.HIGHEST, preferred_element_type=F32,
    )


def small_solve(gram):
    inv = 1.0 / SCALE

    def total(values):
        values = list(values)
        while len(values) > 1:
            nxt = [values[k] + values[k + 1] for k in range(0, len(values) - 1, 2)]
            if len(values) % 2:
                nxt.append(values[-1])
            values = nxt
        return values[0]

    def shifted(vec):
        out = []
        for k in range(len(vec) + 1):
            terms = [vec[m] for m in (k - 1, k + 1) if 0 <= m < len(vec)]
            parts = [total(terms) * inv] if terms else []
            if k < len(vec):
                parts.append(vec[k] * CENTRE)
            out.append(total(parts))
        return out

    def dot(one, two):
        return total(x * y for x, y in zip(one, two))

    first = jnp.sqrt(gram[0][0] + GUARD)
    inv_first = 1.0 / first
    basis = [[inv_first]]
    images = [[gram[k][0] * inv_first for k in range(NUM)]]
    cosines, sines, upper = [], [], []
    target = [first]
    for col in range(ITERS):
        work = shifted(basis[col])
        image = [dot(work, gram[k]) for k in range(NUM)]
        coeffs = [dot(basis[i], image) for i in range(col + 1)]
        work = [
            total([work[k]] + [-(coeffs[i] * basis[i][k]) for i in range(col + 1) if k < len(basis[i])])
            for k in range(len(work))
        ]
        image = [total([image[k]] + [-(coeffs[i] * images[i][k]) for i in range(col + 1)]) for k in range(NUM)]
        subdiag = jnp.sqrt(jnp.maximum(dot(work, image), 0.0) + GUARD)
        if col + 1 < ITERS:
            scale = 1.0 / subdiag
            basis.append([x * scale for x in work])
            images.append([x * scale for x in image])
        column = list(coeffs)
        for k in range(col):
            a, b = column[k], column[k + 1]
            column[k] = cosines[k] * a + sines[k] * b
            column[k + 1] = cosines[k] * b - sines[k] * a
        a, b = column[col], subdiag
        radius = jnp.sqrt(a * a + b * b)
        inv_radius = 1.0 / radius
        cosines.append(a * inv_radius)
        sines.append(b * inv_radius)
        column[col] = radius
        upper.append((column, inv_radius))
        last = target[col]
        target[col] = cosines[col] * last
        target.append(-(sines[col] * last))
    weights = [None] * ITERS
    for col in reversed(range(ITERS)):
        rest = [target[col]] + [-(upper[k][0][col] * weights[k]) for k in range(col + 1, ITERS)]
        weights[col] = total(rest) * upper[col][1]
    coef = [total([weights[j] * basis[j][k] for j in range(k, ITERS)]) for k in range(ITERS)]
    return coef, shifted(coef)


def final_kernel(*refs):
    p_refs = refs[:NUM]
    rows_ref, x_ref, r_ref, xv_ref, rv_ref, work_ref, sem = refs[NUM:]
    summed = jnp.sum(rows_ref[...], axis=0, keepdims=True)
    gram = [[None] * NUM for _ in range(NUM)]
    for n, (i, j) in enumerate(PAIRS):
        gram[i][j] = gram[j][i] = jnp.broadcast_to(summed[:, n : n + 1], (8, 128))
    coef, image = small_solve(gram)
    for k in range(ITERS):
        work_ref[k] = coef[k]
    work_ref[ITERS] = 1.0 - image[0]
    for k in range(1, NUM):
        work_ref[ITERS + k] = -image[k]
    copies = []
    for b in range(ROWS // 8):
        rows = slice(8 * b, 8 * b + 8)
        for c in range(2):
            for t in range(2):
                xs = rs = None
                for k in range(NUM):
                    vec = p_refs[k][RIM + 8 * b : RIM + 8 * b + 8, 8 * c : 8 * c + 8, 128 * t : 128 * t + 128]
                    part = vec * work_ref[ITERS + k]
                    rs = part if rs is None else rs + part
                    if k < ITERS:
                        part = vec * work_ref[k]
                        xs = part if xs is None else xs + part
                where = (slice(8 * c, 8 * c + 8), rows, slice(128 * t, 128 * t + 128))
                xv_ref[where] = jnp.swapaxes(xs, 0, 1)
                rv_ref[where] = jnp.swapaxes(rs, 0, 1)
        for n, (src, dst) in enumerate(((xv_ref, x_ref), (rv_ref, r_ref))):
            copy = pltpu.make_async_copy(src.at[:, rows], dst.at[:, rows], sem.at[2 * b + n])
            copy.start()
            copies.append(copy)
    for copy in copies:
        copy.wait()


def diffusion_table(lat_total):
    row = np.arange(-RIM, lat_total + RIM, dtype=np.float64)
    phi = -math.pi / 2 + (row + 0.5) * (math.pi / lat_total)
    kx = DIFF_LON / (np.cos(phi) ** 2 + 0.1)
    kx = np.where((row >= 0) & (row < lat_total), kx, 0.0)
    return np.repeat(kx[:, None], 128, axis=1).astype(np.float32)


VMEM = pl.BlockSpec(memory_space=pltpu.VMEM)
HBM = pl.BlockSpec(memory_space=pltpu.HBM)


def shape(*dims):
    return jax.ShapeDtypeStruct(dims, F32)


def pairing(count, odd, closed):
    pairs = []
    for i in range(count):
        partner = i + 1 if (i % 2 == 0) != odd else i - 1
        if closed:
            partner %= count
        if 0 <= partner < count:
            pairs.append((i, partner))
    return pairs


def per_device(forcing, damping, coupling, wind_lon, wind_lat, *, nx, ny):
    s1, s2, x1, x2 = pl.pallas_call(
        pack_kernel,
        in_specs=[VMEM] * 4,
        out_specs=[VMEM] * 4,
        out_shape=[shape(34, 16, COLS)] * 2 + [shape(2, 72, 128)] * 2,
        compiler_params=pltpu.CompilerParams(vmem_limit_bytes=8 * 2**20),
        name="pack",
    )(forcing, damping, wind_lon, wind_lat)
    g1 = lax.ppermute(x1, "gx", pairing(nx, False, True))
    g2 = lax.ppermute(x2, "gx", pairing(nx, True, True))
    r1 = lax.ppermute(s1, "gy", pairing(ny, False, False))
    r2 = lax.ppermute(s2, "gy", pairing(ny, True, False))
    both = jnp.stack([g1, g2])
    par_y = lax.rem(lax.axis_index("gy"), 2)
    k1 = lax.dynamic_index_in_dim(both, 1 - par_y, 1, keepdims=False)
    k2 = lax.dynamic_index_in_dim(both, par_y, 1, keepdims=False)
    c1 = lax.ppermute(k1, "gy", pairing(ny, False, False))
    c2 = lax.ppermute(k2, "gy", pairing(ny, True, False))
    table = jnp.asarray(diffusion_table(ny * ROWS))
    kron = jnp.kron(jnp.eye(8, dtype=F32), coupling * (COUPLE * SCALE))
    field = shape(EXT_ROWS, CH, EXT_COLS)
    mix = [pltpu.VMEM((8, CH, EXT_COLS), F32)] * 2
    carried = [field] * (INNER_STEPS + 2) + [shape(6, EXT_ROWS, EXT_COLS)]
    *state, k_rows = pl.pallas_call(
        inner_kernel,
        in_specs=[VMEM] * 4 + [HBM, VMEM],
        out_specs=[VMEM] * (len(carried) + 1),
        out_shape=carried + [shape(EXT_ROWS, 128)],
        scratch_shapes=mix + [pltpu.SemaphoreType.DMA],
        compiler_params=pltpu.CompilerParams(vmem_limit_bytes=8 * 2**20),
        cost_estimate=pl.CostEstimate(flops=10**8, bytes_accessed=2**20, transcendentals=0),
        name="inner",
    )(s1, s2, g1, g2, table, kron)
    extra = [field] * (NUM - INNER_STEPS - 1)
    results = pl.pallas_call(
        outer_kernel,
        in_specs=[VMEM] * (6 + len(carried)),
        out_specs=[VMEM] * (len(carried) + len(extra) + 1),
        out_shape=carried + extra + [shape(128, 128)],
        input_output_aliases={6 + n: n for n in range(len(carried))},
        scratch_shapes=mix + [pltpu.VMEM((128, 128), F32)],
        compiler_params=pltpu.CompilerParams(vmem_limit_bytes=8 * 2**20),
        name="outer",
    )(r1, r2, c1, c2, k_rows, kron, *state)
    basis = results[: INNER_STEPS + 1] + results[len(carried) : -1]
    rows = lax.all_to_all(results[-1], ("gx", "gy"), 0, 0, tiled=True)
    return pl.pallas_call(
        final_kernel,
        in_specs=[VMEM] * (NUM + 1),
        out_specs=[HBM, HBM],
        out_shape=[shape(CH, ROWS, COLS)] * 2,
        scratch_shapes=[
            pltpu.VMEM((CH, ROWS, COLS), F32),
            pltpu.VMEM((CH, ROWS, COLS), F32),
            pltpu.VMEM((ITERS + NUM, 8, 128), F32),
            pltpu.SemaphoreType.DMA((ROWS // 4,)),
        ],
        compiler_params=pltpu.CompilerParams(vmem_limit_bytes=8 * 2**20),
        name="finish",
    )(*basis, rows)


def solution(mesh):
    spec = P(None, "gy", "gx")
    flat = P("gy", "gx")
    return jax.shard_map(
        functools.partial(per_device, nx=mesh.shape["gx"], ny=mesh.shape["gy"]),
        mesh=mesh,
        in_specs=(spec, spec, P(), flat, flat),
        out_specs=(spec, spec),
        check_vma=False,
    )
```

time: 78.9 us -> 59.7 us (0.76)
  Pallas kernels: 29.3 us -> 16 us
  waiting for transfers between devices: 5.81 us -> 1.77 us
  local copies, waits for them, and re-layouts: 5.37 us -> 3.78 us
    pallas_call x2 -> x3, Pallas kernels: 26.7 us -> 15.6 us  [the longest x1 9.6 us: per_device(): pl.pallas_call(outer_kernel, in_specs=[VMEM] * (6 + len(carried)), out_sp...]
    ppermute x1, waiting for transfers between devices: 5.79 us -> 1.76 us  [per_device(): c1 = lax.ppermute(k1, 'gy', pairing(ny, False, False))]
    pallas_call x1, Pallas kernels: 2.56 us -> 0.41 us  [per_device(): pl.pallas_call(pack_kernel, in_specs=[VMEM] * 4, out_specs=[VMEM] * 4, ou...]
    unnamed x8 -> x10, local copies, waits for them, and re-layouts: 5.19 us -> 3.59 us
  transfers between devices with their start and end apart: 6 -> 6, of which waited for: 1 -> 1; matrix products, arithmetic and copies ran while one was open for 1% -> 2% of each run, Pallas kernels for 0% -> 7%
where the time goes in v2:
time: 59.7 us; the launch traced here: 58.7 us
  blocking collectives  24.2 us (41%)
  Pallas kernels  16 us (27%)
  starting transfers between devices  11.4 us (19%)
  local copies, waits for them, and re-layouts  3.78 us (6%)
  waiting for transfers between devices  1.77 us (3%)
  other arithmetic  0.83 us (1%)
  between operations  0.73 us (1%)
    all_to_all x1, blocking collectives, per_device(): rows = lax.all_to_all(results[-1], ('gx', 'gy'), 0, 0, tiled=True)  24.2 us
    pallas_call x1, Pallas kernels, per_device(): pl.pallas_call(outer_kernel, in_specs=[VMEM] * (6 + len(carried)), out_sp...  9.6 us
    ppermute x1, starting transfers between devices, per_device(): c1 = lax.ppermute(k1, 'gy', pairing(ny, False, False))  5.24 us
    pallas_call x1, Pallas kernels, per_device(): pl.pallas_call(inner_kernel, in_specs=[VMEM] * 4 + [HBM, VMEM], out_specs...  3.84 us
    unnamed x10, local copies, waits for them, and re-layouts  3.59 us
    ppermute x1, starting transfers between devices, per_device(): g2 = lax.ppermute(x2, 'gx', pairing(nx, True, True))  3.23 us
    pallas_call x1, Pallas kernels, per_device(): pl.pallas_call(final_kernel, in_specs=[VMEM] * (NUM + 1), out_specs=[HBM,...  2.14 us
    ppermute x1, waiting for transfers between devices, per_device(): c1 = lax.ppermute(k1, 'gy', pairing(ny, False, False))  1.76 us
  transfers between devices with their start and end apart: 6, of which 1 were waited for; matrix products, arithmetic and copies ran while one was open for 2% of the time, Pallas kernels for 7%

profile of v2, /device:TPU:0, one launch (start us, length us, event | category | flops | bytes accessed | tf_op | source)
XLA Modules:
  0.0 58.7 jit_solution(13268152111360248145)
XLA Ops:
  0.6 0.0 copy-start
  0.6 1.0 %copy-done = f32[16,32,256]{2,1,0:T(8,128)S(1)} copy-done((f32[16,32,256]{2,1,0:T(8,128)S(1)}, f32[16,32,256]{2,1,0:T(8,128)}, u32[]{:S(2)}) %copy-start) | copy-done | bytes 524312
  1.7 0.0 copy-start.1
  1.7 1.0 %copy-done.1 = f32[16,32,256]{2,1,0:T(8,128)S(1)} copy-done((f32[16,32,256]{2,1,0:T(8,128)S(1)}, f32[16,32,256]{2,1,0:T(8,128)}, u32[]{:S(2)}) %copy-start.1) | copy-done | bytes 524312
  2.7 0.0 copy-start.3
  2.7 0.8 %copy-done.3 = f32[32,256]{1,0:T(8,128)S(1)} copy-done((f32[32,256]{1,0:T(8,128)S(1)}, f32[32,256]{1,0:T(8,128)}, u32[]{:S(2)}) %copy-start.3) | copy-done | bytes 32792
  3.5 0.0 copy-start.4
  3.5 0.8 %copy-done.4 = f32[32,256]{1,0:T(8,128)S(1)} copy-done((f32[32,256]{1,0:T(8,128)S(1)}, f32[32,256]{1,0:T(8,128)}, u32[]{:S(2)}) %copy-start.4) | copy-done | bytes 32792
  4.2 0.0 copy-start.2
  4.2 0.4 pack.1
  4.7 0.1 collective-permute-start.2
  4.8 3.2 %collective-permute-start.3 = (f32[2,72,128]{2,1,0:T(8,128)S(1)}, f32[2,72,128]{2,1,0:T(8,128)S(1)}, u32[]{:S(2)}, u32[]{:S(2)}) collective-permute-start(f32[2,72,128]{2,1,0:T(8,128)S(1)} %get-tuple-element.29), channel_id=1, source_target_pairs={{0,112},{16,32},{32,16},{48,64},{64,48},{80,96},{96,80},{112,0},{1... | collective-permute-start | bytes 221192 | tf_op jit(solution)/shard_map/ppermute | solution.py:413
  8.0 1.5 %collective-permute-start = (f32[34,16,256]{2,1,0:T(8,128)S(1)}, f32[34,16,256]{2,1,0:T(8,128)S(1)}, u32[]{:S(2)}, u32[]{:S(2)}) collective-permute-start(f32[34,16,256]{2,1,0:T(8,128)S(1)} %get-tuple-element.26.s1_ref), channel_id=1, source_target_pairs={{0,1},{1,0},{2,3},{3,2},{4,5},{5,4},{6,7},{7,6},{8,9},{9,8},{10,11... | collective-permute-start | bytes 1671176 | tf_op jit(solution)/shard_map/ppermute | solution.py:414
  9.5 0.7 %collective-permute-start.1 = (f32[34,16,256]{2,1,0:T(8,128)S(1)}, f32[34,16,256]{2,1,0:T(8,128)S(1)}, u32[]{:S(2)}, u32[]{:S(2)}) collective-permute-start(f32[34,16,256]{2,1,0:T(8,128)S(1)} %get-tuple-element.27.s2_ref), channel_id=1, source_target_pairs={{1,2},{2,1},{3,4},{4,3},{5,6},{6,5},{7,8},{8,7},{9,10},{10,9},{11,... | collective-permute-start | bytes 1671176 | tf_op jit(solution)/shard_map/ppermute | solution.py:415
  10.2 0.7 %broadcast_multiply_fusion.1 = f32[16,16]{1,0:T(8,128)S(1)} fusion(f32[16,16]{1,0:T(8,128)} %param.8), kind=kLoop, calls=%fused_computation.9 | loop fusion | flops 256 | bytes 2048 | tf_op jit(solution)/shard_map/mul | solution.py:423
  10.9 0.0 collective-permute-done.2.g1_ref
  10.9 0.0 collective-permute-done.3.g2_ref
  10.9 0.7 %collective-permute-start.5 = (f32[2,72,128]{2,1,0:T(8,128)S(1)}, f32[2,72,128]{2,1,0:T(8,128)S(1)}, u32[]{:S(2)}, u32[]{:S(2)}) collective-permute-start(f32[2,72,128]{2,1,0:T(8,128)S(1)} %get-tuple-element.50), channel_id=1, source_target_pairs={{1,2},{2,1},{3,4},{4,3},{5,6},{6,5},{7,8},{8,7},{9,10},{10,9},{11,... | collective-permute-start | bytes 221192 | tf_op jit(solution)/shard_map/ppermute | solution.py:421
  11.6 5.2 %collective-permute-start.4 = (f32[2,72,128]{2,1,0:T(8,128)S(1)}, f32[2,72,128]{2,1,0:T(8,128)S(1)}, u32[]{:S(2)}, u32[]{:S(2)}) collective-permute-start(f32[2,72,128]{2,1,0:T(8,128)S(1)} %get-tuple-element.51), channel_id=1, source_target_pairs={{0,1},{1,0},{2,3},{3,2},{4,5},{5,4},{6,7},{7,6},{8,9},{9,8},{10,11... | collective-permute-start | bytes 221192 | tf_op jit(solution)/shard_map/ppermute | solution.py:420
  16.8 0.1 broadcast_multiply_fusion
  16.9 0.2 mul.35.kron_ref
  17.1 0.0 copy-done.2
  17.1 3.8 %inner.1 = (f32[64,16,384]{2,1,0:T(8,128)S(1)}, f32[64,16,384]{2,1,0:T(8,128)S(1)}, f32[64,16,384]{2,1,0:T(8,128)S(1)}, f32[64,16,384]{2,1,0:T(8,128)S(1)}, f32[...) custom-call(f32[34,16,256]{2,1,0:T(8,128)S(1)} %get-tuple-element.26, ...), custom_call_target="tpu_custom_call" | custom-call | flops 100000000 | bytes 1048576 | tf_op jit(solution)/shard_map/inner/pallas_call | solution.py:427
  21.0 0.0 collective-permute-done.5.c2_ref
  21.0 1.8 %collective-permute-done.4.c1_ref = f32[2,72,128]{2,1,0:T(8,128)S(1)} collective-permute-done((f32[2,72,128]{2,1,0:T(8,128)S(1)}, f32[2,72,128]{2,1,0:T(8,128)S(1)}, u32[]{:S(2)}, u32[]{:S(2)}) %collective-permute-start.4) | collective-permute-done | bytes 73760 | tf_op jit(solution)/shard_map/ppermute | solution.py:420
  22.7 0.0 collective-permute-done.r1_ref
  22.7 0.0 collective-permute-done.1.r2_ref
  22.8 9.6 %outer.1 = (f32[64,16,384]{2,1,0:T(8,128)S(1)}, f32[64,16,384]{2,1,0:T(8,128)S(1)}, f32[64,16,384]{2,1,0:T(8,128)S(1)}, f32[64,16,384]{2,1,0:T(8,128)S(1)}, f32[...) custom-call(f32[34,16,256]{2,1,0:T(8,128)S(1)} %collective-permute-d, ...), custom_call_target="tpu_custom_call", output_to_operand_aliasing={{0}: (6, {}), {1}: (7, {}), {2}: (8, {}), {3}: (9, {}), {4}... | custom-call | tf_op jit(solution)/shard_map/outer/pallas_call | solution.py:438
  32.4 24.2 %all_to_all.11 = f32[128,1,128]{2,1,0:T(1,128)S(1)} all-to-all(f32[128,1,128]{2,1,0:T(1,128)S(1)} %bitcast.15), channel_id=1, replica_groups=mesh['gx'=8,'gy'=16] {'gx','gy'}, dimensions={0} | all-to-all | bytes 131072 | tf_op jit(solution)/shard_map/all_to_all | solution.py:449
  56.6 2.1 %finish.1 = (f32[16,32,256]{2,1,0:T(8,128)}, f32[16,32,256]{2,1,0:T(8,128)}) custom-call(f32[64,16,384]{2,1,0:T(8,128)S(1)} %get-tuple-element.40.refs_0_, f32[64,16,384]{2,1,0:T(8,128)S(1)} %get-tuple-element.41.refs_1_, f32[64,16,384]{2,1,0:T(8,128)S(1)} %get-tuple-element.42.refs_2_, f32[64,16,384]{2,1,0:T(8,128)S(1)} %get-tuple-element.43.refs_3_, ...), custom_call_target="tpu_custom_call" | custom-call | tf_op jit(solution)/shard_map/finish/pallas_call | solution.py:450
  (2 shorter events, 0.0 us)
Async XLA Ops:
  0.6 1.0 %copy-start = (f32[16,32,256]{2,1,0:T(8,128)S(1)}, f32[16,32,256]{2,1,0:T(8,128)}, u32[]{:S(2)}) copy-start(f32[16,32,256]{2,1,0:T(8,128)} %f_ref.1) | copy-start | bytes 1572868
  1.7 1.0 %copy-start.1 = (f32[16,32,256]{2,1,0:T(8,128)S(1)}, f32[16,32,256]{2,1,0:T(8,128)}, u32[]{:S(2)}) copy-start(f32[16,32,256]{2,1,0:T(8,128)} %d_ref.1) | copy-start | bytes 1572868
  2.7 0.8 %copy-start.3 = (f32[32,256]{1,0:T(8,128)S(1)}, f32[32,256]{1,0:T(8,128)}, u32[]{:S(2)}) copy-start(f32[32,256]{1,0:T(8,128)} %wl_ref.1) | copy-start | bytes 98308
  3.5 0.8 %copy-start.4 = (f32[32,256]{1,0:T(8,128)S(1)}, f32[32,256]{1,0:T(8,128)}, u32[]{:S(2)}) copy-start(f32[32,256]{1,0:T(8,128)} %wt_ref.1) | copy-start | bytes 98308
  4.2 12.9 %copy-start.2 = (f32[544,128]{1,0:T(8,128)S(1)}, f32[544,128]{1,0:T(8,128)}, u32[]{:S(2)}) copy-start(f32[544,128]{1,0:T(8,128)} %constant.23.clone.tab_ref) | copy-start | bytes 835588
  4.7 6.2 %collective-permute-start.2 = (f32[2,72,128]{2,1,0:T(8,128)S(1)}, f32[2,72,128]{2,1,0:T(8,128)S(1)}, u32[]{:S(2)}, u32[]{:S(2)}) collective-permute-start(f32[2,72,128]{2,1,0:T(8,128)S(1)} %get-tuple-element.28), channel_id=1, source_target_pairs={{0,16},{16,0},{32,48},{48,32},{64,80},{80,64},{96,112},{112,96},{1... | collective-permute-start | bytes 221192 | tf_op jit(solution)/shard_map/ppermute | solution.py:412
  4.8 6.1 %collective-permute-start.3 = (f32[2,72,128]{2,1,0:T(8,128)S(1)}, f32[2,72,128]{2,1,0:T(8,128)S(1)}, u32[]{:S(2)}, u32[]{:S(2)}) collective-permute-start(f32[2,72,128]{2,1,0:T(8,128)S(1)} %get-tuple-element.29), channel_id=1, source_target_pairs={{0,112},{16,32},{32,16},{48,64},{64,48},{80,96},{96,80},{112,0},{1... | collective-permute-start | bytes 221192 | tf_op jit(solution)/shard_map/ppermute | solution.py:413
  8.0 14.8 %collective-permute-start = (f32[34,16,256]{2,1,0:T(8,128)S(1)}, f32[34,16,256]{2,1,0:T(8,128)S(1)}, u32[]{:S(2)}, u32[]{:S(2)}) collective-permute-start(f32[34,16,256]{2,1,0:T(8,128)S(1)} %get-tuple-element.26.s1_ref), channel_id=1, source_target_pairs={{0,1},{1,0},{2,3},{3,2},{4,5},{5,4},{6,7},{7,6},{8,9},{9,8},{10,11... | collective-permute-start | bytes 1671176 | tf_op jit(solution)/shard_map/ppermute | solution.py:414
  9.5 13.3 %collective-permute-start.1 = (f32[34,16,256]{2,1,0:T(8,128)S(1)}, f32[34,16,256]{2,1,0:T(8,128)S(1)}, u32[]{:S(2)}, u32[]{:S(2)}) collective-permute-start(f32[34,16,256]{2,1,0:T(8,128)S(1)} %get-tuple-element.27.s2_ref), channel_id=1, source_target_pairs={{1,2},{2,1},{3,4},{4,3},{5,6},{6,5},{7,8},{8,7},{9,10},{10,9},{11,... | collective-permute-start | bytes 1671176 | tf_op jit(solution)/shard_map/ppermute | solution.py:415
  10.9 10.1 %collective-permute-start.5 = (f32[2,72,128]{2,1,0:T(8,128)S(1)}, f32[2,72,128]{2,1,0:T(8,128)S(1)}, u32[]{:S(2)}, u32[]{:S(2)}) collective-permute-start(f32[2,72,128]{2,1,0:T(8,128)S(1)} %get-tuple-element.50), channel_id=1, source_target_pairs={{1,2},{2,1},{3,4},{4,3},{5,6},{6,5},{7,8},{8,7},{9,10},{10,9},{11,... | collective-permute-start | bytes 221192 | tf_op jit(solution)/shard_map/ppermute | solution.py:421
  11.6 11.2 %collective-permute-start.4 = (f32[2,72,128]{2,1,0:T(8,128)S(1)}, f32[2,72,128]{2,1,0:T(8,128)S(1)}, u32[]{:S(2)}, u32[]{:S(2)}) collective-permute-start(f32[2,72,128]{2,1,0:T(8,128)S(1)} %get-tuple-element.51), channel_id=1, source_target_pairs={{0,1},{1,0},{2,3},{3,2},{4,5},{5,4},{6,7},{7,6},{8,9},{9,8},{10,11... | collective-permute-start | bytes 221192 | tf_op jit(solution)/shard_map/ppermute | solution.py:420

commit v3 on v2

--- a/solution.py
+++ b/solution.py
@@ -8,6 +8,7 @@
 from jax.experimental import pallas as pl
 from jax.experimental.pallas import tpu as pltpu
 from jax.sharding import PartitionSpec as P
+
 
 ITERS = 8
 CH = 16
@@ -29,7 +30,19 @@
 F32 = jnp.float32
 
 
-def pack_kernel(f_ref, d_ref, wl_ref, wt_ref, s1_ref, s2_ref, x1_ref, x2_ref):
+def pack_kernel(
+    f_hbm, d_hbm, wl_hbm, wt_hbm, s1_ref, s2_ref, x1_ref, x2_ref, f_ref, d_ref, wl_ref, wt_ref, sem
+):
+    copies = [
+        pltpu.make_async_copy(src, dst, sem.at[n])
+        for n, (src, dst) in enumerate(
+            ((f_hbm, f_ref), (d_hbm, d_ref), (wl_hbm, wl_ref), (wt_hbm, wt_ref))
+        )
+    ]
+    for copy in copies:
+        copy.start()
+    for copy in copies:
+        copy.wait()
     par_y = lax.rem(lax.axis_index("gy"), 2)
     par_x = lax.rem(lax.axis_index("gx"), 2)
     for ref, half in ((s1_ref, 1 - par_y), (s2_ref, par_y)):
@@ -403,16 +416,23 @@
 def per_device(forcing, damping, coupling, wind_lon, wind_lat, *, nx, ny):
     s1, s2, x1, x2 = pl.pallas_call(
         pack_kernel,
-        in_specs=[VMEM] * 4,
+        in_specs=[HBM] * 4,
         out_specs=[VMEM] * 4,
         out_shape=[shape(34, 16, COLS)] * 2 + [shape(2, 72, 128)] * 2,
+        scratch_shapes=[
+            pltpu.VMEM((CH, ROWS, COLS), F32),
+            pltpu.VMEM((CH, ROWS, COLS), F32),
+            pltpu.VMEM((ROWS, COLS), F32),
+            pltpu.VMEM((ROWS, COLS), F32),
+            pltpu.SemaphoreType.DMA((4,)),
+        ],
         compiler_params=pltpu.CompilerParams(vmem_limit_bytes=8 * 2**20),
         name="pack",
-    )(forcing, damping, wind_lon, wind_lat)
+    )(*(pltpu.with_memory_space_constraint(x, pltpu.HBM) for x in (forcing, damping, wind_lon, wind_lat)))
+    r1 = lax.ppermute(s1, "gy", pairing(ny, False, False))
+    r2 = lax.ppermute(s2, "gy", pairing(ny, True, False))
     g1 = lax.ppermute(x1, "gx", pairing(nx, False, True))
     g2 = lax.ppermute(x2, "gx", pairing(nx, True, True))
-    r1 = lax.ppermute(s1, "gy", pairing(ny, False, False))
-    r2 = lax.ppermute(s2, "gy", pairing(ny, True, False))
     both = jnp.stack([g1, g2])
     par_y = lax.rem(lax.axis_index("gy"), 2)
     k1 = lax.dynamic_index_in_dim(both, 1 - par_y, 1, keepdims=False)

time: 59.7 us -> 57.3 us (0.960)
  local copies, waits for them, and re-layouts: 3.78 us -> 0.19 us
  Pallas kernels: 16 us -> 17.3 us
    unnamed x10 -> x2, local copies, waits for them, and re-layouts: 3.59 us -> 0.01 us
    pallas_call x1, Pallas kernels: 0.41 us -> 1.71 us  [per_device(): pl.pallas_call(pack_kernel, in_specs=[HBM] * 4, out_specs=[VMEM] * 4, out...]
where the time goes in v3:
time: 57.3 us; the launch traced here: 56.4 us
  blocking collectives  24.2 us (42%)
  Pallas kernels  17.3 us (30%)
  starting transfers between devices  11.4 us (20%)
  waiting for transfers between devices  1.77 us (3%)
  other arithmetic  0.83 us (1%)
  between operations  0.73 us (1%)
    all_to_all x1, blocking collectives, per_device(): rows = lax.all_to_all(results[-1], ('gx', 'gy'), 0, 0, tiled=True)  24.2 us
    pallas_call x1, Pallas kernels, per_device(): pl.pallas_call(outer_kernel, in_specs=[VMEM] * (6 + len(carried)), out_sp...  9.6 us
    ppermute x1, starting transfers between devices, per_device(): c1 = lax.ppermute(k1, 'gy', pairing(ny, False, False))  5.24 us
    pallas_call x1, Pallas kernels, per_device(): pl.pallas_call(inner_kernel, in_specs=[VMEM] * 4 + [HBM, VMEM], out_specs...  3.84 us
    ppermute x1, starting transfers between devices, per_device(): g2 = lax.ppermute(x2, 'gx', pairing(nx, True, True))  3.23 us
    pallas_call x1, Pallas kernels, per_device(): pl.pallas_call(final_kernel, in_specs=[VMEM] * (NUM + 1), out_specs=[HBM,...  2.14 us
    ppermute x1, waiting for transfers between devices, per_device(): c1 = lax.ppermute(k1, 'gy', pairing(ny, False, False))  1.76 us
    pallas_call x1, Pallas kernels, per_device(): pl.pallas_call(pack_kernel, in_specs=[HBM] * 4, out_specs=[VMEM] * 4, out...  1.71 us
  transfers between devices with their start and end apart: 6, of which 1 were waited for; matrix products, arithmetic and copies ran while one was open for 2% of the time, Pallas kernels for 7%

profile of v3, /device:TPU:0, one launch (start us, length us, event | category | flops | bytes accessed | tf_op | source)
XLA Modules:
  0.0 56.4 jit_solution(15488771708964685556)
XLA Ops:
  0.6 0.0 copy-start
  0.6 1.7 %pack.1 = (f32[34,16,256]{2,1,0:T(8,128)S(1)}, f32[34,16,256]{2,1,0:T(8,128)S(1)}, f32[2,72,128]{2,1,0:T(8,128)S(1)}, f32[2,72,128]{2,1,0:T(8,128)S(1)}) custom-call(f32[16,32,256]{2,1,0:T(8,128)} %f_hbm.1, f32[16,32,256]{2,1,0:T(8,128)} %d_hbm.1, f32[32,256]{1,0:T(8,128)} %wl_hbm.1, f32[32,256]{1,0:T(8,128)} %wt_hbm.1), custom_call_target="tpu_custom_call" | custom-call | tf_op jit(solution)/shard_map/pack/pallas_call | solution.py:417
  2.4 0.1 collective-permute-start.2
  2.4 3.2 %collective-permute-start.3 = (f32[2,72,128]{2,1,0:T(8,128)S(1)}, f32[2,72,128]{2,1,0:T(8,128)S(1)}, u32[]{:S(2)}, u32[]{:S(2)}) collective-permute-start(f32[2,72,128]{2,1,0:T(8,128)S(1)} %get-tuple-element.29), channel_id=1, source_target_pairs={{0,112},{16,32},{32,16},{48,64},{64,48},{80,96},{96,80},{112,0},{1... | collective-permute-start | bytes 221192 | tf_op jit(solution)/shard_map/ppermute | solution.py:435
  5.7 1.5 %collective-permute-start = (f32[34,16,256]{2,1,0:T(8,128)S(1)}, f32[34,16,256]{2,1,0:T(8,128)S(1)}, u32[]{:S(2)}, u32[]{:S(2)}) collective-permute-start(f32[34,16,256]{2,1,0:T(8,128)S(1)} %get-tuple-element.26.s1_ref), channel_id=1, source_target_pairs={{0,1},{1,0},{2,3},{3,2},{4,5},{5,4},{6,7},{7,6},{8,9},{9,8},{10,11... | collective-permute-start | bytes 1671176 | tf_op jit(solution)/shard_map/ppermute | solution.py:432
  7.2 0.7 %collective-permute-start.1 = (f32[34,16,256]{2,1,0:T(8,128)S(1)}, f32[34,16,256]{2,1,0:T(8,128)S(1)}, u32[]{:S(2)}, u32[]{:S(2)}) collective-permute-start(f32[34,16,256]{2,1,0:T(8,128)S(1)} %get-tuple-element.27.s2_ref), channel_id=1, source_target_pairs={{1,2},{2,1},{3,4},{4,3},{5,6},{6,5},{7,8},{8,7},{9,10},{10,9},{11,... | collective-permute-start | bytes 1671176 | tf_op jit(solution)/shard_map/ppermute | solution.py:433
  7.9 0.7 %broadcast_multiply_fusion.1 = f32[16,16]{1,0:T(8,128)S(1)} fusion(f32[16,16]{1,0:T(8,128)} %param.8), kind=kLoop, calls=%fused_computation.9 | loop fusion | flops 256 | bytes 2048 | tf_op jit(solution)/shard_map/mul | solution.py:443
  8.6 0.0 collective-permute-done.2.g1_ref
  8.6 0.0 collective-permute-done.3.g2_ref
  8.6 0.7 %collective-permute-start.5 = (f32[2,72,128]{2,1,0:T(8,128)S(1)}, f32[2,72,128]{2,1,0:T(8,128)S(1)}, u32[]{:S(2)}, u32[]{:S(2)}) collective-permute-start(f32[2,72,128]{2,1,0:T(8,128)S(1)} %get-tuple-element.50), channel_id=1, source_target_pairs={{1,2},{2,1},{3,4},{4,3},{5,6},{6,5},{7,8},{8,7},{9,10},{10,9},{11,... | collective-permute-start | bytes 221192 | tf_op jit(solution)/shard_map/ppermute | solution.py:441
  9.3 5.2 %collective-permute-start.4 = (f32[2,72,128]{2,1,0:T(8,128)S(1)}, f32[2,72,128]{2,1,0:T(8,128)S(1)}, u32[]{:S(2)}, u32[]{:S(2)}) collective-permute-start(f32[2,72,128]{2,1,0:T(8,128)S(1)} %get-tuple-element.51), channel_id=1, source_target_pairs={{0,1},{1,0},{2,3},{3,2},{4,5},{5,4},{6,7},{7,6},{8,9},{9,8},{10,11... | collective-permute-start | bytes 221192 | tf_op jit(solution)/shard_map/ppermute | solution.py:440
  14.5 0.1 broadcast_multiply_fusion
  14.6 0.2 mul.35.kron_ref
  14.8 0.0 copy-done
  14.8 3.8 %inner.1 = (f32[64,16,384]{2,1,0:T(8,128)S(1)}, f32[64,16,384]{2,1,0:T(8,128)S(1)}, f32[64,16,384]{2,1,0:T(8,128)S(1)}, f32[64,16,384]{2,1,0:T(8,128)S(1)}, f32[...) custom-call(f32[34,16,256]{2,1,0:T(8,128)S(1)} %get-tuple-element.26, ...), custom_call_target="tpu_custom_call" | custom-call | flops 100000000 | bytes 1048576 | tf_op jit(solution)/shard_map/inner/pallas_call | solution.py:447
  18.7 0.0 collective-permute-done.5.c2_ref
  18.7 1.8 %collective-permute-done.4.c1_ref = f32[2,72,128]{2,1,0:T(8,128)S(1)} collective-permute-done((f32[2,72,128]{2,1,0:T(8,128)S(1)}, f32[2,72,128]{2,1,0:T(8,128)S(1)}, u32[]{:S(2)}, u32[]{:S(2)}) %collective-permute-start.4) | collective-permute-done | bytes 73760 | tf_op jit(solution)/shard_map/ppermute | solution.py:440
  20.4 0.0 collective-permute-done.r1_ref
  20.4 0.0 collective-permute-done.1.r2_ref
  20.4 9.6 %outer.1 = (f32[64,16,384]{2,1,0:T(8,128)S(1)}, f32[64,16,384]{2,1,0:T(8,128)S(1)}, f32[64,16,384]{2,1,0:T(8,128)S(1)}, f32[64,16,384]{2,1,0:T(8,128)S(1)}, f32[...) custom-call(f32[34,16,256]{2,1,0:T(8,128)S(1)} %collective-permute-d, ...), custom_call_target="tpu_custom_call", output_to_operand_aliasing={{0}: (6, {}), {1}: (7, {}), {2}: (8, {}), {3}: (9, {}), {4}... | custom-call | tf_op jit(solution)/shard_map/outer/pallas_call | solution.py:458
  30.1 24.2 %all_to_all.11 = f32[128,1,128]{2,1,0:T(1,128)S(1)} all-to-all(f32[128,1,128]{2,1,0:T(1,128)S(1)} %bitcast.15), channel_id=1, replica_groups=mesh['gx'=8,'gy'=16] {'gx','gy'}, dimensions={0} | all-to-all | bytes 131072 | tf_op jit(solution)/shard_map/all_to_all | solution.py:469
  54.3 2.1 %finish.1 = (f32[16,32,256]{2,1,0:T(8,128)}, f32[16,32,256]{2,1,0:T(8,128)}) custom-call(f32[64,16,384]{2,1,0:T(8,128)S(1)} %get-tuple-element.40.refs_0_, f32[64,16,384]{2,1,0:T(8,128)S(1)} %get-tuple-element.41.refs_1_, f32[64,16,384]{2,1,0:T(8,128)S(1)} %get-tuple-element.42.refs_2_, f32[64,16,384]{2,1,0:T(8,128)S(1)} %get-tuple-element.43.refs_3_, ...), custom_call_target="tpu_custom_call" | custom-call | tf_op jit(solution)/shard_map/finish/pallas_call | solution.py:470
  (2 shorter events, 0.0 us)
Async XLA Ops:
  0.6 14.2 %copy-start = (f32[544,128]{1,0:T(8,128)S(1)}, f32[544,128]{1,0:T(8,128)}, u32[]{:S(2)}) copy-start(f32[544,128]{1,0:T(8,128)} %constant.23.clone.tab_ref) | copy-start | bytes 835588
  2.4 6.2 %collective-permute-start.2 = (f32[2,72,128]{2,1,0:T(8,128)S(1)}, f32[2,72,128]{2,1,0:T(8,128)S(1)}, u32[]{:S(2)}, u32[]{:S(2)}) collective-permute-start(f32[2,72,128]{2,1,0:T(8,128)S(1)} %get-tuple-element.28), channel_id=1, source_target_pairs={{0,16},{16,0},{32,48},{48,32},{64,80},{80,64},{96,112},{112,96},{1... | collective-permute-start | bytes 221192 | tf_op jit(solution)/shard_map/ppermute | solution.py:434
  2.4 6.1 %collective-permute-start.3 = (f32[2,72,128]{2,1,0:T(8,128)S(1)}, f32[2,72,128]{2,1,0:T(8,128)S(1)}, u32[]{:S(2)}, u32[]{:S(2)}) collective-permute-start(f32[2,72,128]{2,1,0:T(8,128)S(1)} %get-tuple-element.29), channel_id=1, source_target_pairs={{0,112},{16,32},{32,16},{48,64},{64,48},{80,96},{96,80},{112,0},{1... | collective-permute-start | bytes 221192 | tf_op jit(solution)/shard_map/ppermute | solution.py:435
  5.7 14.8 %collective-permute-start = (f32[34,16,256]{2,1,0:T(8,128)S(1)}, f32[34,16,256]{2,1,0:T(8,128)S(1)}, u32[]{:S(2)}, u32[]{:S(2)}) collective-permute-start(f32[34,16,256]{2,1,0:T(8,128)S(1)} %get-tuple-element.26.s1_ref), channel_id=1, source_target_pairs={{0,1},{1,0},{2,3},{3,2},{4,5},{5,4},{6,7},{7,6},{8,9},{9,8},{10,11... | collective-permute-start | bytes 1671176 | tf_op jit(solution)/shard_map/ppermute | solution.py:432
  7.2 13.3 %collective-permute-start.1 = (f32[34,16,256]{2,1,0:T(8,128)S(1)}, f32[34,16,256]{2,1,0:T(8,128)S(1)}, u32[]{:S(2)}, u32[]{:S(2)}) collective-permute-start(f32[34,16,256]{2,1,0:T(8,128)S(1)} %get-tuple-element.27.s2_ref), channel_id=1, source_target_pairs={{1,2},{2,1},{3,4},{4,3},{5,6},{6,5},{7,8},{8,7},{9,10},{10,9},{11,... | collective-permute-start | bytes 1671176 | tf_op jit(solution)/shard_map/ppermute | solution.py:433
  8.6 10.1 %collective-permute-start.5 = (f32[2,72,128]{2,1,0:T(8,128)S(1)}, f32[2,72,128]{2,1,0:T(8,128)S(1)}, u32[]{:S(2)}, u32[]{:S(2)}) collective-permute-start(f32[2,72,128]{2,1,0:T(8,128)S(1)} %get-tuple-element.50), channel_id=1, source_target_pairs={{1,2},{2,1},{3,4},{4,3},{5,6},{6,5},{7,8},{8,7},{9,10},{10,9},{11,... | collective-permute-start | bytes 221192 | tf_op jit(solution)/shard_map/ppermute | solution.py:441
  9.3 11.2 %collective-permute-start.4 = (f32[2,72,128]{2,1,0:T(8,128)S(1)}, f32[2,72,128]{2,1,0:T(8,128)S(1)}, u32[]{:S(2)}, u32[]{:S(2)}) collective-permute-start(f32[2,72,128]{2,1,0:T(8,128)S(1)} %get-tuple-element.51), channel_id=1, source_target_pairs={{0,1},{1,0},{2,3},{3,2},{4,5},{5,4},{6,7},{7,6},{8,9},{9,8},{10,11... | collective-permute-start | bytes 221192 | tf_op jit(solution)/shard_map/ppermute | solution.py:440

commit v4 on v3

--- a/solution.py
+++ b/solution.py
@@ -31,12 +31,18 @@
 
 
 def pack_kernel(
-    f_hbm, d_hbm, wl_hbm, wt_hbm, s1_ref, s2_ref, x1_ref, x2_ref, f_ref, d_ref, wl_ref, wt_ref, sem
+    f_hbm, d_hbm, wl_hbm, wt_hbm, cp_hbm, tab_hbm,
+    s1_ref, s2_ref, x1_ref, x2_ref, cp_ref, k_ref,
+    f_ref, d_ref, wl_ref, wt_ref, sem,
 ):
+    start = pl.multiple_of(lax.axis_index("gy") * ROWS, ROWS)
     copies = [
         pltpu.make_async_copy(src, dst, sem.at[n])
         for n, (src, dst) in enumerate(
-            ((f_hbm, f_ref), (d_hbm, d_ref), (wl_hbm, wl_ref), (wt_hbm, wt_ref))
+            (
+                (f_hbm, f_ref), (d_hbm, d_ref), (wl_hbm, wl_ref), (wt_hbm, wt_ref),
+                (cp_hbm, cp_ref), (tab_hbm.at[pl.ds(start, EXT_ROWS)], k_ref),
+            )
         )
     ]
     for copy in copies:
@@ -185,20 +191,21 @@
         if more and not late:
             mix(index + 1)
         src, dst = p_refs[step - 1], p_refs[step]
-        for i in range(8):
-            r = r0 + i
-            c = src[r]
-            acc = mix_refs[index % 2][i] + d_ref[r] * c
-            if step > 1:
-                acc = acc - p_refs[step - 2][r]
-            coef = [coef_ref[k, r : r + 1] for k in range(6)]
-            acc = acc + coef[0] * pltpu.roll(c, EXT_COLS - 1, 1)
-            acc = acc + coef[1] * pltpu.roll(c, 1, 1)
-            acc = acc + coef[2] * (pltpu.roll(c, EXT_COLS - 2, 1) - pltpu.roll(c, 2, 1))
-            acc = acc + coef[3] * src[r + 1]
-            acc = acc + coef[4] * src[r - 1]
-            acc = acc + coef[5] * (src[r + 2] - src[r - 2])
-            dst[r] = acc
+        for s in (slice(0, 8), slice(8, 16)):
+            for i in range(8):
+                r = r0 + i
+                c = src[r, s]
+                acc = mix_refs[index % 2][i, s] + d_ref[r, s] * c
+                if step > 1:
+                    acc = acc - p_refs[step - 2][r, s]
+                coef = [coef_ref[k, r : r + 1] for k in range(6)]
+                acc = acc + coef[0] * pltpu.roll(c, EXT_COLS - 1, 1)
+                acc = acc + coef[1] * pltpu.roll(c, 1, 1)
+                acc = acc + coef[2] * (pltpu.roll(c, EXT_COLS - 2, 1) - pltpu.roll(c, 2, 1))
+                acc = acc + coef[3] * src[r + 1, s]
+                acc = acc + coef[4] * src[r - 1, s]
+                acc = acc + coef[5] * (src[r + 2, s] - src[r - 2, s])
+                dst[r, s] = acc
         if late:
             mix(index + 1)
 
@@ -220,22 +227,31 @@
 ]
 
 
-def inner_kernel(s1_ref, s2_ref, g1_ref, g2_ref, tab_ref, kron_ref, *refs):
+def inner_kernel(s1_ref, s2_ref, g1_ref, g2_ref, cp_ref, k_ref, *refs):
     p_refs = refs[: INNER_STEPS + 1]
-    d_ref, coef_ref, k_ref = refs[INNER_STEPS + 1 : INNER_STEPS + 4]
-    mix_refs, sem = refs[INNER_STEPS + 4 : INNER_STEPS + 6], refs[-1]
-    start = pl.multiple_of(lax.axis_index("gy") * ROWS, ROWS)
-    copy = pltpu.make_async_copy(tab_ref.at[pl.ds(start, EXT_ROWS)], k_ref, sem)
-    copy.start()
+    d_ref, coef_ref, k1_ref, k2_ref, kron_ref, *mix_refs = refs[INNER_STEPS + 1 :]
     par_y = lax.rem(lax.axis_index("gy"), 2)
-    kron = split_kron(kron_ref)
-    copy.wait()
+    for n, g_ref in enumerate((g1_ref, g2_ref)):
+        k1_ref[n] = g_ref[1 - par_y]
+        k2_ref[n] = g_ref[par_y]
+    size = 8 * CH
+    pick = lax.broadcasted_iota(jnp.int32, (size, CH), 0) % CH
+    pick = (pick == lax.broadcasted_iota(jnp.int32, (size, CH), 1)).astype(F32)
+    tall = jnp.dot(
+        pick, cp_ref[...] * (COUPLE * SCALE), precision=lax.Precision.HIGHEST, preferred_element_type=F32
+    )
+    full = lax.dot_general(
+        tall, pick, (((1,), (1,)), ((), ())), precision=lax.Precision.HIGHEST, preferred_element_type=F32
+    )
+    row = lax.broadcasted_iota(jnp.int32, (size, size), 0) // CH
+    col = lax.broadcasted_iota(jnp.int32, (size, size), 1) // CH
+    kron_ref[...] = jnp.where(row == col, full, 0.0)
     for src_ref, half in ((s1_ref, 1 - par_y), (s2_ref, par_y)):
         place_half(
             src_ref, lambda sl, h=half: g1_ref[h, sl], lambda sl, h=half: g2_ref[h, sl],
             RIM + 16 * half, half, p_refs[0], d_ref, coef_ref, k_ref,
         )
-    run_blocks(INNER, p_refs, d_ref, coef_ref, kron, mix_refs)
+    run_blocks(INNER, p_refs, d_ref, coef_ref, split_kron(kron_ref), mix_refs)
 
 
 def outer_kernel(r1_ref, r2_ref, c1_ref, c2_ref, k_ref, kron_ref, *refs):
@@ -414,46 +430,43 @@
 
 
 def per_device(forcing, damping, coupling, wind_lon, wind_lat, *, nx, ny):
-    s1, s2, x1, x2 = pl.pallas_call(
+    inputs = (forcing, damping, wind_lon, wind_lat, coupling, jnp.asarray(diffusion_table(ny * ROWS)))
+    s1, s2, x1, x2, couple, k_rows = pl.pallas_call(
         pack_kernel,
-        in_specs=[HBM] * 4,
-        out_specs=[VMEM] * 4,
-        out_shape=[shape(34, 16, COLS)] * 2 + [shape(2, 72, 128)] * 2,
+        in_specs=[HBM] * 6,
+        out_specs=[VMEM] * 6,
+        out_shape=[shape(34, 16, COLS)] * 2
+        + [shape(2, 72, 128)] * 2
+        + [shape(CH, CH), shape(EXT_ROWS, 128)],
         scratch_shapes=[
             pltpu.VMEM((CH, ROWS, COLS), F32),
             pltpu.VMEM((CH, ROWS, COLS), F32),
             pltpu.VMEM((ROWS, COLS), F32),
             pltpu.VMEM((ROWS, COLS), F32),
-            pltpu.SemaphoreType.DMA((4,)),
+            pltpu.SemaphoreType.DMA((6,)),
         ],
         compiler_params=pltpu.CompilerParams(vmem_limit_bytes=8 * 2**20),
         name="pack",
-    )(*(pltpu.with_memory_space_constraint(x, pltpu.HBM) for x in (forcing, damping, wind_lon, wind_lat)))
+    )(*(pltpu.with_memory_space_constraint(x, pltpu.HBM) for x in inputs))
     r1 = lax.ppermute(s1, "gy", pairing(ny, False, False))
     r2 = lax.ppermute(s2, "gy", pairing(ny, True, False))
     g1 = lax.ppermute(x1, "gx", pairing(nx, False, True))
     g2 = lax.ppermute(x2, "gx", pairing(nx, True, True))
-    both = jnp.stack([g1, g2])
-    par_y = lax.rem(lax.axis_index("gy"), 2)
-    k1 = lax.dynamic_index_in_dim(both, 1 - par_y, 1, keepdims=False)
-    k2 = lax.dynamic_index_in_dim(both, par_y, 1, keepdims=False)
-    c1 = lax.ppermute(k1, "gy", pairing(ny, False, False))
-    c2 = lax.ppermute(k2, "gy", pairing(ny, True, False))
-    table = jnp.asarray(diffusion_table(ny * ROWS))
-    kron = jnp.kron(jnp.eye(8, dtype=F32), coupling * (COUPLE * SCALE))
     field = shape(EXT_ROWS, CH, EXT_COLS)
     mix = [pltpu.VMEM((8, CH, EXT_COLS), F32)] * 2
     carried = [field] * (INNER_STEPS + 2) + [shape(6, EXT_ROWS, EXT_COLS)]
-    *state, k_rows = pl.pallas_call(
+    *state, k1, k2, kron = pl.pallas_call(
         inner_kernel,
-        in_specs=[VMEM] * 4 + [HBM, VMEM],
-        out_specs=[VMEM] * (len(carried) + 1),
-        out_shape=carried + [shape(EXT_ROWS, 128)],
-        scratch_shapes=mix + [pltpu.SemaphoreType.DMA],
+        in_specs=[VMEM] * 6,
+        out_specs=[VMEM] * (len(carried) + 3),
+        out_shape=carried + [shape(2, 72, 128)] * 2 + [shape(8 * CH, 8 * CH)],
+        scratch_shapes=mix,
         compiler_params=pltpu.CompilerParams(vmem_limit_bytes=8 * 2**20),
         cost_estimate=pl.CostEstimate(flops=10**8, bytes_accessed=2**20, transcendentals=0),
         name="inner",
-    )(s1, s2, g1, g2, table, kron)
+    )(s1, s2, g1, g2, couple, k_rows)
+    c1 = lax.ppermute(k1, "gy", pairing(ny, False, False))
+    c2 = lax.ppermute(k2, "gy", pairing(ny, True, False))
     extra = [field] * (NUM - INNER_STEPS - 1)
     results = pl.pallas_call(
         outer_kernel,

time: 57.3 us -> 58 us (1.012)
  waiting for transfers between devices: 1.77 us -> 3.53 us
  Pallas kernels: 17.3 us -> 18.4 us
  starting transfers between devices: 11.4 us -> 10.4 us
  other arithmetic: 0.83 us -> 0 us
    ppermute x1, waiting for transfers between devices: 0.01 us -> 2.03 us  [per_device(): g2 = lax.ppermute(x2, 'gx', pairing(nx, True, True))]
    ppermute x1, starting transfers between devices: 5.24 us -> 3.98 us  [per_device(): c1 = lax.ppermute(k1, 'gy', pairing(ny, False, False))]
    mul x2 -> x0, other arithmetic: 0.8 us -> none  [per_device(): kron = jnp.kron(jnp.eye(8, dtype=F32), coupling * (COUPLE * SCALE))]
    pallas_call x1, Pallas kernels: 9.6 us -> 10.3 us  [per_device(): pl.pallas_call(outer_kernel, in_specs=[VMEM] * (6 + len(carried)), out_sp...]
  transfers between devices with their start and end apart: 6 -> 6, of which waited for: 1 -> 2; matrix products, arithmetic and copies ran while one was open for 2% -> 0% of each run, Pallas kernels for 7% -> 7%
where the time goes in v4:
time: 58 us; the launch traced here: 57.2 us
  blocking collectives  24.1 us (42%)
  Pallas kernels  18.4 us (32%)
  starting transfers between devices  10.4 us (18%)
  waiting for transfers between devices  3.53 us (6%)
  between operations  0.85 us (1%)
    all_to_all x1, blocking collectives, per_device(): rows = lax.all_to_all(results[-1], ('gx', 'gy'), 0, 0, tiled=True)  24.1 us
    pallas_call x1, Pallas kernels, per_device(): pl.pallas_call(outer_kernel, in_specs=[VMEM] * (6 + len(carried)), out_sp...  10.3 us
    pallas_call x1, Pallas kernels, per_device(): pl.pallas_call(inner_kernel, in_specs=[VMEM] * 6, out_specs=[VMEM] * (len...  4.19 us
    ppermute x1, starting transfers between devices, per_device(): c1 = lax.ppermute(k1, 'gy', pairing(ny, False, False))  3.98 us
    ppermute x1, starting transfers between devices, per_device(): g2 = lax.ppermute(x2, 'gx', pairing(nx, True, True))  3.12 us
    pallas_call x1, Pallas kernels, per_device(): pl.pallas_call(final_kernel, in_specs=[VMEM] * (NUM + 1), out_specs=[HBM,...  2.15 us
    ppermute x1, waiting for transfers between devices, per_device(): g2 = lax.ppermute(x2, 'gx', pairing(nx, True, True))  2.03 us
    ppermute x1, starting transfers between devices, per_device(): r1 = lax.ppermute(s1, 'gy', pairing(ny, False, False))  1.68 us
  transfers between devices with their start and end apart: 6, of which 2 were waited for; matrix products, arithmetic and copies ran while one was open for 0% of the time, Pallas kernels for 7%

profile of v4, /device:TPU:0, one launch (start us, length us, event | category | flops | bytes accessed | tf_op | source)
XLA Modules:
  0.0 57.2 jit_solution(16469909371521148636)
XLA Ops:
  0.6 1.7 %pack.1 = (f32[34,16,256]{2,1,0:T(8,128)S(1)}, f32[34,16,256]{2,1,0:T(8,128)S(1)}, f32[2,72,128]{2,1,0:T(8,128)S(1)}, f32[2,72,128]{2,1,0:T(8,128)S(1)}, f32[16,16]{1,0:T(8,128)S(1)}, /*index=5*/f32[64,128]{1,0:T(8,128)S(1)}) custom-call(f32[16,32,256]{2,1,0:T(8,128)} %f_hbm.1, f32[16,32,256]{2,1,0:T(8,128)} %d_hbm.1, f32[32,256]{1,0:T(8,128)} %wl_hbm.1, ...), custom_call_target="tpu_custom_call" | custom-call | tf_op jit(solution)/shard_map/pack/pallas_call | solution.py:434
  2.3 1.7 %collective-permute-start = (f32[34,16,256]{2,1,0:T(8,128)S(1)}, f32[34,16,256]{2,1,0:T(8,128)S(1)}, u32[]{:S(2)}, u32[]{:S(2)}) collective-permute-start(f32[34,16,256]{2,1,0:T(8,128)S(1)} %get-tuple-element.30.s1_ref), channel_id=1, source_target_pairs={{0,1},{1,0},{2,3},{3,2},{4,5},{5,4},{6,7},{7,6},{8,9},{9,8},{10,11... | collective-permute-start | bytes 1671176 | tf_op jit(solution)/shard_map/ppermute | solution.py:451
  4.0 0.7 %collective-permute-start.1 = (f32[34,16,256]{2,1,0:T(8,128)S(1)}, f32[34,16,256]{2,1,0:T(8,128)S(1)}, u32[]{:S(2)}, u32[]{:S(2)}) collective-permute-start(f32[34,16,256]{2,1,0:T(8,128)S(1)} %get-tuple-element.31.s2_ref), channel_id=1, source_target_pairs={{1,2},{2,1},{3,4},{4,3},{5,6},{6,5},{7,8},{8,7},{9,10},{10,9},{11,... | collective-permute-start | bytes 1671176 | tf_op jit(solution)/shard_map/ppermute | solution.py:452
  4.7 0.1 collective-permute-start.2
  4.8 3.1 %collective-permute-start.3 = (f32[2,72,128]{2,1,0:T(8,128)S(1)}, f32[2,72,128]{2,1,0:T(8,128)S(1)}, u32[]{:S(2)}, u32[]{:S(2)}) collective-permute-start(f32[2,72,128]{2,1,0:T(8,128)S(1)} %get-tuple-element.33), channel_id=1, source_target_pairs={{0,112},{16,32},{32,16},{48,64},{64,48},{80,96},{96,80},{112,0},{1... | collective-permute-start | bytes 221192 | tf_op jit(solution)/shard_map/ppermute | solution.py:454
  7.9 0.0 collective-permute-done.2.g1_ref
  7.9 2.0 %collective-permute-done.3.g2_ref = f32[2,72,128]{2,1,0:T(8,128)S(1)} collective-permute-done((f32[2,72,128]{2,1,0:T(8,128)S(1)}, f32[2,72,128]{2,1,0:T(8,128)S(1)}, u32[]{:S(2)}, u32[]{:S(2)}) %collective-permute-start.3) | collective-permute-done | bytes 73760 | tf_op jit(solution)/shard_map/ppermute | solution.py:454
  9.9 4.2 %inner.1 = (f32[64,16,384]{2,1,0:T(8,128)S(1)}, f32[64,16,384]{2,1,0:T(8,128)S(1)}, f32[64,16,384]{2,1,0:T(8,128)S(1)}, f32[64,16,384]{2,1,0:T(8,128)S(1)}, f32[...) custom-call(f32[34,16,256]{2,1,0:T(8,128)S(1)} %get-tuple-element.30, ...), custom_call_target="tpu_custom_call" | custom-call | flops 100000000 | bytes 1048576 | tf_op jit(solution)/shard_map/inner/pallas_call | solution.py:458
  14.1 4.0 %collective-permute-start.4 = (f32[2,72,128]{2,1,0:T(8,128)S(1)}, f32[2,72,128]{2,1,0:T(8,128)S(1)}, u32[]{:S(2)}, u32[]{:S(2)}) collective-permute-start(f32[2,72,128]{2,1,0:T(8,128)S(1)} %get-tuple-element.36), channel_id=1, source_target_pairs={{0,1},{1,0},{2,3},{3,2},{4,5},{5,4},{6,7},{7,6},{8,9},{9,8},{10,11... | collective-permute-start | bytes 221192 | tf_op jit(solution)/shard_map/ppermute | solution.py:468
  18.1 0.8 %collective-permute-start.5 = (f32[2,72,128]{2,1,0:T(8,128)S(1)}, f32[2,72,128]{2,1,0:T(8,128)S(1)}, u32[]{:S(2)}, u32[]{:S(2)}) collective-permute-start(f32[2,72,128]{2,1,0:T(8,128)S(1)} %get-tuple-element.37), channel_id=1, source_target_pairs={{1,2},{2,1},{3,4},{4,3},{5,6},{6,5},{7,8},{8,7},{9,10},{10,9},{11,... | collective-permute-start | bytes 221192 | tf_op jit(solution)/shard_map/ppermute | solution.py:469
  19.0 1.5 %collective-permute-done.4.c1_ref = f32[2,72,128]{2,1,0:T(8,128)S(1)} collective-permute-done((f32[2,72,128]{2,1,0:T(8,128)S(1)}, f32[2,72,128]{2,1,0:T(8,128)S(1)}, u32[]{:S(2)}, u32[]{:S(2)}) %collective-permute-start.4) | collective-permute-done | bytes 73760 | tf_op jit(solution)/shard_map/ppermute | solution.py:468
  20.4 0.0 collective-permute-done.5.c2_ref
  20.4 0.0 collective-permute-done.r1_ref
  20.5 0.0 collective-permute-done.1.r2_ref
  20.5 10.3 %outer.1 = (f32[64,16,384]{2,1,0:T(8,128)S(1)}, f32[64,16,384]{2,1,0:T(8,128)S(1)}, f32[64,16,384]{2,1,0:T(8,128)S(1)}, f32[64,16,384]{2,1,0:T(8,128)S(1)}, f32[...) custom-call(f32[34,16,256]{2,1,0:T(8,128)S(1)} %collective-permute-d, ...), custom_call_target="tpu_custom_call", output_to_operand_aliasing={{0}: (6, {}), {1}: (7, {}), {2}: (8, {}), {3}: (9, {}), {4}... | custom-call | tf_op jit(solution)/shard_map/outer/pallas_call | solution.py:471
  30.8 24.1 %all_to_all.11 = f32[128,1,128]{2,1,0:T(1,128)S(1)} all-to-all(f32[128,1,128]{2,1,0:T(1,128)S(1)} %bitcast.5), channel_id=1, replica_groups=mesh['gx'=8,'gy'=16] {'gx','gy'}, dimensions={0} | all-to-all | bytes 131072 | tf_op jit(solution)/shard_map/all_to_all | solution.py:482
  54.9 2.2 %finish.1 = (f32[16,32,256]{2,1,0:T(8,128)}, f32[16,32,256]{2,1,0:T(8,128)}) custom-call(f32[64,16,384]{2,1,0:T(8,128)S(1)} %get-tuple-element.48.refs_0_, f32[64,16,384]{2,1,0:T(8,128)S(1)} %get-tuple-element.49.refs_1_, f32[64,16,384]{2,1,0:T(8,128)S(1)} %get-tuple-element.50.refs_2_, f32[64,16,384]{2,1,0:T(8,128)S(1)} %get-tuple-element.51.refs_3_, ...), custom_call_target="tpu_custom_call" | custom-call | tf_op jit(solution)/shard_map/finish/pallas_call | solution.py:483
Async XLA Ops:
  2.3 18.1 %collective-permute-start = (f32[34,16,256]{2,1,0:T(8,128)S(1)}, f32[34,16,256]{2,1,0:T(8,128)S(1)}, u32[]{:S(2)}, u32[]{:S(2)}) collective-permute-start(f32[34,16,256]{2,1,0:T(8,128)S(1)} %get-tuple-element.30.s1_ref), channel_id=1, source_target_pairs={{0,1},{1,0},{2,3},{3,2},{4,5},{5,4},{6,7},{7,6},{8,9},{9,8},{10,11... | collective-permute-start | bytes 1671176 | tf_op jit(solution)/shard_map/ppermute | solution.py:451
  4.0 16.5 %collective-permute-start.1 = (f32[34,16,256]{2,1,0:T(8,128)S(1)}, f32[34,16,256]{2,1,0:T(8,128)S(1)}, u32[]{:S(2)}, u32[]{:S(2)}) collective-permute-start(f32[34,16,256]{2,1,0:T(8,128)S(1)} %get-tuple-element.31.s2_ref), channel_id=1, source_target_pairs={{1,2},{2,1},{3,4},{4,3},{5,6},{6,5},{7,8},{8,7},{9,10},{10,9},{11,... | collective-permute-start | bytes 1671176 | tf_op jit(solution)/shard_map/ppermute | solution.py:452
  4.7 3.2 %collective-permute-start.2 = (f32[2,72,128]{2,1,0:T(8,128)S(1)}, f32[2,72,128]{2,1,0:T(8,128)S(1)}, u32[]{:S(2)}, u32[]{:S(2)}) collective-permute-start(f32[2,72,128]{2,1,0:T(8,128)S(1)} %get-tuple-element.32), channel_id=1, source_target_pairs={{0,16},{16,0},{32,48},{48,32},{64,80},{80,64},{96,112},{112,96},{1... | collective-permute-start | bytes 221192 | tf_op jit(solution)/shard_map/ppermute | solution.py:453
  4.8 5.2 %collective-permute-start.3 = (f32[2,72,128]{2,1,0:T(8,128)S(1)}, f32[2,72,128]{2,1,0:T(8,128)S(1)}, u32[]{:S(2)}, u32[]{:S(2)}) collective-permute-start(f32[2,72,128]{2,1,0:T(8,128)S(1)} %get-tuple-element.33), channel_id=1, source_target_pairs={{0,112},{16,32},{32,16},{48,64},{64,48},{80,96},{96,80},{112,0},{1... | collective-permute-start | bytes 221192 | tf_op jit(solution)/shard_map/ppermute | solution.py:454
  14.1 6.3 %collective-permute-start.4 = (f32[2,72,128]{2,1,0:T(8,128)S(1)}, f32[2,72,128]{2,1,0:T(8,128)S(1)}, u32[]{:S(2)}, u32[]{:S(2)}) collective-permute-start(f32[2,72,128]{2,1,0:T(8,128)S(1)} %get-tuple-element.36), channel_id=1, source_target_pairs={{0,1},{1,0},{2,3},{3,2},{4,5},{5,4},{6,7},{7,6},{8,9},{9,8},{10,11... | collective-permute-start | bytes 221192 | tf_op jit(solution)/shard_map/ppermute | solution.py:468
  18.1 2.3 %collective-permute-start.5 = (f32[2,72,128]{2,1,0:T(8,128)S(1)}, f32[2,72,128]{2,1,0:T(8,128)S(1)}, u32[]{:S(2)}, u32[]{:S(2)}) collective-permute-start(f32[2,72,128]{2,1,0:T(8,128)S(1)} %get-tuple-element.37), channel_id=1, source_target_pairs={{1,2},{2,1},{3,4},{4,3},{5,6},{6,5},{7,8},{8,7},{9,10},{10,9},{11,... | collective-permute-start | bytes 221192 | tf_op jit(solution)/shard_map/ppermute | solution.py:469

commit v5 on v4

--- a/solution.py
+++ b/solution.py
@@ -16,7 +16,6 @@
 COLS = 256
 RIM = 2 * ITERS
 EXT_ROWS = ROWS + 2 * RIM
-EXT_COLS = COLS + 128
 COUPLE = 0.25
 DIFF_LAT = 0.5
 DIFF_LON = 0.5
@@ -102,67 +101,110 @@
         x2_ref[half, 64:72, :] = winds[1]
 
 
-LANE_SHAPE = (8, 128)
-
-
-def place_half(src_ref, one, two, row, half, p0_ref, d_ref, coef_ref, k_ref):
+HALF = EXT_ROWS // 2
+GHOST = 2
+WIDE = 2 * COLS + 128
+TILES = [slice(128 * t, 128 * t + 128) for t in range(5)]
+
+
+def place_pairs(low, high, low_sides, high_sides, low_half, base, p0_ref, d_ref, coef_refs, k_ref):
     par_x = lax.rem(lax.axis_index("gx"), 2)
-    lane = lax.broadcasted_iota(jnp.int32, LANE_SHAPE, 1)
-    row = pl.multiple_of(row, 16)
-
-    def spread(east, west, g):
-        e = pltpu.roll(east, (128 - 16 * g) % 128, 1) if g else east
-        shift = (112 - 16 * g) % 128
-        w = pltpu.roll(west, shift, 1) if shift else west
-        return jnp.where(lane < 16, e, jnp.where(lane >= 112, w, 0.0))
-
-    def sides(slot):
-        a = one(slice(8 * slot, 8 * slot + 8))
-        b = two(slice(8 * slot, 8 * slot + 8))
+    lane = lax.broadcasted_iota(jnp.int32, (8, 128), 1)
+    turned = jnp.logical_and(lane >= 48, lane < 80)
+    coef_low, coef_high, coef_edge = coef_refs
+
+    def turn(x, by):
+        return pltpu.roll(x, by % 128, 1) if by % 128 else x
+
+    def sides(reader, slot):
+        a, b = reader(slot)
         return jnp.where(par_x == 0, a, b), jnp.where(par_x == 0, b, a)
 
-    east, west = sides(8)
-    scales = []
-    for q in range(2):
-        rows = pl.ds(pl.multiple_of(row + 8 * q, 8), 8)
-        k = k_ref[rows]
-        live = jnp.where(k > 0.0, 1.0, 0.0)
-        kx = k * SCALE
-        half_lat = live * (SCALE * DIFF_LAT)
-        fixed = live * (SCALE * (1.0 + 2.0 * DIFF_LAT - CENTRE)) + 2.0 * kx
-        for t in range(3):
-            lanes = slice(128 * t, 128 * t + 128)
-            winds = []
-            for field in range(2):
-                if t < 2:
-                    wind = src_ref[32 + field, 8 * q : 8 * q + 8, lanes]
-                else:
-                    low = spread(east, west, 4 * field + q)
-                    high = spread(east, west, 4 * field + 2 + q)
-                    wind = jnp.where(half == 0, low, high)
-                winds.append(wind * (live * (SCALE / 12.0)))
-            lon, lat = winds
-            coef_ref[0, rows, lanes] = 8.0 * lon - kx
-            coef_ref[1, rows, lanes] = -8.0 * lon - kx
-            coef_ref[2, rows, lanes] = -lon
-            coef_ref[3, rows, lanes] = 8.0 * lat - half_lat
-            coef_ref[4, rows, lanes] = -8.0 * lat - half_lat
-            coef_ref[5, rows, lanes] = -lat
-        scales.append((live * SCALE, fixed))
-    for q in range(2):
-        for c in range(2):
-            subs = slice(8 * c, 8 * c + 8)
-            fe, fw = sides(2 * q + c)
-            de, dw = sides(4 + 2 * q + c)
-            for g in range(8):
-                r = 8 * q + g
-                p0_ref[row + r, subs, :COLS] = src_ref[r, subs]
-                p0_ref[row + r, subs, COLS:] = spread(fe, fw, g)
-                mul, add = (x[g : g + 1] for x in scales[q])
-                for t in range(2):
-                    lanes = slice(128 * t, 128 * t + 128)
-                    d_ref[row + r, subs, lanes] = src_ref[16 + r, subs, lanes] * mul + add
-                d_ref[row + r, subs, COLS:] = spread(de, dw, g) * mul + add
+    def spread(low_pair, low_group, high_pair, high_group):
+        out = jnp.where(lane < 16, turn(low_pair[0], -16 * low_group), 0.0)
+        out = jnp.where(lane >= 112, turn(low_pair[1], 112 - 16 * low_group), out)
+        upper = jnp.where(lane >= 64, turn(high_pair[0], 64 - 16 * high_group), turn(high_pair[1], 48 - 16 * high_group))
+        return jnp.where(turned, upper, out)
+
+    scales = {}
+    edges = {}
+    wind_sides = (sides(low_sides, 8), sides(high_sides, 8))
+    for side, (reader, half, sign, first) in enumerate(
+        ((low, low_half, 1.0, base), (high, 1 - low_half, -1.0, EXT_ROWS - base - 16))
+    ):
+        for q in range(2):
+            k = k_ref[first + 8 * q : first + 8 * q + 8]
+            live = jnp.where(k > 0.0, 1.0, 0.0)
+            kx = k * SCALE
+            half_lat = live * (SCALE * DIFF_LAT)
+            scales[side, q] = (live * SCALE, live * (SCALE * (1.0 + 2.0 * DIFF_LAT - CENTRE)) + 2.0 * kx)
+            for t in range(3):
+                winds = []
+                for field in range(2):
+                    if t < 2:
+                        wind = reader(32 + field, slice(8 * q, 8 * q + 8), TILES[t])
+                        if side:
+                            wind = turn(wind, 64)
+                    else:
+                        group = 4 * field + 2 * half + q
+                        east, west = wind_sides[side]
+                        if side:
+                            wind = jnp.where(lane >= 64, turn(east, 64 - 16 * group), turn(west, 48 - 16 * group))
+                        else:
+                            wind = jnp.where(lane < 64, turn(east, -16 * group), turn(west, 112 - 16 * group))
+                    winds.append(wind * (live * (SCALE / 12.0)))
+                lon, lat = winds[0], winds[1] * sign
+                values = (
+                    8.0 * lon - kx, -8.0 * lon - kx, -lon,
+                    8.0 * lat - half_lat, -8.0 * lat - half_lat, -lat,
+                )
+                for n, value in enumerate(values):
+                    if t == 2:
+                        edges[side, q, n] = value
+                    elif side:
+                        row = first - HALF + 8 * q
+                        coef_high[n, row : row + 8, TILES[t]] = value
+                    else:
+                        coef_low[n, first + 8 * q : first + 8 * q + 8, TILES[t]] = value
+    inside = jnp.logical_or(lane < 16, lane >= 112)[:1]
+    turned_row = turned[:1]
+    for i in range(16):
+        u = base + i
+        j = 15 - i
+        for n in range(6):
+            a = edges[0, i // 8, n][i % 8 : i % 8 + 1]
+            b = edges[1, j // 8, n][j % 8 : j % 8 + 1]
+            coef_edge[n, u : u + 1, :] = jnp.where(turned_row, b, jnp.where(inside, a, 0.0))
+    for c in range(2):
+        subs = slice(8 * c, 8 * c + 8)
+        pairs = {}
+        for kind in range(2):
+            for q in range(2):
+                pairs[kind, 0, q] = sides(low_sides, 4 * kind + 2 * q + c)
+                pairs[kind, 1, q] = sides(high_sides, 4 * kind + 2 * q + c)
+        for i in range(16):
+            u = base + i
+            j = 15 - i
+            mul_l, add_l = (x[i % 8 : i % 8 + 1] for x in scales[0, i // 8])
+            mul_h, add_h = (x[j % 8 : j % 8 + 1] for x in scales[1, j // 8])
+            for t in range(2):
+                p0_ref[u, subs, TILES[t]] = low(i, subs, TILES[t])
+                p0_ref[u, subs, TILES[2 + t]] = turn(high(j, subs, TILES[t]), 64)
+                d_ref[u, subs, TILES[t]] = low(16 + i, subs, TILES[t]) * mul_l + add_l
+                d_ref[u, subs, TILES[2 + t]] = turn(high(16 + j, subs, TILES[t]), 64) * mul_h + add_h
+            f_edge, d_edge = (
+                spread(pairs[kind, 0, i // 8], i % 8, pairs[kind, 1, j // 8], j % 8) for kind in range(2)
+            )
+            p0_ref[u, subs, TILES[4]] = f_edge
+            mul = jnp.where(turned_row, mul_h, mul_l)
+            add = jnp.where(turned_row, add_h, add_l)
+            d_ref[u, subs, TILES[4]] = d_edge * mul + add
+
+
+def mirror(p_ref):
+    for g in range(GHOST):
+        for dst, src in zip((0, 1, 2, 3, 4), (2, 3, 0, 1, 4)):
+            p_ref[HALF + g, :, TILES[dst]] = pltpu.roll(p_ref[HALF - 1 - g, :, TILES[src]], 64, 1)
 
 
 def split_kron(kron_ref):
@@ -171,69 +213,107 @@
     return hi, (kron - hi.astype(F32)).astype(jnp.bfloat16)
 
 
-def run_blocks(blocks, p_refs, d_ref, coef_ref, kron, mix_refs):
-    kron_hi, kron_lo = kron
+def run_blocks(blocks, p_refs, d_ref, coef_refs, kron, mix_refs):
+    lane = lax.broadcasted_iota(jnp.int32, (CH, 128), 1)
+    coef_low, coef_high, coef_edge = coef_refs
+
+    def width(step):
+        return WIDE if step < ITERS else 2 * COLS
 
     def mix(index):
-        step, r0 = blocks[index]
-        flat = p_refs[step - 1][r0 : r0 + 8].reshape(8 * CH, EXT_COLS)
+        step, u0, count = blocks[index]
+        size = count * CH
+        kron_hi, kron_lo = (k[:size, :size] for k in kron)
+        flat = p_refs[step - 1][u0 : u0 + count, :, : width(step)].reshape(size, width(step))
         hi = flat.astype(jnp.bfloat16)
         lo = (flat - hi.astype(F32)).astype(jnp.bfloat16)
         mixed = jnp.dot(kron_hi, hi, preferred_element_type=F32)
         mixed = mixed + jnp.dot(kron_hi, lo, preferred_element_type=F32)
         mixed = mixed + jnp.dot(kron_lo, hi, preferred_element_type=F32)
-        mix_refs[index % 2][...] = mixed.reshape(8, CH, EXT_COLS)
+        mix_refs[index % 2][:count, :, : width(step)] = mixed.reshape(count, CH, width(step))
+
+    def shifted(tiles, by):
+        rolled = [pltpu.roll(x, by % 128, 1) for x in tiles]
+        if by < 0:
+            low, high = lane >= 128 + by, jnp.logical_and(lane >= 64 + by, lane < 64)
+            nexts = (1, 4, 3, 4)
+        else:
+            low, high = lane < by, jnp.logical_and(lane >= 64, lane < 64 + by)
+            nexts = (4, 0, 4, 2)
+        ends = (0, 2) if by < 0 else (1, 3)
+        out = [jnp.where(low if t < 2 else high, rolled[nexts[t]], rolled[t]) for t in range(4)]
+        out.append(jnp.where(low, rolled[ends[0]], jnp.where(high, rolled[ends[1]], rolled[4])))
+        return out
 
     mix(0)
-    for index, (step, r0) in enumerate(blocks):
+    for index, (step, u0, count) in enumerate(blocks):
         more = index + 1 < len(blocks)
-        late = more and blocks[index + 1][0] == step + 1 and abs(blocks[index + 1][1] - r0) < 8
+        late = False
+        if more:
+            step_n, u_n, count_n = blocks[index + 1]
+            late = step_n == step + 1 and u_n < u0 + count and u0 < u_n + count_n
         if more and not late:
             mix(index + 1)
         src, dst = p_refs[step - 1], p_refs[step]
-        for s in (slice(0, 8), slice(8, 16)):
-            for i in range(8):
-                r = r0 + i
-                c = src[r, s]
-                acc = mix_refs[index % 2][i, s] + d_ref[r, s] * c
+        for i in range(count):
+            u = u0 + i
+            centre = [src[u, :, t] for t in TILES]
+            east, west = shifted(centre, -1), shifted(centre, 1)
+            east2, west2 = shifted(centre, -2), shifted(centre, 2)
+            for t in range(width(step) // 128):
+                at = TILES[t]
+                if t < 2:
+                    coef = [coef_low[n, u : u + 1, at] for n in range(6)]
+                elif t < 4:
+                    v = HALF - 1 - u
+                    coef = [coef_high[n, v : v + 1, TILES[t - 2]] for n in range(6)]
+                else:
+                    coef = [coef_edge[n, u : u + 1, :] for n in range(6)]
+                acc = mix_refs[index % 2][i, :, at] + d_ref[u, :, at] * centre[t]
                 if step > 1:
-                    acc = acc - p_refs[step - 2][r, s]
-                coef = [coef_ref[k, r : r + 1] for k in range(6)]
-                acc = acc + coef[0] * pltpu.roll(c, EXT_COLS - 1, 1)
-                acc = acc + coef[1] * pltpu.roll(c, 1, 1)
-                acc = acc + coef[2] * (pltpu.roll(c, EXT_COLS - 2, 1) - pltpu.roll(c, 2, 1))
-                acc = acc + coef[3] * src[r + 1, s]
-                acc = acc + coef[4] * src[r - 1, s]
-                acc = acc + coef[5] * (src[r + 2, s] - src[r - 2, s])
-                dst[r, s] = acc
+                    acc = acc - p_refs[step - 2][u, :, at]
+                acc = acc + coef[0] * east[t]
+                acc = acc + coef[1] * west[t]
+                acc = acc + coef[2] * (east2[t] - west2[t])
+                acc = acc + coef[3] * src[u + 1, :, at]
+                acc = acc + coef[4] * src[u - 1, :, at]
+                acc = acc + coef[5] * (src[u + 2, :, at] - src[u - 2, :, at])
+                dst[u, :, at] = acc
+        if u0 + count == HALF and step < ITERS:
+            mirror(dst)
         if late:
             mix(index + 1)
 
 
-def cover(low, high):
-    return [min(r, high - 8) for r in range(low, high, 8)]
-
-
 INNER_STEPS = 6
-INNER = [(j, r) for j in range(1, INNER_STEPS + 1) for r in cover(RIM + 2 * j, RIM + ROWS - 2 * j)]
-OUTER = [
-    (j, r)
-    for j in range(1, NUM)
-    for r in (
-        cover(2 * j, RIM + 2 * j) + cover(RIM + ROWS - 2 * j, EXT_ROWS - 2 * j)
-        if j <= INNER_STEPS
-        else cover(2 * j, EXT_ROWS - 2 * j)
-    )
-]
-
-
-def inner_kernel(s1_ref, s2_ref, g1_ref, g2_ref, cp_ref, k_ref, *refs):
-    p_refs = refs[: INNER_STEPS + 1]
-    d_ref, coef_ref, k1_ref, k2_ref, kron_ref, *mix_refs = refs[INNER_STEPS + 1 :]
+INNER = []
+OUTER = []
+for _j in range(1, NUM):
+    _edge = RIM + 2 * _j
+    if _j <= INNER_STEPS:
+        _rest = HALF - _edge
+        if _rest > 8:
+            INNER.append((_j, _edge + 8, _rest - 8))
+        INNER.append((_j, _edge, min(_rest, 8)))
+        OUTER += [(_j, 2 * _j + 8, 8), (_j, 2 * _j, 8)]
+    elif _j < ITERS:
+        OUTER += [(_j, 26, 6), (_j, 20, 6), (_j, 14, 6)]
+    else:
+        OUTER += [(_j, 24, 8), (_j, 16, 8)]
+
+
+def corner_kernel(g1_ref, g2_ref, k1_ref, k2_ref):
     par_y = lax.rem(lax.axis_index("gy"), 2)
     for n, g_ref in enumerate((g1_ref, g2_ref)):
         k1_ref[n] = g_ref[1 - par_y]
         k2_ref[n] = g_ref[par_y]
+
+
+def inner_kernel(s1_ref, s2_ref, g1_ref, g2_ref, cp_ref, k_ref, *refs):
+    p_refs = refs[: INNER_STEPS + 1]
+    d_ref, *coef_refs = refs[INNER_STEPS + 1 : INNER_STEPS + 5]
+    kron_ref, *mix_refs = refs[INNER_STEPS + 5 :]
+    par_y = lax.rem(lax.axis_index("gy"), 2)
     size = 8 * CH
     pick = lax.broadcasted_iota(jnp.int32, (size, CH), 0) % CH
     pick = (pick == lax.broadcasted_iota(jnp.int32, (size, CH), 1)).astype(F32)
@@ -246,30 +326,39 @@
     row = lax.broadcasted_iota(jnp.int32, (size, size), 0) // CH
     col = lax.broadcasted_iota(jnp.int32, (size, size), 1) // CH
     kron_ref[...] = jnp.where(row == col, full, 0.0)
-    for src_ref, half in ((s1_ref, 1 - par_y), (s2_ref, par_y)):
-        place_half(
-            src_ref, lambda sl, h=half: g1_ref[h, sl], lambda sl, h=half: g2_ref[h, sl],
-            RIM + 16 * half, half, p_refs[0], d_ref, coef_ref, k_ref,
-        )
-    run_blocks(INNER, p_refs, d_ref, coef_ref, split_kron(kron_ref), mix_refs)
+    place_pairs(
+        lambda *at: jnp.where(par_y == 0, s2_ref[at], s1_ref[at]),
+        lambda *at: jnp.where(par_y == 0, s1_ref[at], s2_ref[at]),
+        lambda slot: (g1_ref[0, 8 * slot : 8 * slot + 8], g2_ref[0, 8 * slot : 8 * slot + 8]),
+        lambda slot: (g1_ref[1, 8 * slot : 8 * slot + 8], g2_ref[1, 8 * slot : 8 * slot + 8]),
+        0, RIM, p_refs[0], d_ref, coef_refs, k_ref,
+    )
+    mirror(p_refs[0])
+    run_blocks(INNER, p_refs, d_ref, coef_refs, split_kron(kron_ref), mix_refs)
 
 
 def outer_kernel(r1_ref, r2_ref, c1_ref, c2_ref, k_ref, kron_ref, *refs):
-    refs = refs[INNER_STEPS + 3 :]
-    p_refs = refs[: INNER_STEPS + 1] + refs[INNER_STEPS + 3 : NUM + 2]
-    d_ref, coef_ref = refs[INNER_STEPS + 1 : INNER_STEPS + 3]
-    gram_ref, mix_a, mix_b, sums_ref = refs[NUM + 2 :]
+    count = INNER_STEPS + 5
+    refs = refs[count:]
+    p_refs = refs[: INNER_STEPS + 1] + refs[count : count + NUM - INNER_STEPS - 1]
+    d_ref, coef_refs = refs[INNER_STEPS + 1], refs[INNER_STEPS + 2 : count]
+    gram_ref, mix_a, mix_b, sums_ref = refs[count + NUM - INNER_STEPS - 1 :]
     par_y = lax.rem(lax.axis_index("gy"), 2)
-    kron = split_kron(kron_ref)
-    for src_ref, c_ref, row, half in (
-        (r1_ref, c1_ref, 48 - 48 * par_y, par_y),
-        (r2_ref, c2_ref, 48 * par_y, 1 - par_y),
-    ):
-        place_half(
-            src_ref, lambda sl, c=c_ref: c[0, sl], lambda sl, c=c_ref: c[1, sl],
-            row, half, p_refs[0], d_ref, coef_ref, k_ref,
-        )
-    run_blocks(OUTER, p_refs, d_ref, coef_ref, kron, (mix_a, mix_b))
+
+    def corners(one, two):
+        def read(slot):
+            at = slice(8 * slot, 8 * slot + 8)
+            return tuple(jnp.where(par_y == 0, one[n, at], two[n, at]) for n in range(2))
+
+        return read
+
+    place_pairs(
+        lambda *at: jnp.where(par_y == 0, r2_ref[at], r1_ref[at]),
+        lambda *at: jnp.where(par_y == 0, r1_ref[at], r2_ref[at]),
+        corners(c2_ref, c1_ref), corners(c1_ref, c2_ref),
+        1, 0, p_refs[0], d_ref, coef_refs, k_ref,
+    )
+    run_blocks(OUTER, p_refs, d_ref, coef_refs, split_kron(kron_ref), (mix_a, mix_b))
 
     sums_ref[...] = jnp.zeros_like(sums_ref)
     for lo_k, hi_k in ((0, 6), (6, NUM)):
@@ -277,15 +366,11 @@
 
         def body(r, accs, pairs=pairs, hi_k=hi_k):
             accs = list(accs)
-            for u in range(2):
-                for c in range(2):
-                    for t in range(2):
-                        vecs = [
-                            p_refs[k][RIM + 2 * r + u, 8 * c : 8 * c + 8, 128 * t : 128 * t + 128]
-                            for k in range(hi_k)
-                        ]
-                        for n, (_, i, j) in enumerate(pairs):
-                            accs[n] = accs[n] + vecs[i] * vecs[j]
+            for c in range(2):
+                for t in range(4):
+                    vecs = [p_refs[k][RIM + r, 8 * c : 8 * c + 8, TILES[t]] for k in range(hi_k)]
+                    for n, (_, i, j) in enumerate(pairs):
+                        accs[n] = accs[n] + vecs[i] * vecs[j]
             return tuple(accs)
 
         accs = lax.fori_loop(0, ROWS // 2, body, tuple(jnp.zeros((8, 128), F32) for _ in pairs))
@@ -383,17 +468,22 @@
         rows = slice(8 * b, 8 * b + 8)
         for c in range(2):
             for t in range(2):
+                upper = b >= 2
+                first = HALF - 1 - 8 * (b - 2) - 7 if upper else RIM + 8 * b
+                tile = TILES[2 + t] if upper else TILES[t]
                 xs = rs = None
                 for k in range(NUM):
-                    vec = p_refs[k][RIM + 8 * b : RIM + 8 * b + 8, 8 * c : 8 * c + 8, 128 * t : 128 * t + 128]
+                    vec = p_refs[k][first : first + 8, 8 * c : 8 * c + 8, tile]
                     part = vec * work_ref[ITERS + k]
                     rs = part if rs is None else rs + part
                     if k < ITERS:
                         part = vec * work_ref[k]
                         xs = part if xs is None else xs + part
                 where = (slice(8 * c, 8 * c + 8), rows, slice(128 * t, 128 * t + 128))
-                xv_ref[where] = jnp.swapaxes(xs, 0, 1)
-                rv_ref[where] = jnp.swapaxes(rs, 0, 1)
+                for ref, value in ((xv_ref, xs), (rv_ref, rs)):
+                    if upper:
+                        value = jnp.stack([pltpu.roll(value[7 - i], 64, 1) for i in range(8)])
+                    ref[where] = jnp.swapaxes(value, 0, 1)
         for n, (src, dst) in enumerate(((xv_ref, x_ref), (rv_ref, r_ref))):
             copy = pltpu.make_async_copy(src.at[:, rows], dst.at[:, rows], sem.at[2 * b + n])
             copy.start()
@@ -452,21 +542,30 @@
     r2 = lax.ppermute(s2, "gy", pairing(ny, True, False))
     g1 = lax.ppermute(x1, "gx", pairing(nx, False, True))
     g2 = lax.ppermute(x2, "gx", pairing(nx, True, True))
-    field = shape(EXT_ROWS, CH, EXT_COLS)
-    mix = [pltpu.VMEM((8, CH, EXT_COLS), F32)] * 2
-    carried = [field] * (INNER_STEPS + 2) + [shape(6, EXT_ROWS, EXT_COLS)]
-    *state, k1, k2, kron = pl.pallas_call(
+    k1, k2 = pl.pallas_call(
+        corner_kernel,
+        in_specs=[VMEM] * 2,
+        out_specs=[VMEM] * 2,
+        out_shape=[shape(2, 72, 128)] * 2,
+        compiler_params=pltpu.CompilerParams(vmem_limit_bytes=2**20),
+        name="corner",
+    )(g1, g2)
+    c1 = lax.ppermute(k1, "gy", pairing(ny, False, False))
+    c2 = lax.ppermute(k2, "gy", pairing(ny, True, False))
+    field = shape(HALF + GHOST, CH, WIDE)
+    mix = [pltpu.VMEM((8, CH, WIDE), F32)] * 2
+    carried = [field] * (INNER_STEPS + 1) + [shape(HALF, CH, WIDE)]
+    carried += [shape(6, HALF, COLS)] * 2 + [shape(6, HALF, 128)]
+    *state, kron = pl.pallas_call(
         inner_kernel,
         in_specs=[VMEM] * 6,
-        out_specs=[VMEM] * (len(carried) + 3),
-        out_shape=carried + [shape(2, 72, 128)] * 2 + [shape(8 * CH, 8 * CH)],
+        out_specs=[VMEM] * (len(carried) + 1),
+        out_shape=carried + [shape(8 * CH, 8 * CH)],
         scratch_shapes=mix,
         compiler_params=pltpu.CompilerParams(vmem_limit_bytes=8 * 2**20),
         cost_estimate=pl.CostEstimate(flops=10**8, bytes_accessed=2**20, transcendentals=0),
         name="inner",
     )(s1, s2, g1, g2, couple, k_rows)
-    c1 = lax.ppermute(k1, "gy", pairing(ny, False, False))
-    c2 = lax.ppermute(k2, "gy", pairing(ny, True, False))
     extra = [field] * (NUM - INNER_STEPS - 1)
     results = pl.pallas_call(
         outer_kernel,

time: 58 us -> 55.9 us (0.964)
  waiting for transfers between devices: 3.53 us -> 2.04 us
    ppermute x1, waiting for transfers between devices: 1.49 us -> 0.01 us  [per_device(): c1 = lax.ppermute(k1, 'gy', pairing(ny, False, False))]
  transfers between devices with their start and end apart: 6 -> 6, of which waited for: 2 -> 1; matrix products, arithmetic and copies ran while one was open for 0% -> 0% of each run, Pallas kernels for 7% -> 8%
where the time goes in v5:
time: 55.9 us; the launch traced here: 55.1 us
  blocking collectives  24 us (43%)
  Pallas kernels  18.2 us (33%)
  starting transfers between devices  10.2 us (18%)
  waiting for transfers between devices  2.04 us (4%)
  between operations  0.72 us (1%)
    all_to_all x1, blocking collectives, per_device(): rows = lax.all_to_all(results[-1], ('gx', 'gy'), 0, 0, tiled=True)  24 us
    pallas_call x1, Pallas kernels, per_device(): pl.pallas_call(outer_kernel, in_specs=[VMEM] * (6 + len(carried)), out_sp...  9.91 us
    pallas_call x1, Pallas kernels, per_device(): pl.pallas_call(inner_kernel, in_specs=[VMEM] * 6, out_specs=[VMEM] * (len...  4.33 us
    ppermute x1, starting transfers between devices, per_device(): c1 = lax.ppermute(k1, 'gy', pairing(ny, False, False))  3.98 us
    ppermute x1, starting transfers between devices, per_device(): g2 = lax.ppermute(x2, 'gx', pairing(nx, True, True))  3.12 us
    pallas_call x1, Pallas kernels, per_device(): pl.pallas_call(final_kernel, in_specs=[VMEM] * (NUM + 1), out_specs=[HBM,...  2.23 us
    ppermute x1, waiting for transfers between devices, per_device(): g2 = lax.ppermute(x2, 'gx', pairing(nx, True, True))  2.03 us
    pallas_call x1, Pallas kernels, per_device(): pl.pallas_call(pack_kernel, in_specs=[HBM] * 6, out_specs=[VMEM] * 6, out...  1.69 us
  transfers between devices with their start and end apart: 6, of which 1 were waited for; matrix products, arithmetic and copies ran while one was open for 0% of the time, Pallas kernels for 8%

profile of v5, /device:TPU:0, one launch (start us, length us, event | category | flops | bytes accessed | tf_op | source)
XLA Modules:
  0.0 55.1 jit_solution(12968838959007182275)
XLA Ops:
  0.6 1.7 %pack.1 = (f32[34,16,256]{2,1,0:T(8,128)S(1)}, f32[34,16,256]{2,1,0:T(8,128)S(1)}, f32[2,72,128]{2,1,0:T(8,128)S(1)}, f32[2,72,128]{2,1,0:T(8,128)S(1)}, f32[16,16]{1,0:T(8,128)S(1)}, /*index=5*/f32[64,128]{1,0:T(8,128)S(1)}) custom-call(f32[16,32,256]{2,1,0:T(8,128)} %f_hbm.1, f32[16,32,256]{2,1,0:T(8,128)} %d_hbm.1, f32[32,256]{1,0:T(8,128)} %wl_hbm.1, ...), custom_call_target="tpu_custom_call" | custom-call | tf_op jit(solution)/shard_map/pack/pallas_call | solution.py:524
  2.3 1.7 %collective-permute-start = (f32[34,16,256]{2,1,0:T(8,128)S(1)}, f32[34,16,256]{2,1,0:T(8,128)S(1)}, u32[]{:S(2)}, u32[]{:S(2)}) collective-permute-start(f32[34,16,256]{2,1,0:T(8,128)S(1)} %get-tuple-element.32.s1_ref), channel_id=1, source_target_pairs={{0,1},{1,0},{2,3},{3,2},{4,5},{5,4},{6,7},{7,6},{8,9},{9,8},{10,11... | collective-permute-start | bytes 1671176 | tf_op jit(solution)/shard_map/ppermute | solution.py:541
  4.0 0.7 %collective-permute-start.1 = (f32[34,16,256]{2,1,0:T(8,128)S(1)}, f32[34,16,256]{2,1,0:T(8,128)S(1)}, u32[]{:S(2)}, u32[]{:S(2)}) collective-permute-start(f32[34,16,256]{2,1,0:T(8,128)S(1)} %get-tuple-element.33.s2_ref), channel_id=1, source_target_pairs={{1,2},{2,1},{3,4},{4,3},{5,6},{6,5},{7,8},{8,7},{9,10},{10,9},{11,... | collective-permute-start | bytes 1671176 | tf_op jit(solution)/shard_map/ppermute | solution.py:542
  4.7 0.1 collective-permute-start.2
  4.8 3.1 %collective-permute-start.3 = (f32[2,72,128]{2,1,0:T(8,128)S(1)}, f32[2,72,128]{2,1,0:T(8,128)S(1)}, u32[]{:S(2)}, u32[]{:S(2)}) collective-permute-start(f32[2,72,128]{2,1,0:T(8,128)S(1)} %get-tuple-element.35), channel_id=1, source_target_pairs={{0,112},{16,32},{32,16},{48,64},{64,48},{80,96},{96,80},{112,0},{1... | collective-permute-start | bytes 221192 | tf_op jit(solution)/shard_map/ppermute | solution.py:544
  7.9 0.0 collective-permute-done.2.g1_ref
  7.9 2.0 %collective-permute-done.3.g2_ref = f32[2,72,128]{2,1,0:T(8,128)S(1)} collective-permute-done((f32[2,72,128]{2,1,0:T(8,128)S(1)}, f32[2,72,128]{2,1,0:T(8,128)S(1)}, u32[]{:S(2)}, u32[]{:S(2)}) %collective-permute-start.3) | collective-permute-done | bytes 73760 | tf_op jit(solution)/shard_map/ppermute | solution.py:544
  10.0 4.0 %collective-permute-start.4 = (f32[2,72,128]{2,1,0:T(8,128)S(1)}, f32[2,72,128]{2,1,0:T(8,128)S(1)}, u32[]{:S(2)}, u32[]{:S(2)}) collective-permute-start(f32[2,72,128]{2,1,0:T(8,128)S(1)} %get-tuple-element.36), channel_id=1, source_target_pairs={{0,1},{1,0},{2,3},{3,2},{4,5},{5,4},{6,7},{7,6},{8,9},{9,8},{10,11... | collective-permute-start | bytes 221192 | tf_op jit(solution)/shard_map/ppermute | solution.py:553
  13.9 0.7 %collective-permute-start.5 = (f32[2,72,128]{2,1,0:T(8,128)S(1)}, f32[2,72,128]{2,1,0:T(8,128)S(1)}, u32[]{:S(2)}, u32[]{:S(2)}) collective-permute-start(f32[2,72,128]{2,1,0:T(8,128)S(1)} %get-tuple-element.37), channel_id=1, source_target_pairs={{1,2},{2,1},{3,4},{4,3},{5,6},{6,5},{7,8},{8,7},{9,10},{10,9},{11,... | collective-permute-start | bytes 221192 | tf_op jit(solution)/shard_map/ppermute | solution.py:554
  14.6 4.3 %inner.1 = (f32[34,16,640]{2,1,0:T(8,128)S(1)}, f32[34,16,640]{2,1,0:T(8,128)S(1)}, f32[34,16,640]{2,1,0:T(8,128)S(1)}, f32[34,16,640]{2,1,0:T(8,128)S(1)}, f32[...) custom-call(f32[34,16,256]{2,1,0:T(8,128)S(1)} %get-tuple-element.32, ...), custom_call_target="tpu_custom_call" | custom-call | flops 100000000 | bytes 1048576 | tf_op jit(solution)/shard_map/inner/pallas_call | solution.py:559
  18.9 0.0 collective-permute-done.4.c1_ref
  18.9 0.0 collective-permute-done.5.c2_ref
  19.0 0.0 collective-permute-done.r1_ref
  19.0 0.0 collective-permute-done.1.r2_ref
  19.0 9.9 %outer.1 = (f32[34,16,640]{2,1,0:T(8,128)S(1)}, f32[34,16,640]{2,1,0:T(8,128)S(1)}, f32[34,16,640]{2,1,0:T(8,128)S(1)}, f32[34,16,640]{2,1,0:T(8,128)S(1)}, f32[...) custom-call(f32[34,16,256]{2,1,0:T(8,128)S(1)} %collective-permute-d, ...), custom_call_target="tpu_custom_call", output_to_operand_aliasing={{0}: (6, {}), {1}: (7, {}), {2}: (8, {}), {3}: (9, {}), {4}... | custom-call | tf_op jit(solution)/shard_map/outer/pallas_call | solution.py:570
  28.9 24.0 %all_to_all.11 = f32[128,1,128]{2,1,0:T(1,128)S(1)} all-to-all(f32[128,1,128]{2,1,0:T(1,128)S(1)} %bitcast.5), channel_id=1, replica_groups=mesh['gx'=8,'gy'=16] {'gx','gy'}, dimensions={0} | all-to-all | bytes 131072 | tf_op jit(solution)/shard_map/all_to_all | solution.py:581
  52.9 2.2 %finish.1 = (f32[16,32,256]{2,1,0:T(8,128)}, f32[16,32,256]{2,1,0:T(8,128)}) custom-call(f32[34,16,640]{2,1,0:T(8,128)S(1)} %get-tuple-element.52.refs_0_, f32[34,16,640]{2,1,0:T(8,128)S(1)} %get-tuple-element.53.refs_1_, f32[34,16,640]{2,1,0:T(8,128)S(1)} %get-tuple-element.54.refs_2_, f32[34,16,640]{2,1,0:T(8,128)S(1)} %get-tuple-element.55.refs_3_, ...), custom_call_target="tpu_custom_call" | custom-call | tf_op jit(solution)/shard_map/finish/pallas_call | solution.py:582
  (1 shorter events, 0.0 us)
Async XLA Ops:
  2.3 16.6 %collective-permute-start = (f32[34,16,256]{2,1,0:T(8,128)S(1)}, f32[34,16,256]{2,1,0:T(8,128)S(1)}, u32[]{:S(2)}, u32[]{:S(2)}) collective-permute-start(f32[34,16,256]{2,1,0:T(8,128)S(1)} %get-tuple-element.32.s1_ref), channel_id=1, source_target_pairs={{0,1},{1,0},{2,3},{3,2},{4,5},{5,4},{6,7},{7,6},{8,9},{9,8},{10,11... | collective-permute-start | bytes 1671176 | tf_op jit(solution)/shard_map/ppermute | solution.py:541
  4.0 15.0 %collective-permute-start.1 = (f32[34,16,256]{2,1,0:T(8,128)S(1)}, f32[34,16,256]{2,1,0:T(8,128)S(1)}, u32[]{:S(2)}, u32[]{:S(2)}) collective-permute-start(f32[34,16,256]{2,1,0:T(8,128)S(1)} %get-tuple-element.33.s2_ref), channel_id=1, source_target_pairs={{1,2},{2,1},{3,4},{4,3},{5,6},{6,5},{7,8},{8,7},{9,10},{10,9},{11,... | collective-permute-start | bytes 1671176 | tf_op jit(solution)/shard_map/ppermute | solution.py:542
  4.7 3.2 %collective-permute-start.2 = (f32[2,72,128]{2,1,0:T(8,128)S(1)}, f32[2,72,128]{2,1,0:T(8,128)S(1)}, u32[]{:S(2)}, u32[]{:S(2)}) collective-permute-start(f32[2,72,128]{2,1,0:T(8,128)S(1)} %get-tuple-element.34), channel_id=1, source_target_pairs={{0,16},{16,0},{32,48},{48,32},{64,80},{80,64},{96,112},{112,96},{1... | collective-permute-start | bytes 221192 | tf_op jit(solution)/shard_map/ppermute | solution.py:543
  4.8 5.2 %collective-permute-start.3 = (f32[2,72,128]{2,1,0:T(8,128)S(1)}, f32[2,72,128]{2,1,0:T(8,128)S(1)}, u32[]{:S(2)}, u32[]{:S(2)}) collective-permute-start(f32[2,72,128]{2,1,0:T(8,128)S(1)} %get-tuple-element.35), channel_id=1, source_target_pairs={{0,112},{16,32},{32,16},{48,64},{64,48},{80,96},{96,80},{112,0},{1... | collective-permute-start | bytes 221192 | tf_op jit(solution)/shard_map/ppermute | solution.py:544
  10.0 9.0 %collective-permute-start.4 = (f32[2,72,128]{2,1,0:T(8,128)S(1)}, f32[2,72,128]{2,1,0:T(8,128)S(1)}, u32[]{:S(2)}, u32[]{:S(2)}) collective-permute-start(f32[2,72,128]{2,1,0:T(8,128)S(1)} %get-tuple-element.36), channel_id=1, source_target_pairs={{0,1},{1,0},{2,3},{3,2},{4,5},{5,4},{6,7},{7,6},{8,9},{9,8},{10,11... | collective-permute-start | bytes 221192 | tf_op jit(solution)/shard_map/ppermute | solution.py:553
  13.9 5.0 %collective-permute-start.5 = (f32[2,72,128]{2,1,0:T(8,128)S(1)}, f32[2,72,128]{2,1,0:T(8,128)S(1)}, u32[]{:S(2)}, u32[]{:S(2)}) collective-permute-start(f32[2,72,128]{2,1,0:T(8,128)S(1)} %get-tuple-element.37), channel_id=1, source_target_pairs={{1,2},{2,1},{3,4},{4,3},{5,6},{6,5},{7,8},{8,7},{9,10},{10,9},{11,... | collective-permute-start | bytes 221192 | tf_op jit(solution)/shard_map/ppermute | solution.py:554

commit v6 on v5

--- a/solution.py
+++ b/solution.py
@@ -107,11 +107,14 @@
 TILES = [slice(128 * t, 128 * t + 128) for t in range(5)]
 
 
-def place_pairs(low, high, low_sides, high_sides, low_half, base, p0_ref, d_ref, coef_refs, k_ref):
+def place_pairs(
+    low, high, low_sides, high_sides, low_half, base, p0_ref, d_ref, coef_refs, k_ref, main=True, edge=True
+):
     par_x = lax.rem(lax.axis_index("gx"), 2)
     lane = lax.broadcasted_iota(jnp.int32, (8, 128), 1)
     turned = jnp.logical_and(lane >= 48, lane < 80)
     coef_low, coef_high, coef_edge = coef_refs
+    spans = [t for t in range(3) if (edge if t == 2 else main)]
 
     def turn(x, by):
         return pltpu.roll(x, by % 128, 1) if by % 128 else x
@@ -128,7 +131,7 @@
 
     scales = {}
     edges = {}
-    wind_sides = (sides(low_sides, 8), sides(high_sides, 8))
+    wind_sides = (sides(low_sides, 8), sides(high_sides, 8)) if edge else None
     for side, (reader, half, sign, first) in enumerate(
         ((low, low_half, 1.0, base), (high, 1 - low_half, -1.0, EXT_ROWS - base - 16))
     ):
@@ -138,7 +141,7 @@
             kx = k * SCALE
             half_lat = live * (SCALE * DIFF_LAT)
             scales[side, q] = (live * SCALE, live * (SCALE * (1.0 + 2.0 * DIFF_LAT - CENTRE)) + 2.0 * kx)
-            for t in range(3):
+            for t in spans:
                 winds = []
                 for field in range(2):
                     if t < 2:
@@ -171,14 +174,14 @@
     for i in range(16):
         u = base + i
         j = 15 - i
-        for n in range(6):
+        for n in range(6 if edge else 0):
             a = edges[0, i // 8, n][i % 8 : i % 8 + 1]
             b = edges[1, j // 8, n][j % 8 : j % 8 + 1]
             coef_edge[n, u : u + 1, :] = jnp.where(turned_row, b, jnp.where(inside, a, 0.0))
     for c in range(2):
         subs = slice(8 * c, 8 * c + 8)
         pairs = {}
-        for kind in range(2):
+        for kind in range(2 if edge else 0):
             for q in range(2):
                 pairs[kind, 0, q] = sides(low_sides, 4 * kind + 2 * q + c)
                 pairs[kind, 1, q] = sides(high_sides, 4 * kind + 2 * q + c)
@@ -187,11 +190,13 @@
             j = 15 - i
             mul_l, add_l = (x[i % 8 : i % 8 + 1] for x in scales[0, i // 8])
             mul_h, add_h = (x[j % 8 : j % 8 + 1] for x in scales[1, j // 8])
-            for t in range(2):
+            for t in range(2 if main else 0):
                 p0_ref[u, subs, TILES[t]] = low(i, subs, TILES[t])
                 p0_ref[u, subs, TILES[2 + t]] = turn(high(j, subs, TILES[t]), 64)
                 d_ref[u, subs, TILES[t]] = low(16 + i, subs, TILES[t]) * mul_l + add_l
                 d_ref[u, subs, TILES[2 + t]] = turn(high(16 + j, subs, TILES[t]), 64) * mul_h + add_h
+            if not edge:
+                continue
             f_edge, d_edge = (
                 spread(pairs[kind, 0, i // 8], i % 8, pairs[kind, 1, j // 8], j % 8) for kind in range(2)
             )
@@ -214,7 +219,7 @@
 
 
 def run_blocks(blocks, p_refs, d_ref, coef_refs, kron, mix_refs):
-    lane = lax.broadcasted_iota(jnp.int32, (CH, 128), 1)
+    lane = lax.broadcasted_iota(jnp.int32, (8, 128), 1)
     coef_low, coef_high, coef_edge = coef_refs
 
     def width(step):
@@ -255,30 +260,40 @@
         if more and not late:
             mix(index + 1)
         src, dst = p_refs[step - 1], p_refs[step]
-        for i in range(count):
+        for i, s in [(i, s) for i in range(count) for s in (slice(0, 8), slice(8, 16))]:
             u = u0 + i
-            centre = [src[u, :, t] for t in TILES]
+            centre = [src[u, s, t] for t in TILES]
             east, west = shifted(centre, -1), shifted(centre, 1)
             east2, west2 = shifted(centre, -2), shifted(centre, 2)
-            for t in range(width(step) // 128):
-                at = TILES[t]
-                if t < 2:
-                    coef = [coef_low[n, u : u + 1, at] for n in range(6)]
-                elif t < 4:
-                    v = HALF - 1 - u
-                    coef = [coef_high[n, v : v + 1, TILES[t - 2]] for n in range(6)]
-                else:
-                    coef = [coef_edge[n, u : u + 1, :] for n in range(6)]
-                acc = mix_refs[index % 2][i, :, at] + d_ref[u, :, at] * centre[t]
-                if step > 1:
-                    acc = acc - p_refs[step - 2][u, :, at]
-                acc = acc + coef[0] * east[t]
-                acc = acc + coef[1] * west[t]
-                acc = acc + coef[2] * (east2[t] - west2[t])
-                acc = acc + coef[3] * src[u + 1, :, at]
-                acc = acc + coef[4] * src[u - 1, :, at]
-                acc = acc + coef[5] * (src[u + 2, :, at] - src[u - 2, :, at])
-                dst[u, :, at] = acc
+            span = range(width(step) // 128)
+
+            def coef(n):
+                out = []
+                for t in span:
+                    if t < 2:
+                        out.append(coef_low[n, u : u + 1, TILES[t]])
+                    elif t < 4:
+                        v = HALF - 1 - u
+                        out.append(coef_high[n, v : v + 1, TILES[t - 2]])
+                    else:
+                        out.append(coef_edge[n, u : u + 1, :])
+                return out
+
+            acc = [mix_refs[index % 2][i, s, TILES[t]] + d_ref[u, s, TILES[t]] * centre[t] for t in span]
+            if step > 1:
+                acc = [acc[t] - p_refs[step - 2][u, s, TILES[t]] for t in span]
+            for n, values in (
+                (0, lambda t: east[t]),
+                (1, lambda t: west[t]),
+                (2, lambda t: east2[t] - west2[t]),
+                (3, lambda t: src[u + 1, s, TILES[t]]),
+                (4, lambda t: src[u - 1, s, TILES[t]]),
+                (5, lambda t: src[u + 2, s, TILES[t]] - src[u - 2, s, TILES[t]]),
+            ):
+                scale = coef(n)
+                acc = [acc[t] + scale[t] * values(t) for t in span]
+            for t in span:
+                dst[u, s, TILES[t]] = acc[t]
         if u0 + count == HALF and step < ITERS:
             mirror(dst)
         if late:
@@ -309,10 +324,7 @@
         k2_ref[n] = g_ref[par_y]
 
 
-def inner_kernel(s1_ref, s2_ref, g1_ref, g2_ref, cp_ref, k_ref, *refs):
-    p_refs = refs[: INNER_STEPS + 1]
-    d_ref, *coef_refs = refs[INNER_STEPS + 1 : INNER_STEPS + 5]
-    kron_ref, *mix_refs = refs[INNER_STEPS + 5 :]
+def stage_kernel(s1_ref, s2_ref, cp_ref, k_ref, p0_ref, d_ref, coef_low, coef_high, kron_ref):
     par_y = lax.rem(lax.axis_index("gy"), 2)
     size = 8 * CH
     pick = lax.broadcasted_iota(jnp.int32, (size, CH), 0) % CH
@@ -329,9 +341,20 @@
     place_pairs(
         lambda *at: jnp.where(par_y == 0, s2_ref[at], s1_ref[at]),
         lambda *at: jnp.where(par_y == 0, s1_ref[at], s2_ref[at]),
+        None, None, 0, RIM, p0_ref, d_ref, (coef_low, coef_high, None), k_ref, edge=False,
+    )
+
+
+def inner_kernel(g1_ref, g2_ref, k_ref, kron_ref, *refs):
+    refs = refs[4:]
+    p_refs = refs[: INNER_STEPS + 1]
+    d_ref, *coef_refs = refs[INNER_STEPS + 1 : INNER_STEPS + 5]
+    mix_refs = refs[INNER_STEPS + 5 :]
+    place_pairs(
+        None, None,
         lambda slot: (g1_ref[0, 8 * slot : 8 * slot + 8], g2_ref[0, 8 * slot : 8 * slot + 8]),
         lambda slot: (g1_ref[1, 8 * slot : 8 * slot + 8], g2_ref[1, 8 * slot : 8 * slot + 8]),
-        0, RIM, p_refs[0], d_ref, coef_refs, k_ref,
+        0, RIM, p_refs[0], d_ref, coef_refs, k_ref, main=False,
     )
     mirror(p_refs[0])
     run_blocks(INNER, p_refs, d_ref, coef_refs, split_kron(kron_ref), mix_refs)
@@ -552,20 +575,33 @@
     )(g1, g2)
     c1 = lax.ppermute(k1, "gy", pairing(ny, False, False))
     c2 = lax.ppermute(k2, "gy", pairing(ny, True, False))
-    field = shape(HALF + GHOST, CH, WIDE)
-    mix = [pltpu.VMEM((8, CH, WIDE), F32)] * 2
+    field = shape(HALF + GHOST + 1, CH, WIDE)
+    mix = [pltpu.VMEM((8, CH, WIDE), F32), pltpu.VMEM((9, CH, WIDE), F32)]
     carried = [field] * (INNER_STEPS + 1) + [shape(HALF, CH, WIDE)]
     carried += [shape(6, HALF, COLS)] * 2 + [shape(6, HALF, 128)]
-    *state, kron = pl.pallas_call(
+    first = [carried[n] for n in (0, -4, -3, -2)]
+    stage = pl.pallas_call(
+        stage_kernel,
+        in_specs=[VMEM] * 4,
+        out_specs=[VMEM] * 5,
+        out_shape=first + [shape(8 * CH, 8 * CH)],
+        compiler_params=pltpu.CompilerParams(vmem_limit_bytes=4 * 2**20),
+        cost_estimate=pl.CostEstimate(flops=10**7, bytes_accessed=2**20, transcendentals=0),
+        name="stage",
+    )
+    *staged, kron = stage(s1, s2, couple, k_rows)
+    where = (0, INNER_STEPS + 1, INNER_STEPS + 2, INNER_STEPS + 3)
+    state = pl.pallas_call(
         inner_kernel,
-        in_specs=[VMEM] * 6,
-        out_specs=[VMEM] * (len(carried) + 1),
-        out_shape=carried + [shape(8 * CH, 8 * CH)],
+        in_specs=[VMEM] * 8,
+        out_specs=[VMEM] * len(carried),
+        out_shape=carried,
+        input_output_aliases={4 + n: at for n, at in enumerate(where)},
         scratch_shapes=mix,
         compiler_params=pltpu.CompilerParams(vmem_limit_bytes=8 * 2**20),
         cost_estimate=pl.CostEstimate(flops=10**8, bytes_accessed=2**20, transcendentals=0),
         name="inner",
-    )(s1, s2, g1, g2, couple, k_rows)
+    )(g1, g2, k_rows, kron, *staged)
     extra = [field] * (NUM - INNER_STEPS - 1)
     results = pl.pallas_call(
         outer_kernel,

time: 55.9 us -> 55.4 us (level)
    pallas_call x1 -> x2, Pallas kernels: 4.33 us -> 4.45 us  [the longest x1 3.98 us: per_device(): pl.pallas_call(inner_kernel, in_specs=[VMEM] * 8, out_specs=[VMEM] * len(...]
where the time goes in v6:
time: 55.4 us; the launch traced here: 54.6 us
  blocking collectives  23.8 us (43%)
  Pallas kernels  17.8 us (32%)
  starting transfers between devices  10.2 us (18%)
  waiting for transfers between devices  2.04 us (4%)
  between operations  0.72 us (1%)
    all_to_all x1, blocking collectives, per_device(): rows = lax.all_to_all(results[-1], ('gx', 'gy'), 0, 0, tiled=True)  23.8 us
    pallas_call x1, Pallas kernels, per_device(): pl.pallas_call(outer_kernel, in_specs=[VMEM] * (6 + len(carried)), out_sp...  9.38 us
    pallas_call x1, Pallas kernels, per_device(): pl.pallas_call(inner_kernel, in_specs=[VMEM] * 8, out_specs=[VMEM] * len(...  3.98 us
    ppermute x1, starting transfers between devices, per_device(): c1 = lax.ppermute(k1, 'gy', pairing(ny, False, False))  3.98 us
    ppermute x1, starting transfers between devices, per_device(): g2 = lax.ppermute(x2, 'gx', pairing(nx, True, True))  3.12 us
    pallas_call x1, Pallas kernels, per_device(): pl.pallas_call(final_kernel, in_specs=[VMEM] * (NUM + 1), out_specs=[HBM,...  2.24 us
    ppermute x1, waiting for transfers between devices, per_device(): g2 = lax.ppermute(x2, 'gx', pairing(nx, True, True))  2.03 us
    ppermute x1, starting transfers between devices, per_device(): r1 = lax.ppermute(s1, 'gy', pairing(ny, False, False))  1.68 us
  transfers between devices with their start and end apart: 6, of which 1 were waited for; matrix products, arithmetic and copies ran while one was open for 0% of the time, Pallas kernels for 8%

profile of v6, /device:TPU:0, one launch (start us, length us, event | category | flops | bytes accessed | tf_op | source)
XLA Modules:
  0.0 54.6 jit_solution(6238259490408130499)
XLA Ops:
  0.6 1.7 %pack.1 = (f32[34,16,256]{2,1,0:T(8,128)S(1)}, f32[34,16,256]{2,1,0:T(8,128)S(1)}, f32[2,72,128]{2,1,0:T(8,128)S(1)}, f32[2,72,128]{2,1,0:T(8,128)S(1)}, f32[16,16]{1,0:T(8,128)S(1)}, /*index=5*/f32[64,128]{1,0:T(8,128)S(1)}) custom-call(f32[16,32,256]{2,1,0:T(8,128)} %f_hbm.1, f32[16,32,256]{2,1,0:T(8,128)} %d_hbm.1, f32[32,256]{1,0:T(8,128)} %wl_hbm.1, ...), custom_call_target="tpu_custom_call" | custom-call | tf_op jit(solution)/shard_map/pack/pallas_call | solution.py:547
  2.3 1.7 %collective-permute-start = (f32[34,16,256]{2,1,0:T(8,128)S(1)}, f32[34,16,256]{2,1,0:T(8,128)S(1)}, u32[]{:S(2)}, u32[]{:S(2)}) collective-permute-start(f32[34,16,256]{2,1,0:T(8,128)S(1)} %get-tuple-element.36.s1_ref), channel_id=1, source_target_pairs={{0,1},{1,0},{2,3},{3,2},{4,5},{5,4},{6,7},{7,6},{8,9},{9,8},{10,11... | collective-permute-start | bytes 1671176 | tf_op jit(solution)/shard_map/ppermute | solution.py:564
  4.0 0.7 %collective-permute-start.1 = (f32[34,16,256]{2,1,0:T(8,128)S(1)}, f32[34,16,256]{2,1,0:T(8,128)S(1)}, u32[]{:S(2)}, u32[]{:S(2)}) collective-permute-start(f32[34,16,256]{2,1,0:T(8,128)S(1)} %get-tuple-element.37.s2_ref), channel_id=1, source_target_pairs={{1,2},{2,1},{3,4},{4,3},{5,6},{6,5},{7,8},{8,7},{9,10},{10,9},{11,... | collective-permute-start | bytes 1671176 | tf_op jit(solution)/shard_map/ppermute | solution.py:565
  4.7 0.1 collective-permute-start.2
  4.8 3.1 %collective-permute-start.3 = (f32[2,72,128]{2,1,0:T(8,128)S(1)}, f32[2,72,128]{2,1,0:T(8,128)S(1)}, u32[]{:S(2)}, u32[]{:S(2)}) collective-permute-start(f32[2,72,128]{2,1,0:T(8,128)S(1)} %get-tuple-element.39), channel_id=1, source_target_pairs={{0,112},{16,32},{32,16},{48,64},{64,48},{80,96},{96,80},{112,0},{1... | collective-permute-start | bytes 221192 | tf_op jit(solution)/shard_map/ppermute | solution.py:567
  7.9 0.0 collective-permute-done.2.g1_ref
  7.9 2.0 %collective-permute-done.3.g2_ref = f32[2,72,128]{2,1,0:T(8,128)S(1)} collective-permute-done((f32[2,72,128]{2,1,0:T(8,128)S(1)}, f32[2,72,128]{2,1,0:T(8,128)S(1)}, u32[]{:S(2)}, u32[]{:S(2)}) %collective-permute-start.3) | collective-permute-done | bytes 73760 | tf_op jit(solution)/shard_map/ppermute | solution.py:567
  10.0 4.0 %collective-permute-start.4 = (f32[2,72,128]{2,1,0:T(8,128)S(1)}, f32[2,72,128]{2,1,0:T(8,128)S(1)}, u32[]{:S(2)}, u32[]{:S(2)}) collective-permute-start(f32[2,72,128]{2,1,0:T(8,128)S(1)} %get-tuple-element.40), channel_id=1, source_target_pairs={{0,1},{1,0},{2,3},{3,2},{4,5},{5,4},{6,7},{7,6},{8,9},{9,8},{10,11... | collective-permute-start | bytes 221192 | tf_op jit(solution)/shard_map/ppermute | solution.py:576
  13.9 0.7 %collective-permute-start.5 = (f32[2,72,128]{2,1,0:T(8,128)S(1)}, f32[2,72,128]{2,1,0:T(8,128)S(1)}, u32[]{:S(2)}, u32[]{:S(2)}) collective-permute-start(f32[2,72,128]{2,1,0:T(8,128)S(1)} %get-tuple-element.41), channel_id=1, source_target_pairs={{1,2},{2,1},{3,4},{4,3},{5,6},{6,5},{7,8},{8,7},{9,10},{10,9},{11,... | collective-permute-start | bytes 221192 | tf_op jit(solution)/shard_map/ppermute | solution.py:577
  14.6 0.5 stage.1
  15.1 4.0 %inner.1 = (f32[35,16,640]{2,1,0:T(8,128)S(1)}, f32[35,16,640]{2,1,0:T(8,128)S(1)}, f32[35,16,640]{2,1,0:T(8,128)S(1)}, f32[35,16,640]{2,1,0:T(8,128)S(1)}, f32[...) custom-call(f32[2,72,128]{2,1,0:T(8,128)S(1)} %collective-permute-do, ...), custom_call_target="tpu_custom_call", output_to_operand_aliasing={{0}: (4, {}), {7}: (5, {}), {8}: (6, {}), {9}: (7, {})} | custom-call | flops 100000000 | bytes 1048576 | tf_op jit(solution)/shard_map/inner/pallas_call | solution.py:594
  19.1 0.0 collective-permute-done.4.c1_ref
  19.1 0.0 collective-permute-done.5.c2_ref
  19.1 0.0 collective-permute-done.r1_ref
  19.1 0.0 collective-permute-done.1.r2_ref
  19.1 9.4 %outer.1 = (f32[35,16,640]{2,1,0:T(8,128)S(1)}, f32[35,16,640]{2,1,0:T(8,128)S(1)}, f32[35,16,640]{2,1,0:T(8,128)S(1)}, f32[35,16,640]{2,1,0:T(8,128)S(1)}, f32[...) custom-call(f32[34,16,256]{2,1,0:T(8,128)S(1)} %collective-permute-d, ...), custom_call_target="tpu_custom_call", output_to_operand_aliasing={{0}: (6, {}), {1}: (7, {}), {2}: (8, {}), {3}: (9, {}), {4}... | custom-call | tf_op jit(solution)/shard_map/outer/pallas_call | solution.py:606
  28.5 23.8 %all_to_all.11 = f32[128,1,128]{2,1,0:T(1,128)S(1)} all-to-all(f32[128,1,128]{2,1,0:T(1,128)S(1)} %bitcast.5), channel_id=1, replica_groups=mesh['gx'=8,'gy'=16] {'gx','gy'}, dimensions={0} | all-to-all | bytes 131072 | tf_op jit(solution)/shard_map/all_to_all | solution.py:617
  52.3 2.2 %finish.1 = (f32[16,32,256]{2,1,0:T(8,128)}, f32[16,32,256]{2,1,0:T(8,128)}) custom-call(f32[35,16,640]{2,1,0:T(8,128)S(1)} %get-tuple-element.60.refs_0_, f32[35,16,640]{2,1,0:T(8,128)S(1)} %get-tuple-element.61.refs_1_, f32[35,16,640]{2,1,0:T(8,128)S(1)} %get-tuple-element.62.refs_2_, f32[35,16,640]{2,1,0:T(8,128)S(1)} %get-tuple-element.63.refs_3_, ...), custom_call_target="tpu_custom_call" | custom-call | tf_op jit(solution)/shard_map/finish/pallas_call | solution.py:618
  (1 shorter events, 0.0 us)
Async XLA Ops:
  2.3 16.8 %collective-permute-start = (f32[34,16,256]{2,1,0:T(8,128)S(1)}, f32[34,16,256]{2,1,0:T(8,128)S(1)}, u32[]{:S(2)}, u32[]{:S(2)}) collective-permute-start(f32[34,16,256]{2,1,0:T(8,128)S(1)} %get-tuple-element.36.s1_ref), channel_id=1, source_target_pairs={{0,1},{1,0},{2,3},{3,2},{4,5},{5,4},{6,7},{7,6},{8,9},{9,8},{10,11... | collective-permute-start | bytes 1671176 | tf_op jit(solution)/shard_map/ppermute | solution.py:564
  4.0 15.1 %collective-permute-start.1 = (f32[34,16,256]{2,1,0:T(8,128)S(1)}, f32[34,16,256]{2,1,0:T(8,128)S(1)}, u32[]{:S(2)}, u32[]{:S(2)}) collective-permute-start(f32[34,16,256]{2,1,0:T(8,128)S(1)} %get-tuple-element.37.s2_ref), channel_id=1, source_target_pairs={{1,2},{2,1},{3,4},{4,3},{5,6},{6,5},{7,8},{8,7},{9,10},{10,9},{11,... | collective-permute-start | bytes 1671176 | tf_op jit(solution)/shard_map/ppermute | solution.py:565
  4.7 3.2 %collective-permute-start.2 = (f32[2,72,128]{2,1,0:T(8,128)S(1)}, f32[2,72,128]{2,1,0:T(8,128)S(1)}, u32[]{:S(2)}, u32[]{:S(2)}) collective-permute-start(f32[2,72,128]{2,1,0:T(8,128)S(1)} %get-tuple-element.38), channel_id=1, source_target_pairs={{0,16},{16,0},{32,48},{48,32},{64,80},{80,64},{96,112},{112,96},{1... | collective-permute-start | bytes 221192 | tf_op jit(solution)/shard_map/ppermute | solution.py:566
  4.8 5.2 %collective-permute-start.3 = (f32[2,72,128]{2,1,0:T(8,128)S(1)}, f32[2,72,128]{2,1,0:T(8,128)S(1)}, u32[]{:S(2)}, u32[]{:S(2)}) collective-permute-start(f32[2,72,128]{2,1,0:T(8,128)S(1)} %get-tuple-element.39), channel_id=1, source_target_pairs={{0,112},{16,32},{32,16},{48,64},{64,48},{80,96},{96,80},{112,0},{1... | collective-permute-start | bytes 221192 | tf_op jit(solution)/shard_map/ppermute | solution.py:567
  10.0 9.1 %collective-permute-start.4 = (f32[2,72,128]{2,1,0:T(8,128)S(1)}, f32[2,72,128]{2,1,0:T(8,128)S(1)}, u32[]{:S(2)}, u32[]{:S(2)}) collective-permute-start(f32[2,72,128]{2,1,0:T(8,128)S(1)} %get-tuple-element.40), channel_id=1, source_target_pairs={{0,1},{1,0},{2,3},{3,2},{4,5},{5,4},{6,7},{7,6},{8,9},{9,8},{10,11... | collective-permute-start | bytes 221192 | tf_op jit(solution)/shard_map/ppermute | solution.py:576
  13.9 5.1 %collective-permute-start.5 = (f32[2,72,128]{2,1,0:T(8,128)S(1)}, f32[2,72,128]{2,1,0:T(8,128)S(1)}, u32[]{:S(2)}, u32[]{:S(2)}) collective-permute-start(f32[2,72,128]{2,1,0:T(8,128)S(1)} %get-tuple-element.41), channel_id=1, source_target_pairs={{1,2},{2,1},{3,4},{4,3},{5,6},{6,5},{7,8},{8,7},{9,10},{10,9},{11,... | collective-permute-start | bytes 221192 | tf_op jit(solution)/shard_map/ppermute | solution.py:577

commit v7 on v6

--- a/solution.py
+++ b/solution.py
@@ -29,9 +29,21 @@
 F32 = jnp.float32
 
 
+def own_row(ref, rest, half, row, *at):
+    first = 2 * half
+    if row < 16:
+        return ref[(row, *at)]
+    if row >= 32:
+        return ref[(row - 2, *at)]
+    row -= 16
+    if first <= row < first + 14:
+        return ref[(16 + row - first, *at)]
+    return rest[(row % 14, *at)]
+
+
 def pack_kernel(
     f_hbm, d_hbm, wl_hbm, wt_hbm, cp_hbm, tab_hbm,
-    s1_ref, s2_ref, x1_ref, x2_ref, cp_ref, k_ref,
+    s1_ref, s2_ref, x1_ref, x2_ref, cp_ref, k_ref, rest_ref,
     f_ref, d_ref, wl_ref, wt_ref, sem,
 ):
     start = pl.multiple_of(lax.axis_index("gy") * ROWS, ROWS)
@@ -50,17 +62,19 @@
         copy.wait()
     par_y = lax.rem(lax.axis_index("gy"), 2)
     par_x = lax.rem(lax.axis_index("gx"), 2)
-    for ref, half in ((s1_ref, 1 - par_y), (s2_ref, par_y)):
-        for q in range(2):
-            off = pl.multiple_of(half * 16 + 8 * q, 8)
-            for src, base in ((f_ref, 0), (d_ref, 16)):
-                for c in range(2):
-                    ref[base + 8 * q : base + 8 * q + 8, 8 * c : 8 * c + 8, :] = jnp.swapaxes(
-                        src[8 * c : 8 * c + 8, pl.ds(off, 8), :], 0, 1
-                    )
+    for n, (ref, half) in enumerate(((s1_ref, 1 - par_y), (s2_ref, par_y))):
+        offs = [pl.multiple_of(half * 16 + 8 * q, 8) for q in range(2)]
+        for c in range(2):
+            subs = slice(8 * c, 8 * c + 8)
+            rows = [jnp.swapaxes(d_ref[subs, pl.ds(off, 8), :], 0, 1) for off in offs]
+            for q in range(2):
+                ref[pl.ds(16 + 8 * q - 2 * half, 8), subs, :] = rows[q]
+            rest_ref[n, :, subs, :] = jnp.where(half == 1, rows[0][:2], rows[1][6:])
+            for q in range(2):
+                ref[8 * q : 8 * q + 8, subs, :] = jnp.swapaxes(f_ref[subs, pl.ds(offs[q], 8), :], 0, 1)
         off = pl.multiple_of(half * 16, 16)
-        ref[32] = wl_ref[pl.ds(off, 16), :]
-        ref[33] = wt_ref[pl.ds(off, 16), :]
+        ref[30] = wl_ref[pl.ds(off, 16), :]
+        ref[31] = wt_ref[pl.ds(off, 16), :]
     group = lax.broadcasted_iota(jnp.int32, (8, 128), 1) // 16
 
     def gather(tiles):
@@ -89,8 +103,9 @@
                         row = base + 8 * q + g
                         pick = []
                         for t in range(2):
-                            one = s1_ref[row, 8 * c : 8 * c + 8, 128 * t : 128 * t + 128]
-                            two = s2_ref[row, 8 * c : 8 * c + 8, 128 * t : 128 * t + 128]
+                            at = (slice(8 * c, 8 * c + 8), slice(128 * t, 128 * t + 128))
+                            one = own_row(s1_ref, rest_ref.at[0], half, row, *at)
+                            two = own_row(s2_ref, rest_ref.at[1], half, row, *at)
                             pick.append(jnp.where(par_y == half, two, one))
                         tiles.append(tuple(pick))
                     first, second = gather(tiles)
@@ -193,6 +208,8 @@
             for t in range(2 if main else 0):
                 p0_ref[u, subs, TILES[t]] = low(i, subs, TILES[t])
                 p0_ref[u, subs, TILES[2 + t]] = turn(high(j, subs, TILES[t]), 64)
+                if u < 2:
+                    continue
                 d_ref[u, subs, TILES[t]] = low(16 + i, subs, TILES[t]) * mul_l + add_l
                 d_ref[u, subs, TILES[2 + t]] = turn(high(16 + j, subs, TILES[t]), 64) * mul_h + add_h
             if not edge:
@@ -201,6 +218,8 @@
                 spread(pairs[kind, 0, i // 8], i % 8, pairs[kind, 1, j // 8], j % 8) for kind in range(2)
             )
             p0_ref[u, subs, TILES[4]] = f_edge
+            if u < 2:
+                continue
             mul = jnp.where(turned_row, mul_h, mul_l)
             add = jnp.where(turned_row, add_h, add_l)
             d_ref[u, subs, TILES[4]] = d_edge * mul + add
@@ -324,7 +343,7 @@
         k2_ref[n] = g_ref[par_y]
 
 
-def stage_kernel(s1_ref, s2_ref, cp_ref, k_ref, p0_ref, d_ref, coef_low, coef_high, kron_ref):
+def stage_kernel(s1_ref, s2_ref, cp_ref, k_ref, rest_ref, p0_ref, d_ref, coef_low, coef_high, kron_ref):
     par_y = lax.rem(lax.axis_index("gy"), 2)
     size = 8 * CH
     pick = lax.broadcasted_iota(jnp.int32, (size, CH), 0) % CH
@@ -339,8 +358,12 @@
     col = lax.broadcasted_iota(jnp.int32, (size, size), 1) // CH
     kron_ref[...] = jnp.where(row == col, full, 0.0)
     place_pairs(
-        lambda *at: jnp.where(par_y == 0, s2_ref[at], s1_ref[at]),
-        lambda *at: jnp.where(par_y == 0, s1_ref[at], s2_ref[at]),
+        lambda *at: jnp.where(
+            par_y == 0, own_row(s2_ref, rest_ref.at[1], 0, *at), own_row(s1_ref, rest_ref.at[0], 0, *at)
+        ),
+        lambda *at: jnp.where(
+            par_y == 0, own_row(s1_ref, rest_ref.at[0], 1, *at), own_row(s2_ref, rest_ref.at[1], 1, *at)
+        ),
         None, None, 0, RIM, p0_ref, d_ref, (coef_low, coef_high, None), k_ref, edge=False,
     )
 
@@ -376,8 +399,8 @@
         return read
 
     place_pairs(
-        lambda *at: jnp.where(par_y == 0, r2_ref[at], r1_ref[at]),
-        lambda *at: jnp.where(par_y == 0, r1_ref[at], r2_ref[at]),
+        lambda *at: jnp.where(par_y == 0, own_row(r2_ref, None, 1, *at), own_row(r1_ref, None, 1, *at)),
+        lambda *at: jnp.where(par_y == 0, own_row(r1_ref, None, 0, *at), own_row(r2_ref, None, 0, *at)),
         corners(c2_ref, c1_ref), corners(c1_ref, c2_ref),
         1, 0, p_refs[0], d_ref, coef_refs, k_ref,
     )
@@ -544,13 +567,13 @@
 
 def per_device(forcing, damping, coupling, wind_lon, wind_lat, *, nx, ny):
     inputs = (forcing, damping, wind_lon, wind_lat, coupling, jnp.asarray(diffusion_table(ny * ROWS)))
-    s1, s2, x1, x2, couple, k_rows = pl.pallas_call(
+    s1, s2, x1, x2, couple, k_rows, rest = pl.pallas_call(
         pack_kernel,
         in_specs=[HBM] * 6,
-        out_specs=[VMEM] * 6,
-        out_shape=[shape(34, 16, COLS)] * 2
+        out_specs=[VMEM] * 7,
+        out_shape=[shape(32, 16, COLS)] * 2
         + [shape(2, 72, 128)] * 2
-        + [shape(CH, CH), shape(EXT_ROWS, 128)],
+        + [shape(CH, CH), shape(EXT_ROWS, 128), shape(2, 2, CH, COLS)],
         scratch_shapes=[
             pltpu.VMEM((CH, ROWS, COLS), F32),
             pltpu.VMEM((CH, ROWS, COLS), F32),
@@ -582,14 +605,14 @@
     first = [carried[n] for n in (0, -4, -3, -2)]
     stage = pl.pallas_call(
         stage_kernel,
-        in_specs=[VMEM] * 4,
+        in_specs=[VMEM] * 5,
         out_specs=[VMEM] * 5,
         out_shape=first + [shape(8 * CH, 8 * CH)],
         compiler_params=pltpu.CompilerParams(vmem_limit_bytes=4 * 2**20),
         cost_estimate=pl.CostEstimate(flops=10**7, bytes_accessed=2**20, transcendentals=0),
         name="stage",
     )
-    *staged, kron = stage(s1, s2, couple, k_rows)
+    *staged, kron = stage(s1, s2, couple, k_rows, rest)
     where = (0, INNER_STEPS + 1, INNER_STEPS + 2, INNER_STEPS + 3)
     state = pl.pallas_call(
         inner_kernel,

time: 55.4 us -> 54.7 us (0.987)
  blocking collectives: 23.8 us -> 23.1 us
    all_to_all x1, blocking collectives: 23.8 us -> 23.1 us  [per_device(): rows = lax.all_to_all(results[-1], ('gx', 'gy'), 0, 0, tiled=True)]
where the time goes in v7:
time: 54.7 us; the launch traced here: 53.9 us
  blocking collectives  23.1 us (42%)
  Pallas kernels  17.8 us (33%)
  starting transfers between devices  10.2 us (19%)
  waiting for transfers between devices  2.04 us (4%)
  between operations  0.72 us (1%)
    all_to_all x1, blocking collectives, per_device(): rows = lax.all_to_all(results[-1], ('gx', 'gy'), 0, 0, tiled=True)  23.1 us
    pallas_call x1, Pallas kernels, per_device(): pl.pallas_call(outer_kernel, in_specs=[VMEM] * (6 + len(carried)), out_sp...  9.38 us
    pallas_call x1, Pallas kernels, per_device(): pl.pallas_call(inner_kernel, in_specs=[VMEM] * 8, out_specs=[VMEM] * len(...  3.99 us
    ppermute x1, starting transfers between devices, per_device(): c1 = lax.ppermute(k1, 'gy', pairing(ny, False, False))  3.98 us
    ppermute x1, starting transfers between devices, per_device(): g2 = lax.ppermute(x2, 'gx', pairing(nx, True, True))  3.12 us
    pallas_call x1, Pallas kernels, per_device(): pl.pallas_call(final_kernel, in_specs=[VMEM] * (NUM + 1), out_specs=[HBM,...  2.24 us
    ppermute x1, waiting for transfers between devices, per_device(): g2 = lax.ppermute(x2, 'gx', pairing(nx, True, True))  2.03 us
    pallas_call x1, Pallas kernels, per_device(): pl.pallas_call(pack_kernel, in_specs=[HBM] * 6, out_specs=[VMEM] * 7, out...  1.74 us
  transfers between devices with their start and end apart: 6, of which 1 were waited for; matrix products, arithmetic and copies ran while one was open for 0% of the time, Pallas kernels for 8%

profile of v7, /device:TPU:0, one launch (start us, length us, event | category | flops | bytes accessed | tf_op | source)
XLA Modules:
  0.0 53.9 jit_solution(722935283451702663)
XLA Ops:
  0.6 1.7 %pack.1 = (f32[32,16,256]{2,1,0:T(8,128)S(1)}, f32[32,16,256]{2,1,0:T(8,128)S(1)}, f32[2,72,128]{2,1,0:T(8,128)S(1)}, f32[2,72,128]{2,1,0:T(8,128)S(1)}, f32[16,...) custom-call(f32[16,32,256]{2,1,0:T(8,128)} %f_hbm.1, f32[16,32,256]{2,1,0:T(8,128)} %d_hbm.1, ...), custom_call_target="tpu_custom_call" | custom-call | tf_op jit(solution)/shard_map/pack/pallas_call | solution.py:570
  2.4 1.7 %collective-permute-start = (f32[32,16,256]{2,1,0:T(8,128)S(1)}, f32[32,16,256]{2,1,0:T(8,128)S(1)}, u32[]{:S(2)}, u32[]{:S(2)}) collective-permute-start(f32[32,16,256]{2,1,0:T(8,128)S(1)} %get-tuple-element.37.s1_ref), channel_id=1, source_target_pairs={{0,1},{1,0},{2,3},{3,2},{4,5},{5,4},{6,7},{7,6},{8,9},{9,8},{10,11... | collective-permute-start | bytes 1572872 | tf_op jit(solution)/shard_map/ppermute | solution.py:587
  4.1 0.7 %collective-permute-start.1 = (f32[32,16,256]{2,1,0:T(8,128)S(1)}, f32[32,16,256]{2,1,0:T(8,128)S(1)}, u32[]{:S(2)}, u32[]{:S(2)}) collective-permute-start(f32[32,16,256]{2,1,0:T(8,128)S(1)} %get-tuple-element.38.s2_ref), channel_id=1, source_target_pairs={{1,2},{2,1},{3,4},{4,3},{5,6},{6,5},{7,8},{8,7},{9,10},{10,9},{11,... | collective-permute-start | bytes 1572872 | tf_op jit(solution)/shard_map/ppermute | solution.py:588
  4.8 0.1 collective-permute-start.2
  4.9 3.1 %collective-permute-start.3 = (f32[2,72,128]{2,1,0:T(8,128)S(1)}, f32[2,72,128]{2,1,0:T(8,128)S(1)}, u32[]{:S(2)}, u32[]{:S(2)}) collective-permute-start(f32[2,72,128]{2,1,0:T(8,128)S(1)} %get-tuple-element.40), channel_id=1, source_target_pairs={{0,112},{16,32},{32,16},{48,64},{64,48},{80,96},{96,80},{112,0},{1... | collective-permute-start | bytes 221192 | tf_op jit(solution)/shard_map/ppermute | solution.py:590
  8.0 0.0 collective-permute-done.2.g1_ref
  8.0 2.0 %collective-permute-done.3.g2_ref = f32[2,72,128]{2,1,0:T(8,128)S(1)} collective-permute-done((f32[2,72,128]{2,1,0:T(8,128)S(1)}, f32[2,72,128]{2,1,0:T(8,128)S(1)}, u32[]{:S(2)}, u32[]{:S(2)}) %collective-permute-start.3) | collective-permute-done | bytes 73760 | tf_op jit(solution)/shard_map/ppermute | solution.py:590
  10.0 4.0 %collective-permute-start.4 = (f32[2,72,128]{2,1,0:T(8,128)S(1)}, f32[2,72,128]{2,1,0:T(8,128)S(1)}, u32[]{:S(2)}, u32[]{:S(2)}) collective-permute-start(f32[2,72,128]{2,1,0:T(8,128)S(1)} %get-tuple-element.41), channel_id=1, source_target_pairs={{0,1},{1,0},{2,3},{3,2},{4,5},{5,4},{6,7},{7,6},{8,9},{9,8},{10,11... | collective-permute-start | bytes 221192 | tf_op jit(solution)/shard_map/ppermute | solution.py:599
  14.0 0.7 %collective-permute-start.5 = (f32[2,72,128]{2,1,0:T(8,128)S(1)}, f32[2,72,128]{2,1,0:T(8,128)S(1)}, u32[]{:S(2)}, u32[]{:S(2)}) collective-permute-start(f32[2,72,128]{2,1,0:T(8,128)S(1)} %get-tuple-element.42), channel_id=1, source_target_pairs={{1,2},{2,1},{3,4},{4,3},{5,6},{6,5},{7,8},{8,7},{9,10},{10,9},{11,... | collective-permute-start | bytes 221192 | tf_op jit(solution)/shard_map/ppermute | solution.py:600
  14.7 0.5 stage.1
  15.1 4.0 %inner.1 = (f32[35,16,640]{2,1,0:T(8,128)S(1)}, f32[35,16,640]{2,1,0:T(8,128)S(1)}, f32[35,16,640]{2,1,0:T(8,128)S(1)}, f32[35,16,640]{2,1,0:T(8,128)S(1)}, f32[...) custom-call(f32[2,72,128]{2,1,0:T(8,128)S(1)} %collective-permute-do, ...), custom_call_target="tpu_custom_call", output_to_operand_aliasing={{0}: (4, {}), {7}: (5, {}), {8}: (6, {}), {9}: (7, {})} | custom-call | flops 100000000 | bytes 1048576 | tf_op jit(solution)/shard_map/inner/pallas_call | solution.py:617
  19.1 0.0 collective-permute-done.4.c1_ref
  19.2 0.0 collective-permute-done.5.c2_ref
  19.2 0.0 collective-permute-done.r1_ref
  19.2 0.0 collective-permute-done.1.r2_ref
  19.2 9.4 %outer.1 = (f32[35,16,640]{2,1,0:T(8,128)S(1)}, f32[35,16,640]{2,1,0:T(8,128)S(1)}, f32[35,16,640]{2,1,0:T(8,128)S(1)}, f32[35,16,640]{2,1,0:T(8,128)S(1)}, f32[...) custom-call(f32[32,16,256]{2,1,0:T(8,128)S(1)} %collective-permute-d, ...), custom_call_target="tpu_custom_call", output_to_operand_aliasing={{0}: (6, {}), {1}: (7, {}), {2}: (8, {}), {3}: (9, {}), {4}... | custom-call | tf_op jit(solution)/shard_map/outer/pallas_call | solution.py:629
  28.6 23.1 %all_to_all.11 = f32[128,1,128]{2,1,0:T(1,128)S(1)} all-to-all(f32[128,1,128]{2,1,0:T(1,128)S(1)} %bitcast.5), channel_id=1, replica_groups=mesh['gx'=8,'gy'=16] {'gx','gy'}, dimensions={0} | all-to-all | bytes 131072 | tf_op jit(solution)/shard_map/all_to_all | solution.py:640
  51.7 2.2 %finish.1 = (f32[16,32,256]{2,1,0:T(8,128)}, f32[16,32,256]{2,1,0:T(8,128)}) custom-call(f32[35,16,640]{2,1,0:T(8,128)S(1)} %get-tuple-element.62.refs_0_, f32[35,16,640]{2,1,0:T(8,128)S(1)} %get-tuple-element.63.refs_1_, f32[35,16,640]{2,1,0:T(8,128)S(1)} %get-tuple-element.64.refs_2_, f32[35,16,640]{2,1,0:T(8,128)S(1)} %get-tuple-element.65.refs_3_, ...), custom_call_target="tpu_custom_call" | custom-call | tf_op jit(solution)/shard_map/finish/pallas_call | solution.py:641
  (1 shorter events, 0.0 us)
Async XLA Ops:
  2.4 16.8 %collective-permute-start = (f32[32,16,256]{2,1,0:T(8,128)S(1)}, f32[32,16,256]{2,1,0:T(8,128)S(1)}, u32[]{:S(2)}, u32[]{:S(2)}) collective-permute-start(f32[32,16,256]{2,1,0:T(8,128)S(1)} %get-tuple-element.37.s1_ref), channel_id=1, source_target_pairs={{0,1},{1,0},{2,3},{3,2},{4,5},{5,4},{6,7},{7,6},{8,9},{9,8},{10,11... | collective-permute-start | bytes 1572872 | tf_op jit(solution)/shard_map/ppermute | solution.py:587
  4.1 15.1 %collective-permute-start.1 = (f32[32,16,256]{2,1,0:T(8,128)S(1)}, f32[32,16,256]{2,1,0:T(8,128)S(1)}, u32[]{:S(2)}, u32[]{:S(2)}) collective-permute-start(f32[32,16,256]{2,1,0:T(8,128)S(1)} %get-tuple-element.38.s2_ref), channel_id=1, source_target_pairs={{1,2},{2,1},{3,4},{4,3},{5,6},{6,5},{7,8},{8,7},{9,10},{10,9},{11,... | collective-permute-start | bytes 1572872 | tf_op jit(solution)/shard_map/ppermute | solution.py:588
  4.8 3.2 %collective-permute-start.2 = (f32[2,72,128]{2,1,0:T(8,128)S(1)}, f32[2,72,128]{2,1,0:T(8,128)S(1)}, u32[]{:S(2)}, u32[]{:S(2)}) collective-permute-start(f32[2,72,128]{2,1,0:T(8,128)S(1)} %get-tuple-element.39), channel_id=1, source_target_pairs={{0,16},{16,0},{32,48},{48,32},{64,80},{80,64},{96,112},{112,96},{1... | collective-permute-start | bytes 221192 | tf_op jit(solution)/shard_map/ppermute | solution.py:589
  4.9 5.2 %collective-permute-start.3 = (f32[2,72,128]{2,1,0:T(8,128)S(1)}, f32[2,72,128]{2,1,0:T(8,128)S(1)}, u32[]{:S(2)}, u32[]{:S(2)}) collective-permute-start(f32[2,72,128]{2,1,0:T(8,128)S(1)} %get-tuple-element.40), channel_id=1, source_target_pairs={{0,112},{16,32},{32,16},{48,64},{64,48},{80,96},{96,80},{112,0},{1... | collective-permute-start | bytes 221192 | tf_op jit(solution)/shard_map/ppermute | solution.py:590
  10.0 9.1 %collective-permute-start.4 = (f32[2,72,128]{2,1,0:T(8,128)S(1)}, f32[2,72,128]{2,1,0:T(8,128)S(1)}, u32[]{:S(2)}, u32[]{:S(2)}) collective-permute-start(f32[2,72,128]{2,1,0:T(8,128)S(1)} %get-tuple-element.41), channel_id=1, source_target_pairs={{0,1},{1,0},{2,3},{3,2},{4,5},{5,4},{6,7},{7,6},{8,9},{9,8},{10,11... | collective-permute-start | bytes 221192 | tf_op jit(solution)/shard_map/ppermute | solution.py:599
  14.0 5.2 %collective-permute-start.5 = (f32[2,72,128]{2,1,0:T(8,128)S(1)}, f32[2,72,128]{2,1,0:T(8,128)S(1)}, u32[]{:S(2)}, u32[]{:S(2)}) collective-permute-start(f32[2,72,128]{2,1,0:T(8,128)S(1)} %get-tuple-element.42), channel_id=1, source_target_pairs={{1,2},{2,1},{3,4},{4,3},{5,6},{6,5},{7,8},{8,7},{9,10},{10,9},{11,... | collective-permute-start | bytes 221192 | tf_op jit(solution)/shard_map/ppermute | solution.py:600
